TPU v7x, 1024 devices: a whole 4x8x16 slice. The times are simulated.
1024 devices in a mesh: gx: 64 (over x_hi, z, core), gy: 16 (over x_lo, y).
Axes of the slice: x: 4 (x_hi: 2, x_lo: 2; x = x_hi * 2 + x_lo), y: 8, z: 16, core: 2. Of those that a mesh axis runs over, the one named last changes fastest.
Arguments:
- velocity: float32 [3, 256, 128, 128], P(None, 'gx', 'gy'), may hold values from -4 to 4
- forcing: float32 [3, 256, 128, 128], P(None, 'gx', 'gy'), may hold values from -6 to 6
- viscosity: float32 [256, 128, 128], P('gx', 'gy'), may hold values from 0.05 to 0.5
- residual_prev: float32 [3, 256, 128, 128], P(None, 'gx', 'gy'), may hold values from -4 to 4
- value_prev: float32 [3, 256, 128, 128], P(None, 'gx', 'gy'), may hold values from -4 to 4
- hist_res: float32 [5, 3, 256, 128, 128], P(None, None, 'gx', 'gy'), may hold values from -16 to 16
- hist_val: float32 [5, 3, 256, 128, 128], P(None, None, 'gx', 'gy'), may hold values from -4 to 4
Outputs:
- velocity_out: float32 [3, 256, 128, 128], P(None, 'gx', 'gy')
- residual_out: float32 [3, 256, 128, 128], P(None, 'gx', 'gy')
All inputs are finite; a program needn't handle non-finite values.
Results may differ from a plain program's by a relative error of at most 0.0003.
Values sent between devices are 32-bit elements; how exact they have to be, the bound alone decides.
No kernel may reach another device: no remote copies, remote signals or barrier semaphores. Data moves between devices by JAX's collectives and lax.ppermute only.
A program may use at most 64 MiB of HBM per device.

v0:
```python
import jax
import jax.numpy as jnp
from jax import lax
from jax.sharding import Mesh
from jax.sharding import PartitionSpec as P

M = 5
SWEEPS = 3
ITERS = 2
GX = ("gx_0", "gx_1", "gx_2")
GY = ("gy_0", "gy_1")
GX_GY = ("gx_0", "gx_1", "gx_2", "gy_0", "gy_1")


REG = 0.05
FLOOR = 0.001


def padded(cells, sides, width):
    for axis, dim in sides:
        count = lax.axis_size(axis)
        ends = count - 1
        head = lax.slice_in_dim(cells, 0, width, axis=dim)
        tail = lax.slice_in_dim(cells, cells.shape[dim] - width, cells.shape[dim], axis=dim)
        cells = jnp.concatenate(
            [
                lax.ppermute(tail, axis, [(i, (i + 1) % count) for i in range(ends)]),
                cells,
                lax.ppermute(head, axis, [((i + 1) % count, i) for i in range(ends)]),
            ],
            axis=dim,
        )
    return cells


def by_axis(x, axes):
    for axis in axes:
        x = lax.psum(x, axis)
    return x


def relax(wide, vel, forcing, visc):
    deep = jnp.pad(wide, ((0, 0), (0, 0), (0, 0), (1, 1)))
    west = deep[:, :-2, 1:-1, 1:-1]
    east = deep[:, 2:, 1:-1, 1:-1]
    south = deep[:, 1:-1, :-2, 1:-1]
    north = deep[:, 1:-1, 2:, 1:-1]
    below = deep[:, 1:-1, 1:-1, :-2]
    above = deep[:, 1:-1, 1:-1, 2:]
    upward = jnp.maximum(vel, 0.0)
    downward = jnp.minimum(vel, 0.0)
    diag = 1.0 + 6.0 * visc + jnp.sum(jnp.abs(vel), axis=0)
    total = forcing + vel + visc * (west + east + south + north + below + above)
    total = total + upward[0] * west - downward[0] * east
    total = total + upward[1] * south - downward[1] * north
    total = total + upward[2] * below - downward[2] * above
    return total / diag


def solve_small(gram, rhs, entries):
    shift = REG * jnp.trace(gram) / M + FLOOR * entries
    factor = jnp.linalg.cholesky(gram + shift * jnp.eye(M, dtype=jnp.float32))
    return jax.scipy.linalg.cho_solve((factor, True), rhs)


def local(velocity, forcing, viscosity, residual_prev, value_prev, hist_res, hist_val):
    cells = velocity.shape[1] * velocity.shape[2] * velocity.shape[3]
    entries = 3.0 * cells * lax.axis_size(GX) * lax.axis_size(GY)
    stacked = jnp.concatenate([forcing, viscosity[None]], 0)
    static = padded(stacked, ((GX, 1), (GY, 2)), SWEEPS - 1)
    field = velocity
    res_last = residual_prev
    val_last = value_prev
    hist_f = hist_res
    hist_g = hist_val
    for step in range(ITERS):
        extended = padded(field, ((GX, 1), (GY, 2)), SWEEPS)
        state = extended
        for sweep in range(SWEEPS):
            inner = SWEEPS - 1 - sweep
            vel = extended[
                :,
                sweep + 1 : extended.shape[1] - sweep - 1,
                sweep + 1 : extended.shape[2] - sweep - 1,
            ]
            if inner == 0:
                state = relax(state, field, forcing, viscosity)
            else:
                part_f = static[
                    :3, sweep : static.shape[1] - sweep, sweep : static.shape[2] - sweep
                ]
                part_v = static[3, sweep : static.shape[1] - sweep, sweep : static.shape[2] - sweep]
                state = relax(state, vel, part_f, part_v)
        resid = state - field
        flat = hist_f.reshape(M, -1)
        resid_flat = resid.reshape(-1)
        newest = (resid - res_last).reshape(-1)
        gram_now, rhs = (
            by_axis(jnp.dot(flat, flat.T, precision=lax.Precision.HIGHEST), GX_GY),
            by_axis(jnp.dot(flat, resid_flat, precision=lax.Precision.HIGHEST), GX_GY),
        )
        gamma = solve_small(gram_now, rhs, entries)
        field = state - jnp.tensordot(gamma, hist_g, axes=1, precision=lax.Precision.HIGHEST)
        hist_f = jnp.concatenate([hist_f[1:], newest.reshape(resid.shape)[None]], 0)
        hist_g = jnp.concatenate([hist_g[1:], (state - val_last)[None]], 0)
        res_last = resid
        val_last = state
    return (field, res_last)


def solution(mesh):
    torus = Mesh(mesh.devices.reshape(2, 16, 2, 2, 8), ("gx_0", "gx_1", "gx_2", "gy_0", "gy_1"))
    in_specs = (
        P(None, GX, GY, None),
        P(None, GX, GY, None),
        P(GX, GY, None),
        P(None, GX, GY, None),
        P(None, GX, GY, None),
        P(None, None, GX, GY, None),
        P(None, None, GX, GY, None),
    )
    out_specs = (P(None, GX, GY, None), P(None, GX, GY, None))
    return jax.shard_map(local, mesh=torus, in_specs=in_specs, out_specs=out_specs, check_vma=False)
```

profile of v0, /device:TPU:14, one launch (start us, length us, event | category | flops | bytes accessed | tf_op | source)
XLA Modules:
  0.0 204.5 jit_solution(12514477721572044287)
XLA Ops:
  3.4 18.5 %collective-permute-start.5 = (f32[3,3,8,128]{3,2,1,0:T(8,128)S(1)}, f32[3,3,8,128]{3,2,1,0:T(8,128)S(1)}, u32[]{:S(2)}, u32[]{:S(2)}) collective-permute-start(f32[3,3,8,128]{3,2,1,0:T(8,128)S(1)} %get-tuple-element.90), channel_id=1, source_target_pairs={{16,0},{32,16},{48,32},{64,48},{80,64},{96,80},{112,96},{128,112},... | collective-permute-start | bytes 110600 | tf_op jit(solution)/shard_map/ppermute | solution.py:29
  22.7 2.6 %collective-permute-start.1 = (f32[4,2,8,128]{3,2,1,0:T(8,128)S(1)}, f32[4,2,8,128]{3,2,1,0:T(8,128)S(1)}, u32[]{:S(2)}, u32[]{:S(2)}) collective-permute-start(f32[4,2,8,128]{3,2,1,0:T(8,128)S(1)} %get-tuple-element.79), channel_id=1, source_target_pairs={{16,0},{32,16},{48,32},{64,48},{80,64},{96,80},{112,96},{128,112},... | collective-permute-start | bytes 98312 | tf_op jit(solution)/shard_map/ppermute | solution.py:29
  25.3 1.9 collective-permute-start
  29.3 4.9 %collective-permute-done = f32[4,2,8,128]{3,2,1,0:T(8,128)S(1)} collective-permute-done((f32[4,2,8,128]{3,2,1,0:T(8,128)S(1)}, f32[4,2,8,128]{3,2,1,0:T(8,128)S(1)}, u32[]{:S(2)}, u32[]{:S(2)}) %collective-permute-start) | collective-permute-done | bytes 32800 | tf_op jit(solution)/shard_map/ppermute | solution.py:27
  34.2 2.5 %collective-permute-start.3 = (f32[4,8,2,128]{3,2,1,0:T(2,128)S(1)}, f32[4,8,2,128]{3,2,1,0:T(2,128)S(1)}, u32[]{:S(2)}, u32[]{:S(2)}) collective-permute-start(f32[4,8,2,128]{3,2,1,0:T(2,128)S(1)} %get-tuple-element.73), channel_id=1, source_target_pairs={{1,0},{2,1},{3,2},{4,3},{5,4},{6,5},{7,6},{8,7},{9,8},{10,9},{11,1... | collective-permute-start | bytes 98312 | tf_op jit(solution)/shard_map/ppermute | solution.py:29
  36.7 3.5 %collective-permute-start.2 = (f32[4,8,2,128]{3,2,1,0:T(2,128)S(1)}, f32[4,8,2,128]{3,2,1,0:T(2,128)S(1)}, u32[]{:S(2)}, u32[]{:S(2)}) collective-permute-start(f32[4,8,2,128]{3,2,1,0:T(2,128)S(1)} %get-tuple-element.72), channel_id=1, source_target_pairs={{0,1},{1,2},{2,3},{3,4},{4,5},{5,6},{6,7},{7,8},{8,9},{9,10},{10,1... | collective-permute-start | bytes 98312 | tf_op jit(solution)/shard_map/ppermute | solution.py:27
  40.3 3.2 %collective-permute-start.7 = (f32[3,10,3,128]{3,2,1,0:T(4,128)S(1)}, f32[3,10,3,128]{3,2,1,0:T(4,128)S(1)}, u32[]{:S(2)}, u32[]{:S(2)}) collective-permute-start(f32[3,10,3,128]{3,2,1,0:T(4,128)S(1)} %get-tuple-element.77), channel_id=1, source_target_pairs={{1,0},{2,1},{3,2},{4,3},{5,4},{6,5},{7,6},{8,7},{9,8},{10,9},{11,1... | collective-permute-start | bytes 138248 | tf_op jit(solution)/shard_map/ppermute | solution.py:29
  43.5 2.7 %collective-permute-start.6 = (f32[3,10,3,128]{3,2,1,0:T(4,128)S(1)}, f32[3,10,3,128]{3,2,1,0:T(4,128)S(1)}, u32[]{:S(2)}, u32[]{:S(2)}) collective-permute-start(f32[3,10,3,128]{3,2,1,0:T(4,128)S(1)} %get-tuple-element.76), channel_id=1, source_target_pairs={{0,1},{1,2},{2,3},{3,4},{4,5},{5,6},{6,7},{7,8},{8,9},{9,10},{10,1... | collective-permute-start | bytes 138248 | tf_op jit(solution)/shard_map/ppermute | solution.py:27
  46.4 5.3 %collective-permute-done.6 = f32[3,10,3,128]{3,2,1,0:T(4,128)S(1)} collective-permute-done((f32[3,10,3,128]{3,2,1,0:T(4,128)S(1)}, f32[3,10,3,128]{3,2,1,0:T(4,128)S(1)}, u32[]{:S(2)}, u32[]{:S(2)}) %collective-permute-start.6) | collective-permute-done | bytes 46112 | tf_op jit(solution)/shard_map/ppermute | solution.py:27
  54.9 6.5 %all-reduce.15 = (f32[5,5]{0,1:T(8,128)S(1)}, f32[5]{0:T(128)S(1)}) all-reduce(f32[5,5]{0,1:T(8,128)S(1)} %convolution_bitcast_fusion.1, f32[5]{0:T(128)S(1)} %convolution_bitcast_fusion.7), channel_id=1, replica_groups=mesh['gx_0'=2,'gx_1'=16,'gx_2'=2,'gy_0'=2,'gy_1'=8] {'gx_0'}, use_global_device_ids=true, to_apply=%region_3.4 | all-reduce | flops 30 | bytes 240 | tf_op jit(solution)/shard_map/psum | solution.py:38
  61.3 27.5 %all-reduce.7 = (f32[5,5]{0,1:T(8,128)S(1)}, f32[5]{0:T(128)S(1)}) all-reduce(f32[5,5]{0,1:T(8,128)S(1)} %get-tuple-element.22, f32[5]{0:T(128)S(1)} %get-tuple-element.23), channel_id=1, replica_groups=mesh['gx_0'=2,'gx_1'=16,'gx_2'=2,'gy_0'=2,'gy_1'=8] {'gx_1'}, use_global_device_ids=true, to_apply=%region_4.5 | all-reduce | flops 30 | bytes 240 | tf_op jit(solution)/shard_map/psum | solution.py:38
  88.9 2.5 %all-reduce.13 = (f32[5,5]{0,1:T(8,128)S(1)}, f32[5]{0:T(128)S(1)}) all-reduce(f32[5,5]{0,1:T(8,128)S(1)} %get-tuple-element.6, f32[5]{0:T(128)S(1)} %get-tuple-element.7), channel_id=1, replica_groups=mesh['gx_0'=2,'gx_1'=16,'gx_2'=2,'gy_0'=2,'gy_1'=8] {'gx_2'}, use_global_device_ids=true, to_apply=%region_5.6 | all-reduce | flops 30 | bytes 240 | tf_op jit(solution)/shard_map/psum | solution.py:38
  91.3 5.0 %all-reduce.11 = (f32[5,5]{0,1:T(8,128)S(1)}, f32[5]{0:T(128)S(1)}) all-reduce(f32[5,5]{0,1:T(8,128)S(1)} %get-tuple-element.18, f32[5]{0:T(128)S(1)} %get-tuple-element.19), channel_id=1, replica_groups=mesh['gx_0'=2,'gx_1'=16,'gx_2'=2,'gy_0'=2,'gy_1'=8] {'gy_0'}, use_global_device_ids=true, to_apply=%region_6.7 | all-reduce | flops 30 | bytes 240 | tf_op jit(solution)/shard_map/psum | solution.py:38
  96.3 18.5 %all-reduce.9 = (f32[5,5]{0,1:T(8,128)S(1)}, f32[5]{0:T(128)S(1)}) all-reduce(f32[5,5]{0,1:T(8,128)S(1)} %get-tuple-element.14, f32[5]{0:T(128)S(1)} %get-tuple-element.15), channel_id=1, replica_groups=mesh['gx_0'=2,'gx_1'=16,'gx_2'=2,'gy_0'=2,'gy_1'=8] {'gy_1'}, use_global_device_ids=true, to_apply=%region_7.8 | all-reduce | flops 30 | bytes 240 | tf_op jit(solution)/shard_map/psum | solution.py:38
  119.3 1.9 collective-permute-start.9
  121.2 2.4 %collective-permute-start.8 = (f32[3,3,8,128]{3,2,1,0:T(8,128)S(1)}, f32[3,3,8,128]{3,2,1,0:T(8,128)S(1)}, u32[]{:S(2)}, u32[]{:S(2)}) collective-permute-start(f32[3,3,8,128]{3,2,1,0:T(8,128)S(1)} %get-tuple-element.80), channel_id=1, source_target_pairs={{0,16},{16,32},{32,48},{48,64},{64,80},{80,96},{96,112},{112,128},... | collective-permute-start | bytes 110600 | tf_op jit(solution)/shard_map/ppermute | solution.py:27
  123.7 6.4 %collective-permute-done.8 = f32[3,3,8,128]{3,2,1,0:T(8,128)S(1)} collective-permute-done((f32[3,3,8,128]{3,2,1,0:T(8,128)S(1)}, f32[3,3,8,128]{3,2,1,0:T(8,128)S(1)}, u32[]{:S(2)}, u32[]{:S(2)}) %collective-permute-start.8) | collective-permute-done | bytes 36896 | tf_op jit(solution)/shard_map/ppermute | solution.py:27
  130.2 1.9 collective-permute-start.11
  132.1 3.9 %collective-permute-start.10 = (f32[3,10,3,128]{3,2,1,0:T(4,128)S(1)}, f32[3,10,3,128]{3,2,1,0:T(4,128)S(1)}, u32[]{:S(2)}, u32[]{:S(2)}) collective-permute-start(f32[3,10,3,128]{3,2,1,0:T(4,128)S(1)} %get-tuple-element.74), channel_id=1, source_target_pairs={{0,1},{1,2},{2,3},{3,4},{4,5},{5,6},{6,7},{7,8},{8,9},{9,10},{10,1... | collective-permute-start | bytes 138248 | tf_op jit(solution)/shard_map/ppermute | solution.py:27
  140.0 6.5 %all-reduce.14 = (f32[5,5]{0,1:T(8,128)S(1)}, f32[5]{0:T(128)S(1)}) all-reduce(f32[5,5]{0,1:T(8,128)S(1)} %convolution_bitcast_fusion, f32[5]{0:T(128)S(1)} %convolution_bitcast_fusion.6), channel_id=1, replica_groups=mesh['gx_0'=2,'gx_1'=16,'gx_2'=2,'gy_0'=2,'gy_1'=8] {'gx_0'}, use_global_device_ids=true, to_apply=%region_19.22 | all-reduce | flops 30 | bytes 240 | tf_op jit(solution)/shard_map/psum | solution.py:38
  146.5 27.5 %all-reduce.6 = (f32[5,5]{0,1:T(8,128)S(1)}, f32[5]{0:T(128)S(1)}) all-reduce(f32[5,5]{0,1:T(8,128)S(1)} %get-tuple-element.20, f32[5]{0:T(128)S(1)} %get-tuple-element.21), channel_id=1, replica_groups=mesh['gx_0'=2,'gx_1'=16,'gx_2'=2,'gy_0'=2,'gy_1'=8] {'gx_1'}, use_global_device_ids=true, to_apply=%region_20.23 | all-reduce | flops 30 | bytes 240 | tf_op jit(solution)/shard_map/psum | solution.py:38
  174.1 2.5 %all-reduce.12 = (f32[5,5]{0,1:T(8,128)S(1)}, f32[5]{0:T(128)S(1)}) all-reduce(f32[5,5]{0,1:T(8,128)S(1)} %get-tuple-element.4, f32[5]{0:T(128)S(1)} %get-tuple-element.5), channel_id=1, replica_groups=mesh['gx_0'=2,'gx_1'=16,'gx_2'=2,'gy_0'=2,'gy_1'=8] {'gx_2'}, use_global_device_ids=true, to_apply=%region_21.24 | all-reduce | flops 30 | bytes 240 | tf_op jit(solution)/shard_map/psum | solution.py:38
  176.5 5.0 %all-reduce.10 = (f32[5,5]{0,1:T(8,128)S(1)}, f32[5]{0:T(128)S(1)}) all-reduce(f32[5,5]{0,1:T(8,128)S(1)} %get-tuple-element.16, f32[5]{0:T(128)S(1)} %get-tuple-element.17), channel_id=1, replica_groups=mesh['gx_0'=2,'gx_1'=16,'gx_2'=2,'gy_0'=2,'gy_1'=8] {'gy_0'}, use_global_device_ids=true, to_apply=%region_22.25 | all-reduce | flops 30 | bytes 240 | tf_op jit(solution)/shard_map/psum | solution.py:38
  181.5 17.9 %all-reduce.8 = (f32[5,5]{0,1:T(8,128)S(1)}, f32[5]{0:T(128)S(1)}) all-reduce(f32[5,5]{0,1:T(8,128)S(1)} %get-tuple-element.12, f32[5]{0:T(128)S(1)} %get-tuple-element.13), channel_id=1, replica_groups=mesh['gx_0'=2,'gx_1'=16,'gx_2'=2,'gy_0'=2,'gy_1'=8] {'gy_1'}, use_global_device_ids=true, to_apply=%region_23.26 | all-reduce | flops 30 | bytes 240 | tf_op jit(solution)/shard_map/psum | solution.py:38
  (102 shorter events, 21.0 us)
Async XLA Ops:
  0.6 26.6 %copy-start = (f32[5,3,4,8,128]{4,3,2,1,0:T(8,128)S(1)}, f32[5,3,4,8,128]{4,3,2,1,0:T(8,128)}, u32[]{:S(2)}) copy-start(f32[5,3,4,8,128]{4,3,2,1,0:T(8,128)} %param.15) | copy-start | bytes 737284
  1.5 38.7 %collective-permute-start.4 = (f32[3,3,8,128]{3,2,1,0:T(8,128)S(1)}, f32[3,3,8,128]{3,2,1,0:T(8,128)S(1)}, u32[]{:S(2)}, u32[]{:S(2)}) collective-permute-start(f32[3,3,8,128]{3,2,1,0:T(8,128)S(1)} %get-tuple-element.91), channel_id=1, source_target_pairs={{0,16},{16,32},{32,48},{48,64},{64,80},{80,96},{96,112},{112,128},... | collective-permute-start | bytes 110600 | tf_op jit(solution)/shard_map/ppermute | solution.py:27
  3.4 36.8 %collective-permute-start.5 = (f32[3,3,8,128]{3,2,1,0:T(8,128)S(1)}, f32[3,3,8,128]{3,2,1,0:T(8,128)S(1)}, u32[]{:S(2)}, u32[]{:S(2)}) collective-permute-start(f32[3,3,8,128]{3,2,1,0:T(8,128)S(1)} %get-tuple-element.90), channel_id=1, source_target_pairs={{16,0},{32,16},{48,32},{64,48},{80,64},{96,80},{112,96},{128,112},... | collective-permute-start | bytes 110600 | tf_op jit(solution)/shard_map/ppermute | solution.py:29
  22.7 6.6 %collective-permute-start.1 = (f32[4,2,8,128]{3,2,1,0:T(8,128)S(1)}, f32[4,2,8,128]{3,2,1,0:T(8,128)S(1)}, u32[]{:S(2)}, u32[]{:S(2)}) collective-permute-start(f32[4,2,8,128]{3,2,1,0:T(8,128)S(1)} %get-tuple-element.79), channel_id=1, source_target_pairs={{16,0},{32,16},{48,32},{64,48},{80,64},{96,80},{112,96},{128,112},... | collective-permute-start | bytes 98312 | tf_op jit(solution)/shard_map/ppermute | solution.py:29
  25.3 8.8 %collective-permute-start = (f32[4,2,8,128]{3,2,1,0:T(8,128)S(1)}, f32[4,2,8,128]{3,2,1,0:T(8,128)S(1)}, u32[]{:S(2)}, u32[]{:S(2)}) collective-permute-start(f32[4,2,8,128]{3,2,1,0:T(8,128)S(1)} %get-tuple-element.78), channel_id=1, source_target_pairs={{0,16},{16,32},{32,48},{48,64},{64,80},{80,96},{96,112},{112,128},... | collective-permute-start | bytes 98312 | tf_op jit(solution)/shard_map/ppermute | solution.py:27
  28.2 0.9 slice-start
  29.2 4.9 %copy-start.1 = (f32[3,4,8,128]{3,2,1,0:T(8,128)S(1)}, f32[3,4,8,128]{3,2,1,0:T(8,128)}, u32[]{:S(2)}) copy-start(f32[3,4,8,128]{3,2,1,0:T(8,128)} %param.11) | copy-start | bytes 147460
  29.2 4.9 %copy-start.3 = (f32[4,8,128]{2,1,0:T(8,128)S(1)}, f32[4,8,128]{2,1,0:T(8,128)}, u32[]{:S(2)}) copy-start(f32[4,8,128]{2,1,0:T(8,128)} %param.12) | copy-start | bytes 49156
  34.2 6.0 %copy-start.4 = (f32[3,4,8,128]{3,2,1,0:T(8,128)S(1)}, f32[3,4,8,128]{3,2,1,0:T(8,128)}, u32[]{:S(2)}) copy-start(f32[3,4,8,128]{3,2,1,0:T(8,128)} %param.10) | copy-start | bytes 147460
  34.2 12.0 %collective-permute-start.3 = (f32[4,8,2,128]{3,2,1,0:T(2,128)S(1)}, f32[4,8,2,128]{3,2,1,0:T(2,128)S(1)}, u32[]{:S(2)}, u32[]{:S(2)}) collective-permute-start(f32[4,8,2,128]{3,2,1,0:T(2,128)S(1)} %get-tuple-element.73), channel_id=1, source_target_pairs={{1,0},{2,1},{3,2},{4,3},{5,4},{6,5},{7,6},{8,7},{9,8},{10,9},{11,1... | collective-permute-start | bytes 98312 | tf_op jit(solution)/shard_map/ppermute | solution.py:29
  36.7 9.5 %collective-permute-start.2 = (f32[4,8,2,128]{3,2,1,0:T(2,128)S(1)}, f32[4,8,2,128]{3,2,1,0:T(2,128)S(1)}, u32[]{:S(2)}, u32[]{:S(2)}) collective-permute-start(f32[4,8,2,128]{3,2,1,0:T(2,128)S(1)} %get-tuple-element.72), channel_id=1, source_target_pairs={{0,1},{1,2},{2,3},{3,4},{4,5},{5,6},{6,7},{7,8},{8,9},{9,10},{10,1... | collective-permute-start | bytes 98312 | tf_op jit(solution)/shard_map/ppermute | solution.py:27
  40.3 6.1 %collective-permute-start.7 = (f32[3,10,3,128]{3,2,1,0:T(4,128)S(1)}, f32[3,10,3,128]{3,2,1,0:T(4,128)S(1)}, u32[]{:S(2)}, u32[]{:S(2)}) collective-permute-start(f32[3,10,3,128]{3,2,1,0:T(4,128)S(1)} %get-tuple-element.77), channel_id=1, source_target_pairs={{1,0},{2,1},{3,2},{4,3},{5,4},{6,5},{7,6},{8,7},{9,8},{10,9},{11,1... | collective-permute-start | bytes 138248 | tf_op jit(solution)/shard_map/ppermute | solution.py:29
  43.5 8.2 %collective-permute-start.6 = (f32[3,10,3,128]{3,2,1,0:T(4,128)S(1)}, f32[3,10,3,128]{3,2,1,0:T(4,128)S(1)}, u32[]{:S(2)}, u32[]{:S(2)}) collective-permute-start(f32[3,10,3,128]{3,2,1,0:T(4,128)S(1)} %get-tuple-element.76), channel_id=1, source_target_pairs={{0,1},{1,2},{2,3},{3,4},{4,5},{5,6},{6,7},{7,8},{8,9},{9,10},{10,1... | collective-permute-start | bytes 138248 | tf_op jit(solution)/shard_map/ppermute | solution.py:27
  52.2 0.8 copy-start.5
  53.0 0.8 copy-start.6
  53.9 64.8 %copy-start.2 = (f32[5,3,4,8,128]{4,3,2,1,0:T(8,128)S(1)}, f32[5,3,4,8,128]{4,3,2,1,0:T(8,128)}, u32[]{:S(2)}) copy-start(f32[5,3,4,8,128]{4,3,2,1,0:T(8,128)} %param.16) | copy-start | bytes 737284
  119.3 4.4 %collective-permute-start.9 = (f32[3,3,8,128]{3,2,1,0:T(8,128)S(1)}, f32[3,3,8,128]{3,2,1,0:T(8,128)S(1)}, u32[]{:S(2)}, u32[]{:S(2)}) collective-permute-start(f32[3,3,8,128]{3,2,1,0:T(8,128)S(1)} %get-tuple-element.81), channel_id=1, source_target_pairs={{16,0},{32,16},{48,32},{64,48},{80,64},{96,80},{112,96},{128,112},... | collective-permute-start | bytes 110600 | tf_op jit(solution)/shard_map/ppermute | solution.py:29
  121.2 8.9 %collective-permute-start.8 = (f32[3,3,8,128]{3,2,1,0:T(8,128)S(1)}, f32[3,3,8,128]{3,2,1,0:T(8,128)S(1)}, u32[]{:S(2)}, u32[]{:S(2)}) collective-permute-start(f32[3,3,8,128]{3,2,1,0:T(8,128)S(1)} %get-tuple-element.80), channel_id=1, source_target_pairs={{0,16},{16,32},{32,48},{48,64},{64,80},{80,96},{96,112},{112,128},... | collective-permute-start | bytes 110600 | tf_op jit(solution)/shard_map/ppermute | solution.py:27
  123.7 12.4 %slice-start.1 = ((f32[5,3,4,8,128]{4,3,2,1,0:T(8,128)}), f32[4,3,4,8,128]{4,3,2,1,0:T(8,128)S(1)}, s32[]{:S(2)}) async-start(f32[5,3,4,8,128]{4,3,2,1,0:T(8,128)} %param.16), calls=%async_computation.1 | async-start | bytes 393216 | tf_op jit(solution)/shard_map/slice | solution.py:105
  130.2 6.8 %collective-permute-start.11 = (f32[3,10,3,128]{3,2,1,0:T(4,128)S(1)}, f32[3,10,3,128]{3,2,1,0:T(4,128)S(1)}, u32[]{:S(2)}, u32[]{:S(2)}) collective-permute-start(f32[3,10,3,128]{3,2,1,0:T(4,128)S(1)} %get-tuple-element.75), channel_id=1, source_target_pairs={{1,0},{2,1},{3,2},{4,3},{5,4},{6,5},{7,6},{8,7},{9,8},{10,9},{11,1... | collective-permute-start | bytes 138248 | tf_op jit(solution)/shard_map/ppermute | solution.py:29
  132.1 6.1 %collective-permute-start.10 = (f32[3,10,3,128]{3,2,1,0:T(4,128)S(1)}, f32[3,10,3,128]{3,2,1,0:T(4,128)S(1)}, u32[]{:S(2)}, u32[]{:S(2)}) collective-permute-start(f32[3,10,3,128]{3,2,1,0:T(4,128)S(1)} %get-tuple-element.74), channel_id=1, source_target_pairs={{0,1},{1,2},{2,3},{3,4},{4,5},{5,6},{6,7},{7,8},{8,9},{9,10},{10,1... | collective-permute-start | bytes 138248 | tf_op jit(solution)/shard_map/ppermute | solution.py:27
  139.1 1.0 copy-start.7
where the time goes:
time: 205 us; the launch traced here: 204 us
  blocking collectives  119 us (58%)
  starting transfers between devices  46.9 us (23%)
  waiting for transfers between devices  18 us (9%)
  other arithmetic  8.58 us (4%)
  matrix products  5.54 us (3%)
  local copies, waits for them, and re-layouts  3.61 us (2%)
  between operations  2.53 us (1%)
    psum x10, blocking collectives, by_axis(): x = lax.psum(x, axis)  119 us
    ppermute x6, starting transfers between devices, padded(): lax.ppermute(head, axis, [((i + 1) % count, i) for i in range(ends)])  30.6 us
    ppermute x6, waiting for transfers between devices, padded(): lax.ppermute(tail, axis, [(i, (i + 1) % count) for i in range(ends)])  17.8 us
    ppermute x6, starting transfers between devices, padded(): lax.ppermute(tail, axis, [(i, (i + 1) % count) for i in range(ends)])  16.3 us
  transfers between devices with their start and end apart: 12, of which 5 were waited for; matrix products, arithmetic and copies ran while one was open for 1% of the time, Pallas kernels for 0%

commit v1 on v0

v1 whole, which is shorter than its diff:
```python
import jax
import jax.numpy as jnp
from jax import lax
from jax.sharding import Mesh
from jax.sharding import PartitionSpec as P

M = 5
SWEEPS = 3
GX = ("gx_0", "gx_1", "gx_2")
GY = ("gy_0", "gy_1")
CHAIN = ("gx_1", "gx_2")
PLANE = ("gx_0", "gy_0", "gy_1")

REG = 0.05
FLOOR = 0.001
PAIRS = [(i, j) for i in range(M) for j in range(i, M)]


def padded(cells, sides, width):
    for axis, dim in sides:
        count = lax.axis_size(axis)
        ends = count - 1
        head = lax.slice_in_dim(cells, 0, width, axis=dim)
        tail = lax.slice_in_dim(cells, cells.shape[dim] - width, cells.shape[dim], axis=dim)
        cells = jnp.concatenate(
            [
                lax.ppermute(tail, axis, [(i, (i + 1) % count) for i in range(ends)]),
                cells,
                lax.ppermute(head, axis, [((i + 1) % count, i) for i in range(ends)]),
            ],
            axis=dim,
        )
    return cells


def total_over_devices(row):
    for group in (CHAIN, PLANE):
        count = lax.axis_size(group)
        rows = jnp.broadcast_to(row[None, None, :], (count, 1, row.shape[0]))
        row = jnp.sum(lax.all_to_all(rows, group, 0, 0), axis=(0, 1))
    return row


def relax(wide, vel, forcing, visc):
    deep = jnp.pad(wide, ((0, 0), (0, 0), (0, 0), (1, 1)))
    west = deep[:, :-2, 1:-1, 1:-1]
    east = deep[:, 2:, 1:-1, 1:-1]
    south = deep[:, 1:-1, :-2, 1:-1]
    north = deep[:, 1:-1, 2:, 1:-1]
    below = deep[:, 1:-1, 1:-1, :-2]
    above = deep[:, 1:-1, 1:-1, 2:]
    upward = jnp.maximum(vel, 0.0)
    downward = jnp.minimum(vel, 0.0)
    diag = 1.0 + 6.0 * visc + jnp.sum(jnp.abs(vel), axis=0)
    total = forcing + vel + visc * (west + east + south + north + below + above)
    total = total + upward[0] * west - downward[0] * east
    total = total + upward[1] * south - downward[1] * north
    total = total + upward[2] * below - downward[2] * above
    return total / diag


def picard(extended, static):
    state = extended
    for sweep in range(SWEEPS):
        edge = sweep + 1
        vel = extended[:, edge : extended.shape[1] - edge, edge : extended.shape[2] - edge]
        fixed = static[:, edge : static.shape[1] - edge, edge : static.shape[2] - edge]
        state = relax(state, vel, fixed[:3], fixed[3])
    return state


def solve_small(gram, rhs, entries):
    shift = REG * jnp.trace(gram) / M + FLOOR * entries
    factor = jnp.linalg.cholesky(gram + shift * jnp.eye(M, dtype=jnp.float32))
    return jax.scipy.linalg.cho_solve((factor, True), rhs)


def dot(a, b):
    return jnp.sum(a * b)


def mix(value, gamma, history):
    for j in range(M):
        value = value - gamma[j] * history[j]
    return value


def local(velocity, forcing, viscosity, residual_prev, value_prev, hist_res, hist_val):
    cells = velocity.shape[1] * velocity.shape[2] * velocity.shape[3]
    entries = 3.0 * cells * lax.axis_size(GX) * lax.axis_size(GY)
    sides = ((GX, 1), (GY, 2))
    both = padded(jnp.concatenate([velocity, forcing, viscosity[None]], 0), sides, SWEEPS)
    static = both[3:]

    value = picard(both[:3], static)
    resid = value - velocity
    newest = resid - residual_prev
    sums = [dot(hist_res[i], hist_res[j]) for i, j in PAIRS]
    sums += [dot(hist_res[i], resid) for i in range(M)]
    sums += [dot(hist_res[i], newest) for i in range(M)]
    sums += [dot(newest, newest)]
    sums = total_over_devices(jnp.pad(jnp.stack(sums), (0, 128 - len(sums))))
    first = len(PAIRS)
    place = {pair: k for k, pair in enumerate(PAIRS)}
    gram = jnp.stack(
        [sums[place[min(i, j), max(i, j)]] for i in range(M) for j in range(M)]
    ).reshape(M, M)
    gamma = solve_small(gram, sums[first : first + M], entries)
    field = mix(value, gamma, hist_val)

    cross = sums[first + M + 1 : first + 2 * M]
    gram_next = jnp.concatenate(
        [
            jnp.concatenate([gram[1:, 1:], cross[:, None]], 1),
            jnp.concatenate([cross, sums[first + 2 * M][None]])[None],
        ],
        0,
    )
    value_next = picard(padded(field, sides, SWEEPS), static)
    resid_next = value_next - field
    sums = [dot(hist_res[i], resid_next) for i in range(1, M)] + [dot(newest, resid_next)]
    sums = total_over_devices(jnp.pad(jnp.stack(sums), (0, 128 - M)))
    gamma = solve_small(gram_next, sums[:M], entries)
    field = mix(value_next, gamma, [*hist_val[1:], value - value_prev])
    return (field, resid_next)


def solution(mesh):
    torus = Mesh(mesh.devices.reshape(2, 16, 2, 2, 8), ("gx_0", "gx_1", "gx_2", "gy_0", "gy_1"))
    in_specs = (
        P(None, GX, GY, None),
        P(None, GX, GY, None),
        P(GX, GY, None),
        P(None, GX, GY, None),
        P(None, GX, GY, None),
        P(None, None, GX, GY, None),
        P(None, None, GX, GY, None),
    )
    out_specs = (P(None, GX, GY, None), P(None, GX, GY, None))
    return jax.shard_map(local, mesh=torus, in_specs=in_specs, out_specs=out_specs, check_vma=False)
```

time: 205 us -> 175 us (0.85)
  the two profiles are of different devices: /device:TPU:14 before, /device:TPU:1 now
where the time goes in v1:
time: 175 us; the launch traced here: 173 us
  starting transfers between devices  46.5 us (27%)
  blocking collectives  44 us (25%)
  local copies, waits for them, and re-layouts  32.1 us (18%)
  waiting for transfers between devices  29.7 us (17%)
  other arithmetic  18.1 us (10%)
  between operations  2.41 us (1%)
    all_to_all x2, blocking collectives, total_over_devices(): row = jnp.sum(lax.all_to_all(rows, group, 0, 0), axis=(0, 1))  44 us
    all_to_all x2, waiting for transfers between devices, total_over_devices(): row = jnp.sum(lax.all_to_all(rows, group, 0, 0), axis=(0, 1))  18.5 us
    all_to_all x2, starting transfers between devices, total_over_devices(): row = jnp.sum(lax.all_to_all(rows, group, 0, 0), axis=(0, 1))  16.8 us
    ppermute x4, starting transfers between devices, padded(): lax.ppermute(head, axis, [((i + 1) % count, i) for i in range(ends)])  16.4 us
    another operation x1, local copies, waits for them, and re-layouts, local(): sums = total_over_devices(jnp.pad(jnp.stack(sums), (0, 128 - len(sums))))  16.3 us
    ppermute x4, starting transfers between devices, padded(): lax.ppermute(tail, axis, [(i, (i + 1) % count) for i in range(ends)])  13.3 us
    ppermute x4, waiting for transfers between devices, padded(): lax.ppermute(head, axis, [((i + 1) % count, i) for i in range(ends)])  9.49 us
    another operation x1, local copies, waits for them, and re-layouts, local(): jnp.stack([sums[place[min(i, j), max(i, j)]] for i in range(M) for j in r...  5.67 us
  transfers between devices with their start and end apart: 10, of which 7 were waited for; matrix products, arithmetic and copies ran while one was open for 2% of the time, Pallas kernels for 0%

profile of v1, /device:TPU:1, one launch (start us, length us, event | category | flops | bytes accessed | tf_op | source)
XLA Modules:
  0.0 173.5 jit_solution(13529006322585253560)
XLA Ops:
  1.5 5.4 %collective-permute-start = (f32[7,3,8,128]{3,2,1,0:T(8,128)S(1)}, f32[7,3,8,128]{3,2,1,0:T(8,128)S(1)}, u32[]{:S(2)}, u32[]{:S(2)}) collective-permute-start(f32[7,3,8,128]{3,2,1,0:T(8,128)S(1)} %get-tuple-element.86), channel_id=1, source_target_pairs={{0,16},{16,32},{32,48},{48,64},{64,80},{80,96},{96,112},{112,128},... | collective-permute-start | bytes 258056 | tf_op jit(solution)/shard_map/ppermute | solution.py:27
  6.9 11.9 %collective-permute-start.1 = (f32[7,3,8,128]{3,2,1,0:T(8,128)S(1)}, f32[7,3,8,128]{3,2,1,0:T(8,128)S(1)}, u32[]{:S(2)}, u32[]{:S(2)}) collective-permute-start(f32[7,3,8,128]{3,2,1,0:T(8,128)S(1)} %get-tuple-element.87), channel_id=1, source_target_pairs={{16,0},{32,16},{48,32},{64,48},{80,64},{96,80},{112,96},{128,112},... | collective-permute-start | bytes 258056 | tf_op jit(solution)/shard_map/ppermute | solution.py:29
  19.8 1.3 collective-permute-start.2
  21.1 1.3 collective-permute-start.3
  22.5 1.7 collective-permute-done.2
  24.2 3.8 %collective-permute-done.3 = f32[7,10,3,128]{3,2,1,0:T(4,128)S(1)} collective-permute-done((f32[7,10,3,128]{3,2,1,0:T(4,128)S(1)}, f32[7,10,3,128]{3,2,1,0:T(4,128)S(1)}, u32[]{:S(2)}, u32[]{:S(2)}) %collective-permute-start.3) | collective-permute-done | bytes 107552 | tf_op jit(solution)/shard_map/ppermute | solution.py:29
  32.9 16.3 %stack.129 = f32[26]{0:T(128)S(1)} concatenate(f32[1]{0:T(128)} %bitcast.26, f32[1]{0:T(128)} %bitcast.28, f32[1]{0:T(128)} %bitcast.30, f32[1]{0:T(128)} %bitcast.32, f32[1]{0:T(128)} %bitcast.34, f32[1]{0:T(128)} %bitcast.35, f32[1]{0:T(128)} %bitcast.36, f32[1]{0:T(128)} %bitcast.37, f32[1]{0:T(128)} %bitcast.38, f32[1]{0:T(128)} %bitcast.39, f32[1]{0:T(128)} %bitcast.40, ...), dimensions={0} | concatenate | bytes 208 | tf_op jit(solution)/shard_map/stack | solution.py:102
  49.2 25.7 %all_to_all.20 = f32[32,1,128]{2,1,0:T(1,128)S(1)} all-to-all(f32[32,1,128]{2,1,0:T(1,128)S(1)} %broadcast_in_dim.16), channel_id=1, replica_groups=mesh['gx_0'=2,'gx_1'=16,'gx_2'=2,'gy_0'=2,'gy_1'=8] {'gx_1','gx_2'}, dimensions={0} | all-to-all | bytes 32768 | tf_op jit(solution)/shard_map/all_to_all | solution.py:40
  75.0 18.3 %all_to_all.21 = f32[32,1,128]{2,1,0:T(1,128)S(1)} all-to-all(f32[32,1,128]{2,1,0:T(1,128)S(1)} %broadcast_in_dim.17), channel_id=1, replica_groups=mesh['gx_0'=2,'gx_1'=16,'gx_2'=2,'gy_0'=2,'gy_1'=8] {'gx_0','gy_0','gy_1'}, dimensions={0} | all-to-all | bytes 32768 | tf_op jit(solution)/shard_map/all_to_all | solution.py:40
  94.3 5.7 %stack.130 = f32[25]{0:T(128)S(1)} concatenate(f32[5]{0:T(128)S(1)} %get-tuple-element.115, f32[1]{0:T(128)} %get-tuple-element.131, f32[4]{0:T(128)S(1)} %get-tuple-element.113, f32[1]{0:T(128)} %get-tuple-element.130, f32[1]{0:T(128)} %get-tuple-element.129, f32[3]{0:T(128)S(1)} %slice.574, f32[1]{0:T(128)} %get-tuple-element.128, f32[1]{0:T(128)} %get-tuple-element.127, ...), dimensions={0} | concatenate | bytes 200 | tf_op jit(solution)/shard_map/stack | solution.py:105
  104.7 3.2 %broadcast_maximum_fusion = (f32[3,4,8,128]{3,2,1,0:T(8,128)S(1)}, f32[3,4,8,128]{3,2,1,0:T(8,128)S(1)}) fusion(f32[5,3,4,8,128]{4,3,2,1,0:T(8,128)S(1)} %copy-done.6, f32[]{:T(128)} %bitcast.73, f32[]{:T(128)} %bitcast.71, f32[]{:T(128)} %bitcast.69, f32[]{:T(128)} %bitcast.67, f32[3,4,8,128]{3,2,1,0:T(8,128)S(1)} %get-tuple-element.40, f32[]{:T(128)} %bitcast.65), kind=kLoop, calls=%fused_computation.148 | loop fusion | flops 135168 | bytes 393236 | tf_op jit(solution)/shard_map/max | solution.py:52
  108.0 4.4 %collective-permute-start.4 = (f32[3,3,8,128]{3,2,1,0:T(8,128)S(1)}, f32[3,3,8,128]{3,2,1,0:T(8,128)S(1)}, u32[]{:S(2)}, u32[]{:S(2)}) collective-permute-start(f32[3,3,8,128]{3,2,1,0:T(8,128)S(1)} %get-tuple-element.88), channel_id=1, source_target_pairs={{0,16},{16,32},{32,48},{48,64},{64,80},{80,96},{96,112},{112,128},... | collective-permute-start | bytes 110600 | tf_op jit(solution)/shard_map/ppermute | solution.py:27
  112.4 1.9 %collective-permute-start.5 = (f32[3,3,8,128]{3,2,1,0:T(8,128)S(1)}, f32[3,3,8,128]{3,2,1,0:T(8,128)S(1)}, u32[]{:S(2)}, u32[]{:S(2)}) collective-permute-start(f32[3,3,8,128]{3,2,1,0:T(8,128)S(1)} %get-tuple-element.89), channel_id=1, source_target_pairs={{16,0},{32,16},{48,32},{64,48},{80,64},{96,80},{112,96},{128,112},... | collective-permute-start | bytes 110600 | tf_op jit(solution)/shard_map/ppermute | solution.py:29
  116.5 1.2 collective-permute-done.5
  117.8 2.2 %collective-permute-start.6 = (f32[3,10,3,128]{3,2,1,0:T(4,128)S(1)}, f32[3,10,3,128]{3,2,1,0:T(4,128)S(1)}, u32[]{:S(2)}, u32[]{:S(2)}) collective-permute-start(f32[3,10,3,128]{3,2,1,0:T(4,128)S(1)} %get-tuple-element.84), channel_id=1, source_target_pairs={{0,1},{1,2},{2,3},{3,4},{4,5},{5,6},{6,7},{7,8},{8,9},{9,10},{10,1... | collective-permute-start | bytes 138248 | tf_op jit(solution)/shard_map/ppermute | solution.py:27
  120.0 1.3 collective-permute-start.7
  121.3 3.6 %collective-permute-done.7 = f32[3,10,3,128]{3,2,1,0:T(4,128)S(1)} collective-permute-done((f32[3,10,3,128]{3,2,1,0:T(4,128)S(1)}, f32[3,10,3,128]{3,2,1,0:T(4,128)S(1)}, u32[]{:S(2)}, u32[]{:S(2)}) %collective-permute-start.7) | collective-permute-done | bytes 46112 | tf_op jit(solution)/shard_map/ppermute | solution.py:29
  125.7 1.4 fusion.11
  127.2 3.2 %stack.136 = f32[5]{0:T(128)S(1)} concatenate(f32[1]{0:T(128)} %bitcast.102, f32[1]{0:T(128)} %bitcast.103, f32[1]{0:T(128)} %bitcast.104, f32[1]{0:T(128)} %bitcast.105, f32[1]{0:T(128)} %bitcast.106), dimensions={0} | concatenate | bytes 40 | tf_op jit(solution)/shard_map/stack | solution.py:122
  131.0 8.5 %all-to-all-start.2 = ((f32[32,1,128]{2,1,0:T(1,128)}), f32[32,1,128]{2,1,0:T(1,128)S(1)}, u32[]{:S(2)}, u32[]{:S(2)}) async-start(f32[32,1,128]{2,1,0:T(1,128)} %broadcast_in_dim.20), calls=%async_computation.2 | async-start | bytes 32768 | tf_op jit(solution)/shard_map/all_to_all | solution.py:40
  140.3 11.0 %all-to-all-done.2 = f32[32,1,128]{2,1,0:T(1,128)S(1)} async-done(((f32[32,1,128]{2,1,0:T(1,128)}), f32[32,1,128]{2,1,0:T(1,128)S(1)}, u32[]{:S(2)}, u32[]{:S(2)}) %all-to-all-start.2) | async-done | bytes 16416 | tf_op jit(solution)/shard_map/all_to_all | solution.py:40
  151.9 8.2 %all-to-all-start.3 = ((f32[32,1,128]{2,1,0:T(1,128)}), f32[32,1,128]{2,1,0:T(1,128)S(1)}, u32[]{:S(2)}, u32[]{:S(2)}) async-start(f32[32,1,128]{2,1,0:T(1,128)} %broadcast_in_dim.21), calls=%async_computation.3 | async-start | bytes 32768 | tf_op jit(solution)/shard_map/all_to_all | solution.py:40
  161.3 7.5 %all-to-all-done.3 = f32[32,1,128]{2,1,0:T(1,128)S(1)} async-done(((f32[32,1,128]{2,1,0:T(1,128)}), f32[32,1,128]{2,1,0:T(1,128)S(1)}, u32[]{:S(2)}, u32[]{:S(2)}) %all-to-all-start.3) | async-done | bytes 16416 | tf_op jit(solution)/shard_map/all_to_all | solution.py:40
  169.7 3.8 %fusion.2 = f32[3,4,8,128]{3,2,1,0:T(8,128)} fusion(f32[3,4,8,128]{3,2,1,0:T(8,128)S(1)} %get-tuple-element.36, f32[3,4,8,128]{3,2,1,0:T(8,128)S(1)} %get-tuple-element.40, f32[3,4,8,128]{3,2,1,0:T(8,128)S(1)} %copy-done.8, f32[5,3,4,8,128]{4,3,2,1,0:T(8,128)S(1)} %copy-done.6, f32[]{:T(128)} %bitcast.121, f32[]{:T(128)} %bitcast.119, f32[]{:T(128)} %bitcast.117, ...), kind=kLoop, calls=%fused_computation.69 | loop fusion | flops 135168 | bytes 393236 | tf_op jit(solution)/shard_map/sub | solution.py:84
  (103 shorter events, 18.0 us)
Async XLA Ops:
  1.5 17.4 %copy-start.4 = (f32[3,4,8,128]{3,2,1,0:T(8,128)S(1)}, f32[3,4,8,128]{3,2,1,0:T(8,128)}, u32[]{:S(2)}) copy-start(f32[3,4,8,128]{3,2,1,0:T(8,128)} %param.10) | copy-start | bytes 147460
  1.5 17.4 %collective-permute-start = (f32[7,3,8,128]{3,2,1,0:T(8,128)S(1)}, f32[7,3,8,128]{3,2,1,0:T(8,128)S(1)}, u32[]{:S(2)}, u32[]{:S(2)}) collective-permute-start(f32[7,3,8,128]{3,2,1,0:T(8,128)S(1)} %get-tuple-element.86), channel_id=1, source_target_pairs={{0,16},{16,32},{32,48},{48,64},{64,80},{80,96},{96,112},{112,128},... | collective-permute-start | bytes 258056 | tf_op jit(solution)/shard_map/ppermute | solution.py:27
  6.9 12.9 %collective-permute-start.1 = (f32[7,3,8,128]{3,2,1,0:T(8,128)S(1)}, f32[7,3,8,128]{3,2,1,0:T(8,128)S(1)}, u32[]{:S(2)}, u32[]{:S(2)}) collective-permute-start(f32[7,3,8,128]{3,2,1,0:T(8,128)S(1)} %get-tuple-element.87), channel_id=1, source_target_pairs={{16,0},{32,16},{48,32},{64,48},{80,64},{96,80},{112,96},{128,112},... | collective-permute-start | bytes 258056 | tf_op jit(solution)/shard_map/ppermute | solution.py:29
  18.9 0.9 copy-start.3
  18.9 0.9 copy-start.5
  19.8 4.3 %collective-permute-start.2 = (f32[7,10,3,128]{3,2,1,0:T(4,128)S(1)}, f32[7,10,3,128]{3,2,1,0:T(4,128)S(1)}, u32[]{:S(2)}, u32[]{:S(2)}) collective-permute-start(f32[7,10,3,128]{3,2,1,0:T(4,128)S(1)} %get-tuple-element.52), channel_id=1, source_target_pairs={{0,1},{1,2},{2,3},{3,4},{4,5},{5,6},{6,7},{7,8},{8,9},{9,10},{10,1... | collective-permute-start | bytes 322568 | tf_op jit(solution)/shard_map/ppermute | solution.py:27
  21.1 6.9 %collective-permute-start.3 = (f32[7,10,3,128]{3,2,1,0:T(4,128)S(1)}, f32[7,10,3,128]{3,2,1,0:T(4,128)S(1)}, u32[]{:S(2)}, u32[]{:S(2)}) collective-permute-start(f32[7,10,3,128]{3,2,1,0:T(4,128)S(1)} %get-tuple-element.53), channel_id=1, source_target_pairs={{1,0},{2,1},{3,2},{4,3},{5,4},{6,5},{7,6},{8,7},{9,8},{10,9},{11,1... | collective-permute-start | bytes 322568 | tf_op jit(solution)/shard_map/ppermute | solution.py:29
  28.1 0.8 copy-start
  28.9 1.1 copy-start.1
  29.0 1.1 slice-start
  30.3 0.9 copy-start.2
  31.3 0.8 copy-start.7
  32.9 71.8 %copy-start.6 = (f32[5,3,4,8,128]{4,3,2,1,0:T(8,128)S(1)}, f32[5,3,4,8,128]{4,3,2,1,0:T(8,128)}, u32[]{:S(2)}) copy-start(f32[5,3,4,8,128]{4,3,2,1,0:T(8,128)} %param.16) | copy-start | bytes 737284
  108.0 8.5 %collective-permute-start.4 = (f32[3,3,8,128]{3,2,1,0:T(8,128)S(1)}, f32[3,3,8,128]{3,2,1,0:T(8,128)S(1)}, u32[]{:S(2)}, u32[]{:S(2)}) collective-permute-start(f32[3,3,8,128]{3,2,1,0:T(8,128)S(1)} %get-tuple-element.88), channel_id=1, source_target_pairs={{0,16},{16,32},{32,48},{48,64},{64,80},{80,96},{96,112},{112,128},... | collective-permute-start | bytes 110600 | tf_op jit(solution)/shard_map/ppermute | solution.py:27
  112.4 5.3 %collective-permute-start.5 = (f32[3,3,8,128]{3,2,1,0:T(8,128)S(1)}, f32[3,3,8,128]{3,2,1,0:T(8,128)S(1)}, u32[]{:S(2)}, u32[]{:S(2)}) collective-permute-start(f32[3,3,8,128]{3,2,1,0:T(8,128)S(1)} %get-tuple-element.89), channel_id=1, source_target_pairs={{16,0},{32,16},{48,32},{64,48},{80,64},{96,80},{112,96},{128,112},... | collective-permute-start | bytes 110600 | tf_op jit(solution)/shard_map/ppermute | solution.py:29
  117.8 3.6 %collective-permute-start.6 = (f32[3,10,3,128]{3,2,1,0:T(4,128)S(1)}, f32[3,10,3,128]{3,2,1,0:T(4,128)S(1)}, u32[]{:S(2)}, u32[]{:S(2)}) collective-permute-start(f32[3,10,3,128]{3,2,1,0:T(4,128)S(1)} %get-tuple-element.84), channel_id=1, source_target_pairs={{0,1},{1,2},{2,3},{3,4},{4,5},{5,6},{6,7},{7,8},{8,9},{9,10},{10,1... | collective-permute-start | bytes 138248 | tf_op jit(solution)/shard_map/ppermute | solution.py:27
  120.0 5.0 %collective-permute-start.7 = (f32[3,10,3,128]{3,2,1,0:T(4,128)S(1)}, f32[3,10,3,128]{3,2,1,0:T(4,128)S(1)}, u32[]{:S(2)}, u32[]{:S(2)}) collective-permute-start(f32[3,10,3,128]{3,2,1,0:T(4,128)S(1)} %get-tuple-element.85), channel_id=1, source_target_pairs={{1,0},{2,1},{3,2},{4,3},{5,4},{6,5},{7,6},{8,7},{9,8},{10,9},{11,1... | collective-permute-start | bytes 138248 | tf_op jit(solution)/shard_map/ppermute | solution.py:29
  131.0 20.3 %all-to-all-start.2 = ((f32[32,1,128]{2,1,0:T(1,128)}), f32[32,1,128]{2,1,0:T(1,128)S(1)}, u32[]{:S(2)}, u32[]{:S(2)}) async-start(f32[32,1,128]{2,1,0:T(1,128)} %broadcast_in_dim.20), calls=%async_computation.2 | async-start | bytes 32768 | tf_op jit(solution)/shard_map/all_to_all | solution.py:40
  151.9 17.8 %copy-start.8 = (f32[3,4,8,128]{3,2,1,0:T(8,128)S(1)}, f32[3,4,8,128]{3,2,1,0:T(8,128)}, u32[]{:S(2)}) copy-start(f32[3,4,8,128]{3,2,1,0:T(8,128)} %param.14) | copy-start | bytes 147460
  151.9 16.8 %all-to-all-start.3 = ((f32[32,1,128]{2,1,0:T(1,128)}), f32[32,1,128]{2,1,0:T(1,128)S(1)}, u32[]{:S(2)}, u32[]{:S(2)}) async-start(f32[32,1,128]{2,1,0:T(1,128)} %broadcast_in_dim.21), calls=%async_computation.3 | async-start | bytes 32768 | tf_op jit(solution)/shard_map/all_to_all | solution.py:40

commit v2 on v1

v2 whole, which is shorter than its diff:
```python
import jax
import jax.numpy as jnp
from jax import lax
from jax.experimental import pallas as pl
from jax.experimental.pallas import tpu as pltpu
from jax.sharding import Mesh
from jax.sharding import PartitionSpec as P

M = 5
SWEEPS = 3
AXES = ("gx_0", "gx_1", "gx_2", "gy_0", "gy_1")
GX = ("gx_0", "gx_1", "gx_2")
GY = ("gy_0", "gy_1")
CHAIN = ("gx_1", "gx_2")
PLANE = ("gx_0", "gy_0", "gy_1")

REG = 0.05
FLOOR = 0.001
PAIRS = [(i, j) for i in range(M) for j in range(i, M)]
RHS = len(PAIRS)
PREV = RHS + M
NORM = PREV + M

ROWS = 16
OWN = 3
FIELD = 3
STATIC = 4


def edge_rows(with_static):
    if with_static:
        return [(1, 3, 24, 0, False), (1, 4, 24, 24, True), (2, 8, 16, 48, True), (2, 6, 18, 64, False), (3, 9, 12, 88, False)], 104
    return [(1, 3, 24, 0, False), (2, 6, 18, 24, False), (3, 9, 12, 48, False)], 64


def call(kernel, outs, scratch=(), flops=20000):
    return pl.pallas_call(
        kernel,
        out_shape=[jax.ShapeDtypeStruct(s, jnp.float32) for s in outs],
        scratch_shapes=[pltpu.VMEM(s, jnp.float32) for s in scratch],
        compiler_params=pltpu.CompilerParams(vmem_limit_bytes=8 * 1024 * 1024),
        cost_estimate=pl.CostEstimate(flops=flops, bytes_accessed=100000, transcendentals=0),
    )


def pack_first(vel, forcing, visc, up, down):
    cx = vel.shape[1]
    for out, first_u, first_s in ((up, cx - 3, cx - 2), (down, 0, 0)):
        for d in range(3):
            for c in range(3):
                out[d * 3 + c] = vel[c, first_u + d]
        for d in range(2):
            for c in range(3):
                out[9 + d * 4 + c] = forcing[c, first_s + d]
            out[9 + d * 4 + 3] = visc[first_s + d]


def field_tile(vel, left, right, tile):
    plane, c = divmod(tile, FIELD)
    cx = vel.shape[1]
    if plane < 3:
        return left[tile]
    if plane < 3 + cx:
        return vel[c, plane - 3]
    return right[tile - (3 + cx) * FIELD]


def static_tile(forcing, visc, left, right, tile):
    plane, c = divmod(tile, STATIC)
    cx = visc.shape[0]
    if plane < 2:
        return left[9 + tile]
    if plane < 2 + cx:
        return forcing[c, plane - 2] if c < 3 else visc[plane - 2]
    return right[9 + tile - (2 + cx) * STATIC]


def pack_second(with_static, *refs):
    if with_static:
        vel, forcing, visc, left, right, up, down, tiles, fixed = refs
        for t in range(8 * STATIC):
            fixed[t * 8 : t * 8 + 8] = static_tile(forcing, visc, left, right, t)
    else:
        vel, left, right, up, down, tiles = refs
        fixed = None
    for t in range(10 * FIELD):
        tiles[t * 8 : t * 8 + 8] = field_tile(vel, left, right, t)
    pieces, _ = edge_rows(with_static)
    for dist, first, count, row, static in pieces:
        src = fixed if static else tiles
        up[row : row + count] = src[pl.ds(first * 8 + 8 - dist, count, stride=8), :]
        down[row : row + count] = src[pl.ds(first * 8 + dist - 1, count, stride=8), :]


def fill_frames(with_static, south, north, frames, fixed):
    pieces, _ = edge_rows(with_static)
    for dist, first, count, row, static in pieces:
        dst = fixed if static else frames
        dst[pl.ds(first * ROWS + OWN - dist, count, stride=ROWS), :] = south[row : row + count]
        dst[pl.ds(first * ROWS + OWN + 7 + dist, count, stride=ROWS), :] = north[row : row + count]


def sweeps(frames, fixed, coef, one, two):
    lane = lax.broadcasted_iota(jnp.int32, (ROWS, 128), 1)
    field = lambda p, c: frames[(p * FIELD + c) * ROWS : (p * FIELD + c + 1) * ROWS]
    still = lambda s, c: fixed[(s * STATIC + c) * ROWS : (s * STATIC + c + 1) * ROWS]
    for s in range(8):
        a = [field(s + 1, c) for c in range(3)]
        visc = still(s, 3)
        inv = 1.0 / (1.0 + 6.0 * visc + jnp.abs(a[0]) + jnp.abs(a[1]) + jnp.abs(a[2]))
        for k in range(3):
            low = (visc + jnp.maximum(a[k], 0.0)) * inv
            high = (visc - jnp.minimum(a[k], 0.0)) * inv
            if k == 2:
                low = jnp.where(lane > 0, low, 0.0)
                high = jnp.where(lane < 127, high, 0.0)
            coef[s, 2 * k] = low
            coef[s, 2 * k + 1] = high
            coef[s, 6 + k] = (still(s, k) + a[k]) * inv

    def relax(src, s, c):
        mid = src(0)
        total = coef[s, 6 + c] + coef[s, 0] * src(-1) + coef[s, 1] * src(1)
        total = total + coef[s, 2] * pltpu.roll(mid, 1, 0) + coef[s, 3] * pltpu.roll(mid, ROWS - 1, 0)
        return total + coef[s, 4] * pltpu.roll(mid, 1, 1) + coef[s, 5] * pltpu.roll(mid, 127, 1)

    for s in range(8):
        for c in range(3):
            one[s, c] = relax(lambda d: field(s + 1 + d, c), s, c)
    for s in range(1, 7):
        for c in range(3):
            two[s, c] = relax(lambda d: one[s + d, c], s, c)
    out = {}
    for s in range(2, 6):
        for c in range(3):
            out[c, s - 2] = relax(lambda d: two[s + d, c], s, c)[OWN : OWN + 8]
    return out


def lanes(row, shape=(1, 128)):
    return lax.broadcasted_iota(jnp.int32, shape, 1)


def spread(row, parts):
    lane = lanes(row)
    for k, part in parts.items():
        whole = jnp.sum(jnp.sum(part, axis=0, keepdims=True), axis=1, keepdims=True)
        row = jnp.where(lane == k, whole, row)
    return row


def gram_part(hist, prev, out):
    tiles = [(c, p) for c in range(3) for p in range(hist.shape[2])]
    parts = {}
    for k, (i, j) in enumerate(PAIRS):
        parts[k] = sum(hist[i, c, p] * hist[j, c, p] for c, p in tiles)
    for i in range(M):
        parts[PREV + i] = sum(hist[i, c, p] * prev[c, p] for c, p in tiles)
    out[...] = spread(jnp.zeros((1, 128), jnp.float32), parts)


def first_map(vel, forcing, visc, left, right, south, north, hist, prev, gram, value, newest, fixed, payload, frames, coef, one, two):
    frames[...] = jnp.zeros_like(frames)
    fixed[...] = jnp.zeros_like(fixed)
    for t in range(8 * STATIC):
        fixed[t * ROWS + OWN : t * ROWS + OWN + 8] = static_tile(forcing, visc, left, right, t)
    for t in range(10 * FIELD):
        frames[t * ROWS + OWN : t * ROWS + OWN + 8] = field_tile(vel, left, right, t)
    fill_frames(True, south, north, frames, fixed)
    result = sweeps(frames, fixed, coef, one, two)
    resid = {}
    fresh = {}
    for (c, p), tile in result.items():
        value[c, p] = tile
        resid[c, p] = tile - vel[c, p]
        fresh[c, p] = resid[c, p] - prev[c, p]
        newest[c, p] = fresh[c, p]
    parts = {RHS + i: sum(hist[i, c, p] * r for (c, p), r in resid.items()) for i in range(M)}
    parts[NORM] = sum(f * f for f in fresh.values())
    row = spread(gram[...], parts)
    for k in range(payload.shape[0]):
        payload[k] = row


def second_map(vel, left, right, south, north, fixed, hist, newest, value, resid, payload, frames, coef, one, two):
    frames[...] = jnp.zeros_like(frames)
    for t in range(10 * FIELD):
        frames[t * ROWS + OWN : t * ROWS + OWN + 8] = field_tile(vel, left, right, t)
    fill_frames(False, south, north, frames, None)
    result = sweeps(frames, fixed, coef, one, two)
    for (c, p), tile in result.items():
        value[c, p] = tile
        result[c, p] = tile - vel[c, p]
        resid[c, p] = result[c, p]
    parts = {i: sum(hist[i + 1, c, p] * r for (c, p), r in result.items()) for i in range(M - 1)}
    parts[M - 1] = sum(newest[c, p] * r for (c, p), r in result.items())
    row = spread(jnp.zeros((1, 128), jnp.float32), parts)
    for k in range(payload.shape[0]):
        payload[k] = row


def entry(row, k):
    return jnp.sum(jnp.where(lanes(row) == k, row, 0.0), axis=1, keepdims=True)


def solve(gram, rhs, entries):
    shift = (REG / M) * sum(gram[i, i] for i in range(M)) + FLOOR * entries
    a = {(i, j): gram[min(i, j), max(i, j)] for i in range(M) for j in range(M)}
    for i in range(M):
        a[i, i] = a[i, i] + shift
    r = list(rhs)
    inv = []
    for k in range(M):
        inv.append(1.0 / a[k, k])
        for i in range(k + 1, M):
            f = a[k, i] * inv[k]
            for j in range(i, M):
                a[i, j] = a[i, j] - f * a[k, j]
            r[i] = r[i] - f * r[k]
    out = [None] * M
    for i in reversed(range(M)):
        acc = r[i]
        for j in range(i + 1, M):
            acc = acc - a[i, j] * out[j]
        out[i] = acc * inv[i]
    return out


def gathered(rows):
    total = rows[0]
    for k in range(1, rows.shape[0]):
        total = total + rows[k]
    return total


def mix_first(entries, rows, value, hist, field, up, down):
    row = gathered(rows)
    s = [entry(row, k) for k in range(PREV)]
    gram = {pair: s[k] for k, pair in enumerate(PAIRS)}
    gamma = [jnp.broadcast_to(g, (8, 128)) for g in solve(gram, s[RHS:PREV], entries)]
    cx = value.shape[1]
    for c in range(3):
        for p in range(cx):
            tile = value[c, p]
            for j in range(M):
                tile = tile - gamma[j] * hist[j, c, p]
            field[c, p] = tile
            if p >= cx - 3:
                up[(p - cx + 3) * 3 + c] = tile
            if p < 3:
                down[p * 3 + c] = tile


def mix_second(entries, rows, first_rows, value, hist, first_value, prev, field):
    row = gathered(first_rows)
    s = [entry(row, k) for k in range(NORM + 1)]
    gram = {}
    for k, (i, j) in enumerate(PAIRS):
        if i > 0:
            gram[i - 1, j - 1] = s[k]
    for i in range(M - 1):
        gram[i, M - 1] = s[RHS + 1 + i] - s[PREV + 1 + i]
    gram[M - 1, M - 1] = s[NORM]
    row = gathered(rows)
    gamma = solve(gram, [entry(row, k) for k in range(M)], entries)
    gamma = [jnp.broadcast_to(g, (8, 128)) for g in gamma]
    for c in range(3):
        for p in range(value.shape[1]):
            tile = value[c, p]
            for j in range(M - 1):
                tile = tile - gamma[j] * hist[j + 1, c, p]
            field[c, p] = tile - gamma[M - 1] * (first_value[c, p] - prev[c, p])


def neighbours(axis, up, down):
    count = lax.axis_size(axis)
    ends = count - 1
    before = lax.ppermute(up, axis, [(i, i + 1) for i in range(ends)])
    after = lax.ppermute(down, axis, [(i + 1, i) for i in range(ends)])
    return before, after


def exchange(payload):
    row = jnp.sum(lax.all_to_all(payload, CHAIN, 0, 0), axis=(0, 1))
    rows = jnp.broadcast_to(row[None, None, :], (lax.axis_size(PLANE), 1, 128))
    return lax.all_to_all(rows, PLANE, 0, 0)


def local(velocity, forcing, viscosity, residual_prev, value_prev, hist_res, hist_val):
    shape = velocity.shape
    entries = 1.0 * velocity.size * lax.axis_size(GX) * lax.axis_size(GY)
    fan = (lax.axis_size(CHAIN), 1, 128)
    work = ((8, 9, ROWS, 128), (8, 3, ROWS, 128), (8, 3, ROWS, 128))
    frames = (10 * FIELD * ROWS, 128)
    fixed = (8 * STATIC * ROWS, 128)

    up, down = call(pack_first, [(17, 8, 128)] * 2)(velocity, forcing, viscosity)
    left, right = neighbours(GX, up, down)
    (gram,) = call(gram_part, [(1, 128)], flops=4000000)(hist_res, residual_prev)
    edge = (edge_rows(True)[1], 128)
    up, down = call(
        lambda *refs: pack_second(True, *refs), [edge, edge], [(10 * FIELD * 8, 128), (8 * STATIC * 8, 128)]
    )(velocity, forcing, viscosity, left, right)
    south, north = neighbours(GY, up, down)
    value, newest, static, payload = call(first_map, [shape, shape, fixed, fan], [frames, *work])(
        velocity, forcing, viscosity, left, right, south, north, hist_res, residual_prev, gram
    )
    sums = exchange(payload)
    field, up, down = call(lambda *refs: mix_first(entries, *refs), [shape, (9, 8, 128), (9, 8, 128)])(
        sums, value, hist_val
    )
    left, right = neighbours(GX, up, down)
    edge = (edge_rows(False)[1], 128)
    up, down = call(lambda *refs: pack_second(False, *refs), [edge, edge], [(10 * FIELD * 8, 128)])(
        field, left, right
    )
    south, north = neighbours(GY, up, down)
    value_next, resid, payload = call(second_map, [shape, shape, fan], [frames, *work])(
        field, left, right, south, north, static, hist_res, newest
    )
    (out,) = call(lambda *refs: mix_second(entries, *refs), [shape])(
        exchange(payload), sums, value_next, hist_val, value, value_prev
    )
    return (out, resid)


def build(torus):
    in_specs = (
        P(None, GX, GY, None),
        P(None, GX, GY, None),
        P(GX, GY, None),
        P(None, GX, GY, None),
        P(None, GX, GY, None),
        P(None, None, GX, GY, None),
        P(None, None, GX, GY, None),
    )
    out_specs = (P(None, GX, GY, None), P(None, GX, GY, None))
    return jax.shard_map(local, mesh=torus, in_specs=in_specs, out_specs=out_specs, check_vma=False)


def solution(mesh):
    return build(Mesh(mesh.devices.reshape(2, 16, 2, 2, 8), AXES))
```

time: 175 us -> 127 us (0.73)
  blocking collectives: 44 us -> 79.8 us
  local copies, waits for them, and re-layouts: 32.1 us -> 2.39 us
  waiting for transfers between devices: 29.7 us -> 11 us
  other arithmetic: 18.1 us -> 0.1 us
  starting transfers between devices: 46.5 us -> 29.9 us
  Pallas kernels: 0 us -> 2.77 us
    all_to_all x2 -> x4, blocking collectives: 44 us -> 79.8 us  [the longest x2 46.1 us: exchange(): row = jnp.sum(lax.all_to_all(payload, CHAIN, 0, 0), axis=(0, 1))]
    another operation x3 -> x0, local copies, waits for them, and re-layouts: 25.2 us -> none  [the longest x1 16.3 us: local(): sums = total_over_devices(jnp.pad(jnp.stack(sums), (0, 128 - len(sums))))]
    all_to_all x2 -> x0, waiting for transfers between devices: 18.5 us -> none  [total_over_devices(): row = jnp.sum(lax.all_to_all(rows, group, 0, 0), axis=(0, 1))]
    all_to_all x2 -> x0, starting transfers between devices: 16.8 us -> none  [total_over_devices(): row = jnp.sum(lax.all_to_all(rows, group, 0, 0), axis=(0, 1))]
    another operation x10 -> x0, other arithmetic: 4.42 us -> none  [the longest x6 2.29 us: solve_small(): factor = jnp.linalg.cholesky(gram + shift * jnp.eye(M, dtype=jnp.float32))]
    reduce_sum x9 -> x2, other arithmetic: 4.37 us -> 0.1 us  [exchange(): row = jnp.sum(lax.all_to_all(payload, CHAIN, 0, 0), axis=(0, 1))]
    sub x1 -> x0, other arithmetic: 3.76 us -> none  [mix(): value = value - gamma[j] * history[j]]
    max x6 -> x0, other arithmetic: 3.37 us -> none  [relax(): upward = jnp.maximum(vel, 0.0)]
  transfers between devices with their start and end apart: 10 -> 8, of which waited for: 7 -> 4; matrix products, arithmetic and copies ran while one was open for 2% -> 0% of each run, Pallas kernels for 0% -> 0%
where the time goes in v2:
time: 127 us
  blocking collectives  79.8 us (63%)
  starting transfers between devices  29.9 us (24%)
  waiting for transfers between devices  11 us (9%)
  Pallas kernels  2.77 us (2%)
  local copies, waits for them, and re-layouts  2.39 us (2%)
    all_to_all x2, blocking collectives, exchange(): row = jnp.sum(lax.all_to_all(payload, CHAIN, 0, 0), axis=(0, 1))  46.1 us
    all_to_all x2, blocking collectives, exchange(): return lax.all_to_all(rows, PLANE, 0, 0)  33.7 us
    ppermute x4, starting transfers between devices, neighbours(): after = lax.ppermute(down, axis, [(i + 1, i) for i in range(ends)])  16.6 us
    ppermute x4, starting transfers between devices, neighbours(): before = lax.ppermute(up, axis, [(i, i + 1) for i in range(ends)])  13.3 us
    ppermute x4, waiting for transfers between devices, neighbours(): after = lax.ppermute(down, axis, [(i + 1, i) for i in range(ends)])  10.9 us
  transfers between devices with their start and end apart: 8, of which 4 were waited for; matrix products, arithmetic and copies ran while one was open for 0% of the time, Pallas kernels for 0%

profile of v2, /device:TPU:1, one launch (start us, length us, event | category | flops | bytes accessed | tf_op | source)
XLA Modules:
  0.0 126.7 jit_solution(10168447709006017093)
XLA Ops:
  0.7 0.8 copy-done.2
  1.5 0.8 copy-done.3
  2.3 0.7 copy-done.5
  3.0 5.4 %collective-permute-start = (f32[17,8,128]{2,1,0:T(8,128)S(1)}, f32[17,8,128]{2,1,0:T(8,128)S(1)}, u32[]{:S(2)}, u32[]{:S(2)}) collective-permute-start(f32[17,8,128]{2,1,0:T(8,128)S(1)} %get-tuple-element.18), channel_id=1, source_target_pairs={{0,16},{16,32},{32,48},{48,64},{64,80},{80,96},{96,112},{112,128},... | collective-permute-start | bytes 208904 | tf_op jit(solution)/shard_map/ppermute | solution.py:278
  8.4 12.1 %collective-permute-start.1 = (f32[17,8,128]{2,1,0:T(8,128)S(1)}, f32[17,8,128]{2,1,0:T(8,128)S(1)}, u32[]{:S(2)}, u32[]{:S(2)}) collective-permute-start(f32[17,8,128]{2,1,0:T(8,128)S(1)} %get-tuple-element.19), channel_id=1, source_target_pairs={{16,0},{32,16},{48,32},{64,48},{80,64},{96,80},{112,96},{128,112},... | collective-permute-start | bytes 208904 | tf_op jit(solution)/shard_map/ppermute | solution.py:279
  20.5 0.9 collective-permute-done.1.refs_4_.right
  21.4 1.3 %collective-permute-start.2 = (f32[104,128]{1,0:T(8,128)S(1)}, f32[104,128]{1,0:T(8,128)S(1)}, u32[]{:S(2)}, u32[]{:S(2)}) collective-permute-start(f32[104,128]{1,0:T(8,128)S(1)} %get-tuple-element.20), channel_id=1, source_target_pairs={{0,1},{1,2},{2,3},{3,4},{4,5},{5,6},{6,7},{7,8},{8,9},{9,10},{10,1... | collective-permute-start | bytes 159752 | tf_op jit(solution)/shard_map/ppermute | solution.py:278
  22.7 1.3 %collective-permute-start.3 = (f32[104,128]{1,0:T(8,128)S(1)}, f32[104,128]{1,0:T(8,128)S(1)}, u32[]{:S(2)}, u32[]{:S(2)}) collective-permute-start(f32[104,128]{1,0:T(8,128)S(1)} %get-tuple-element.21), channel_id=1, source_target_pairs={{1,0},{2,1},{3,2},{4,3},{5,4},{6,5},{7,6},{8,7},{9,8},{10,9},{11,1... | collective-permute-start | bytes 159752 | tf_op jit(solution)/shard_map/ppermute | solution.py:279
  24.0 0.2 shard_map.88.gram
  24.2 3.4 %collective-permute-done.3.north = f32[104,128]{1,0:T(8,128)S(1)} collective-permute-done((f32[104,128]{1,0:T(8,128)S(1)}, f32[104,128]{1,0:T(8,128)S(1)}, u32[]{:S(2)}, u32[]{:S(2)}) %collective-permute-start.3) | collective-permute-done | bytes 53280 | tf_op jit(solution)/shard_map/ppermute | solution.py:279
  27.6 0.5 shard_map.89
  28.1 25.8 %all_to_all.20 = f32[32,1,128]{2,1,0:T(1,128)S(1)} all-to-all(f32[32,1,128]{2,1,0:T(1,128)S(1)} %get-tuple-element.22), channel_id=1, replica_groups=mesh['gx_0'=2,'gx_1'=16,'gx_2'=2,'gy_0'=2,'gy_1'=8] {'gx_1','gx_2'}, dimensions={0} | all-to-all | bytes 32768 | tf_op jit(solution)/shard_map/all_to_all | solution.py:284
  54.0 18.3 %all_to_all.21.refs_0_.refs_1_ = f32[32,1,128]{2,1,0:T(1,128)S(1)} all-to-all(f32[32,1,128]{2,1,0:T(1,128)S(1)} %broadcast_in_dim.4), channel_id=1, replica_groups=mesh['gx_0'=2,'gx_1'=16,'gx_2'=2,'gy_0'=2,'gy_1'=8] {'gx_0','gy_0','gy_1'}, dimensions={0} | all-to-all | bytes 32768 | tf_op jit(solution)/shard_map/all_to_all | solution.py:286
  72.4 0.2 shard_map.90
  72.6 4.4 %collective-permute-start.4 = (f32[9,8,128]{2,1,0:T(8,128)S(1)}, f32[9,8,128]{2,1,0:T(8,128)S(1)}, u32[]{:S(2)}, u32[]{:S(2)}) collective-permute-start(f32[9,8,128]{2,1,0:T(8,128)S(1)} %get-tuple-element.25), channel_id=1, source_target_pairs={{0,16},{16,32},{32,48},{48,64},{64,80},{80,96},{96,112},{112,128},... | collective-permute-start | bytes 110600 | tf_op jit(solution)/shard_map/ppermute | solution.py:278
  77.0 1.9 %collective-permute-start.5 = (f32[9,8,128]{2,1,0:T(8,128)S(1)}, f32[9,8,128]{2,1,0:T(8,128)S(1)}, u32[]{:S(2)}, u32[]{:S(2)}) collective-permute-start(f32[9,8,128]{2,1,0:T(8,128)S(1)} %get-tuple-element.26), channel_id=1, source_target_pairs={{16,0},{32,16},{48,32},{64,48},{80,64},{96,80},{112,96},{128,112},... | collective-permute-start | bytes 110600 | tf_op jit(solution)/shard_map/ppermute | solution.py:279
  78.9 3.3 %collective-permute-done.5.refs_2_.right = f32[9,8,128]{2,1,0:T(8,128)S(1)} collective-permute-done((f32[9,8,128]{2,1,0:T(8,128)S(1)}, f32[9,8,128]{2,1,0:T(8,128)S(1)}, u32[]{:S(2)}, u32[]{:S(2)}) %collective-permute-start.5) | collective-permute-done | bytes 36896 | tf_op jit(solution)/shard_map/ppermute | solution.py:279
  82.3 2.2 %collective-permute-start.6 = (f32[64,128]{1,0:T(8,128)S(1)}, f32[64,128]{1,0:T(8,128)S(1)}, u32[]{:S(2)}, u32[]{:S(2)}) collective-permute-start(f32[64,128]{1,0:T(8,128)S(1)} %get-tuple-element.27), channel_id=1, source_target_pairs={{0,1},{1,2},{2,3},{3,4},{4,5},{5,6},{6,7},{7,8},{8,9},{9,10},{10,1... | collective-permute-start | bytes 98312 | tf_op jit(solution)/shard_map/ppermute | solution.py:278
  84.5 1.3 %collective-permute-start.7 = (f32[64,128]{1,0:T(8,128)S(1)}, f32[64,128]{1,0:T(8,128)S(1)}, u32[]{:S(2)}, u32[]{:S(2)}) collective-permute-start(f32[64,128]{1,0:T(8,128)S(1)} %get-tuple-element.28), channel_id=1, source_target_pairs={{1,0},{2,1},{3,2},{4,3},{5,4},{6,5},{7,6},{8,7},{9,8},{10,9},{11,1... | collective-permute-start | bytes 98312 | tf_op jit(solution)/shard_map/ppermute | solution.py:279
  85.9 3.3 %collective-permute-done.7.north = f32[64,128]{1,0:T(8,128)S(1)} collective-permute-done((f32[64,128]{1,0:T(8,128)S(1)}, f32[64,128]{1,0:T(8,128)S(1)}, u32[]{:S(2)}, u32[]{:S(2)}) %collective-permute-start.7) | collective-permute-done | bytes 32800 | tf_op jit(solution)/shard_map/ppermute | solution.py:279
  89.2 1.0 shard_map.92
  90.2 20.3 %all_to_all.22 = f32[32,1,128]{2,1,0:T(1,128)S(1)} all-to-all(f32[32,1,128]{2,1,0:T(1,128)S(1)} %get-tuple-element.31), channel_id=1, replica_groups=mesh['gx_0'=2,'gx_1'=16,'gx_2'=2,'gy_0'=2,'gy_1'=8] {'gx_1','gx_2'}, dimensions={0} | all-to-all | bytes 32768 | tf_op jit(solution)/shard_map/all_to_all | solution.py:284
  110.6 15.3 %all_to_all.23.refs_0_ = f32[32,1,128]{2,1,0:T(1,128)S(1)} all-to-all(f32[32,1,128]{2,1,0:T(1,128)S(1)} %broadcast_in_dim.5), channel_id=1, replica_groups=mesh['gx_0'=2,'gx_1'=16,'gx_2'=2,'gy_0'=2,'gy_1'=8] {'gx_0','gy_0','gy_1'}, dimensions={0} | all-to-all | bytes 32768 | tf_op jit(solution)/shard_map/all_to_all | solution.py:286
  125.9 0.8 shard_map.93
  (22 shorter events, 0.2 us)
Async XLA Ops:
  0.6 23.4 %copy-start = (f32[5,3,4,8,128]{4,3,2,1,0:T(8,128)S(1)}, f32[5,3,4,8,128]{4,3,2,1,0:T(8,128)}, u32[]{:S(2)}) copy-start(f32[5,3,4,8,128]{4,3,2,1,0:T(8,128)} %hist.5) | copy-start | bytes 737284
  0.6 0.8 copy-start.2
  1.5 0.8 copy-start.3
  2.3 0.7 copy-start.5
  3.0 17.5 %collective-permute-start = (f32[17,8,128]{2,1,0:T(8,128)S(1)}, f32[17,8,128]{2,1,0:T(8,128)S(1)}, u32[]{:S(2)}, u32[]{:S(2)}) collective-permute-start(f32[17,8,128]{2,1,0:T(8,128)S(1)} %get-tuple-element.18), channel_id=1, source_target_pairs={{0,16},{16,32},{32,48},{48,64},{64,80},{80,96},{96,112},{112,128},... | collective-permute-start | bytes 208904 | tf_op jit(solution)/shard_map/ppermute | solution.py:278
  8.4 15.6 %copy-start.4 = (f32[3,4,8,128]{3,2,1,0:T(8,128)S(1)}, f32[3,4,8,128]{3,2,1,0:T(8,128)}, u32[]{:S(2)}) copy-start(f32[3,4,8,128]{3,2,1,0:T(8,128)} %prev.3) | copy-start | bytes 147460
  8.4 13.0 %collective-permute-start.1 = (f32[17,8,128]{2,1,0:T(8,128)S(1)}, f32[17,8,128]{2,1,0:T(8,128)S(1)}, u32[]{:S(2)}, u32[]{:S(2)}) collective-permute-start(f32[17,8,128]{2,1,0:T(8,128)S(1)} %get-tuple-element.19), channel_id=1, source_target_pairs={{16,0},{32,16},{48,32},{64,48},{80,64},{96,80},{112,96},{128,112},... | collective-permute-start | bytes 208904 | tf_op jit(solution)/shard_map/ppermute | solution.py:279
  21.4 2.8 %collective-permute-start.2 = (f32[104,128]{1,0:T(8,128)S(1)}, f32[104,128]{1,0:T(8,128)S(1)}, u32[]{:S(2)}, u32[]{:S(2)}) collective-permute-start(f32[104,128]{1,0:T(8,128)S(1)} %get-tuple-element.20), channel_id=1, source_target_pairs={{0,1},{1,2},{2,3},{3,4},{4,5},{5,6},{6,7},{7,8},{8,9},{9,10},{10,1... | collective-permute-start | bytes 159752 | tf_op jit(solution)/shard_map/ppermute | solution.py:278
  22.7 4.9 %collective-permute-start.3 = (f32[104,128]{1,0:T(8,128)S(1)}, f32[104,128]{1,0:T(8,128)S(1)}, u32[]{:S(2)}, u32[]{:S(2)}) collective-permute-start(f32[104,128]{1,0:T(8,128)S(1)} %get-tuple-element.21), channel_id=1, source_target_pairs={{1,0},{2,1},{3,2},{4,3},{5,4},{6,5},{7,6},{8,7},{9,8},{10,9},{11,1... | collective-permute-start | bytes 159752 | tf_op jit(solution)/shard_map/ppermute | solution.py:279
  24.2 48.2 %copy-start.1 = (f32[5,3,4,8,128]{4,3,2,1,0:T(8,128)S(1)}, f32[5,3,4,8,128]{4,3,2,1,0:T(8,128)}, u32[]{:S(2)}) copy-start(f32[5,3,4,8,128]{4,3,2,1,0:T(8,128)} %refs_3_.1) | copy-start | bytes 737284
  72.6 6.4 %collective-permute-start.4 = (f32[9,8,128]{2,1,0:T(8,128)S(1)}, f32[9,8,128]{2,1,0:T(8,128)S(1)}, u32[]{:S(2)}, u32[]{:S(2)}) collective-permute-start(f32[9,8,128]{2,1,0:T(8,128)S(1)} %get-tuple-element.25), channel_id=1, source_target_pairs={{0,16},{16,32},{32,48},{48,64},{64,80},{80,96},{96,112},{112,128},... | collective-permute-start | bytes 110600 | tf_op jit(solution)/shard_map/ppermute | solution.py:278
  77.0 5.3 %collective-permute-start.5 = (f32[9,8,128]{2,1,0:T(8,128)S(1)}, f32[9,8,128]{2,1,0:T(8,128)S(1)}, u32[]{:S(2)}, u32[]{:S(2)}) collective-permute-start(f32[9,8,128]{2,1,0:T(8,128)S(1)} %get-tuple-element.26), channel_id=1, source_target_pairs={{16,0},{32,16},{48,32},{64,48},{80,64},{96,80},{112,96},{128,112},... | collective-permute-start | bytes 110600 | tf_op jit(solution)/shard_map/ppermute | solution.py:279
  82.3 3.6 %collective-permute-start.6 = (f32[64,128]{1,0:T(8,128)S(1)}, f32[64,128]{1,0:T(8,128)S(1)}, u32[]{:S(2)}, u32[]{:S(2)}) collective-permute-start(f32[64,128]{1,0:T(8,128)S(1)} %get-tuple-element.27), channel_id=1, source_target_pairs={{0,1},{1,2},{2,3},{3,4},{4,5},{5,6},{6,7},{7,8},{8,9},{9,10},{10,1... | collective-permute-start | bytes 98312 | tf_op jit(solution)/shard_map/ppermute | solution.py:278
  84.5 4.7 %collective-permute-start.7 = (f32[64,128]{1,0:T(8,128)S(1)}, f32[64,128]{1,0:T(8,128)S(1)}, u32[]{:S(2)}, u32[]{:S(2)}) collective-permute-start(f32[64,128]{1,0:T(8,128)S(1)} %get-tuple-element.28), channel_id=1, source_target_pairs={{1,0},{2,1},{3,2},{4,3},{5,4},{6,5},{7,6},{8,7},{9,8},{10,9},{11,1... | collective-permute-start | bytes 98312 | tf_op jit(solution)/shard_map/ppermute | solution.py:279
  90.2 35.7 %copy-start.6 = (f32[3,4,8,128]{3,2,1,0:T(8,128)S(1)}, f32[3,4,8,128]{3,2,1,0:T(8,128)}, u32[]{:S(2)}) copy-start(f32[3,4,8,128]{3,2,1,0:T(8,128)} %refs_5_.1) | copy-start | bytes 147460

commit v3 on v2

--- a/solution.py
+++ b/solution.py
@@ -33,71 +33,102 @@
     return [(1, 3, 24, 0, False), (2, 6, 18, 24, False), (3, 9, 12, 48, False)], 64
 
 
-def call(kernel, outs, scratch=(), flops=20000):
+def call(kernel, outs, scratch=(), flops=20000, **more):
     return pl.pallas_call(
         kernel,
         out_shape=[jax.ShapeDtypeStruct(s, jnp.float32) for s in outs],
-        scratch_shapes=[pltpu.VMEM(s, jnp.float32) for s in scratch],
+        scratch_shapes=[pltpu.VMEM(s, jnp.float32) if isinstance(s, tuple) else s for s in scratch],
         compiler_params=pltpu.CompilerParams(vmem_limit_bytes=8 * 1024 * 1024),
         cost_estimate=pl.CostEstimate(flops=flops, bytes_accessed=100000, transcendentals=0),
-    )
-
-
-def pack_first(vel, forcing, visc, up, down):
+        **more,
+    )
+
+
+def place(axes):
+    index = 0
+    count = 1
+    for axis in axes:
+        index = index * lax.axis_size(axis) + lax.axis_index(axis)
+        count = count * lax.axis_size(axis)
+    return lax.rem(index, 2) == 1, index == 0, index == count - 1
+
+
+def pack_first(vel, forcing, visc, even_pair, odd_pair, vel_near, forcing_near, visc_near, sem):
     cx = vel.shape[1]
-    for out, first_u, first_s in ((up, cx - 3, cx - 2), (down, 0, 0)):
-        for d in range(3):
-            for c in range(3):
-                out[d * 3 + c] = vel[c, first_u + d]
-        for d in range(2):
-            for c in range(3):
-                out[9 + d * 4 + c] = forcing[c, first_s + d]
-            out[9 + d * 4 + 3] = visc[first_s + d]
+    odd, _, _ = place(GX)
+    copies = []
+    for out, low in ((even_pair, odd), (odd_pair, jnp.logical_not(odd))):
+        three = pl.ds(jnp.where(low, 0, cx - 3), 3)
+        two = pl.ds(jnp.where(low, 0, cx - 2), 2)
+        pieces = [(vel.at[c, three], out.at[pl.ds(3 * c, 3)]) for c in range(3)]
+        pieces += [(forcing.at[c, two], out.at[pl.ds(9 + 2 * c, 2)]) for c in range(3)]
+        pieces += [(visc.at[two], out.at[pl.ds(15, 2)])]
+        for src, dst in pieces:
+            copies.append(pltpu.make_async_copy(src, dst, sem.at[len(copies)]))
+            copies[-1].start()
+    for src, dst in ((vel, vel_near), (forcing, forcing_near), (visc, visc_near)):
+        copies.append(pltpu.make_async_copy(src, dst, sem.at[len(copies)]))
+        copies[-1].start()
+    for copy in copies:
+        copy.wait()
+
+
+def arrived(axes, even_pair, odd_pair):
+    odd, first, last = place(axes)
+    before = lambda i: jnp.where(odd, even_pair[0, i], jnp.where(first, 0.0, odd_pair[0, i]))
+    after = lambda i: jnp.where(odd, jnp.where(last, 0.0, odd_pair[1, i]), even_pair[1, i])
+    return before, after
 
 
 def field_tile(vel, left, right, tile):
     plane, c = divmod(tile, FIELD)
     cx = vel.shape[1]
     if plane < 3:
-        return left[tile]
+        return left(3 * c + plane)
     if plane < 3 + cx:
         return vel[c, plane - 3]
-    return right[tile - (3 + cx) * FIELD]
+    return right(3 * c + plane - 3 - cx)
 
 
 def static_tile(forcing, visc, left, right, tile):
     plane, c = divmod(tile, STATIC)
     cx = visc.shape[0]
     if plane < 2:
-        return left[9 + tile]
+        return left(9 + 2 * c + plane)
     if plane < 2 + cx:
         return forcing[c, plane - 2] if c < 3 else visc[plane - 2]
-    return right[9 + tile - (2 + cx) * STATIC]
+    return right(9 + 2 * c + plane - 2 - cx)
 
 
 def pack_second(with_static, *refs):
     if with_static:
-        vel, forcing, visc, left, right, up, down, tiles, fixed = refs
+        vel, forcing, visc, near, far, even_pair, odd_pair, tiles, fixed = refs
+    else:
+        vel, near, far, even_pair, odd_pair, tiles = refs
+        fixed = None
+    left, right = arrived(GX, near, far)
+    if with_static:
         for t in range(8 * STATIC):
             fixed[t * 8 : t * 8 + 8] = static_tile(forcing, visc, left, right, t)
-    else:
-        vel, left, right, up, down, tiles = refs
-        fixed = None
     for t in range(10 * FIELD):
         tiles[t * 8 : t * 8 + 8] = field_tile(vel, left, right, t)
+    odd, _, _ = place(GY)
     pieces, _ = edge_rows(with_static)
     for dist, first, count, row, static in pieces:
         src = fixed if static else tiles
-        up[row : row + count] = src[pl.ds(first * 8 + 8 - dist, count, stride=8), :]
-        down[row : row + count] = src[pl.ds(first * 8 + dist - 1, count, stride=8), :]
-
-
-def fill_frames(with_static, south, north, frames, fixed):
+        up = src[pl.ds(first * 8 + 8 - dist, count, stride=8), :]
+        down = src[pl.ds(first * 8 + dist - 1, count, stride=8), :]
+        even_pair[row : row + count] = jnp.where(odd, down, up)
+        odd_pair[row : row + count] = jnp.where(odd, up, down)
+
+
+def fill_frames(with_static, even_pair, odd_pair, frames, fixed):
     pieces, _ = edge_rows(with_static)
+    south, north = arrived(GY, even_pair, odd_pair)
     for dist, first, count, row, static in pieces:
         dst = fixed if static else frames
-        dst[pl.ds(first * ROWS + OWN - dist, count, stride=ROWS), :] = south[row : row + count]
-        dst[pl.ds(first * ROWS + OWN + 7 + dist, count, stride=ROWS), :] = north[row : row + count]
+        dst[pl.ds(first * ROWS + OWN - dist, count, stride=ROWS), :] = south(pl.ds(row, count))
+        dst[pl.ds(first * ROWS + OWN + 7 + dist, count, stride=ROWS), :] = north(pl.ds(row, count))
 
 
 def sweeps(frames, fixed, coef, one, two):
@@ -159,14 +190,15 @@
     out[...] = spread(jnp.zeros((1, 128), jnp.float32), parts)
 
 
-def first_map(vel, forcing, visc, left, right, south, north, hist, prev, gram, value, newest, fixed, payload, frames, coef, one, two):
+def first_map(vel, forcing, visc, near, far, even_pair, odd_pair, hist, prev, gram, value, newest, fixed, payload, frames, coef, one, two):
     frames[...] = jnp.zeros_like(frames)
     fixed[...] = jnp.zeros_like(fixed)
+    left, right = arrived(GX, near, far)
     for t in range(8 * STATIC):
         fixed[t * ROWS + OWN : t * ROWS + OWN + 8] = static_tile(forcing, visc, left, right, t)
     for t in range(10 * FIELD):
         frames[t * ROWS + OWN : t * ROWS + OWN + 8] = field_tile(vel, left, right, t)
-    fill_frames(True, south, north, frames, fixed)
+    fill_frames(True, even_pair, odd_pair, frames, fixed)
     result = sweeps(frames, fixed, coef, one, two)
     resid = {}
     fresh = {}
@@ -182,11 +214,12 @@
         payload[k] = row
 
 
-def second_map(vel, left, right, south, north, fixed, hist, newest, value, resid, payload, frames, coef, one, two):
+def second_map(vel, near, far, even_pair, odd_pair, fixed, hist, newest, value, resid, payload, frames, coef, one, two):
     frames[...] = jnp.zeros_like(frames)
+    left, right = arrived(GX, near, far)
     for t in range(10 * FIELD):
         frames[t * ROWS + OWN : t * ROWS + OWN + 8] = field_tile(vel, left, right, t)
-    fill_frames(False, south, north, frames, None)
+    fill_frames(False, even_pair, odd_pair, frames, None)
     result = sweeps(frames, fixed, coef, one, two)
     for (c, p), tile in result.items():
         value[c, p] = tile
@@ -233,22 +266,24 @@
     return total
 
 
-def mix_first(entries, rows, value, hist, field, up, down):
+def mix_first(entries, rows, value, hist, field, even_pair, odd_pair):
     row = gathered(rows)
     s = [entry(row, k) for k in range(PREV)]
     gram = {pair: s[k] for k, pair in enumerate(PAIRS)}
     gamma = [jnp.broadcast_to(g, (8, 128)) for g in solve(gram, s[RHS:PREV], entries)]
     cx = value.shape[1]
+    odd, _, _ = place(GX)
     for c in range(3):
+        mixed = []
         for p in range(cx):
             tile = value[c, p]
             for j in range(M):
                 tile = tile - gamma[j] * hist[j, c, p]
             field[c, p] = tile
-            if p >= cx - 3:
-                up[(p - cx + 3) * 3 + c] = tile
-            if p < 3:
-                down[p * 3 + c] = tile
+            mixed.append(tile)
+        for d in range(3):
+            even_pair[3 * c + d] = jnp.where(odd, mixed[d], mixed[cx - 3 + d])
+            odd_pair[3 * c + d] = jnp.where(odd, mixed[cx - 3 + d], mixed[d])
 
 
 def mix_second(entries, rows, first_rows, value, hist, first_value, prev, field):
@@ -272,12 +307,13 @@
             field[c, p] = tile - gamma[M - 1] * (first_value[c, p] - prev[c, p])
 
 
-def neighbours(axis, up, down):
-    count = lax.axis_size(axis)
-    ends = count - 1
-    before = lax.ppermute(up, axis, [(i, i + 1) for i in range(ends)])
-    after = lax.ppermute(down, axis, [(i + 1, i) for i in range(ends)])
-    return before, after
+def neighbours(axes, even_pair, odd_pair):
+    count = lax.axis_size(axes)
+    pairs = [[[i, (i + 1) % count] for i in range(start, count, 2)] for start in (0, 1)]
+    return (
+        lax.all_gather(even_pair, axes, axis_index_groups=pairs[0]),
+        lax.all_gather(odd_pair, axes, axis_index_groups=pairs[1]),
+    )
 
 
 def exchange(payload):
@@ -294,29 +330,31 @@
     frames = (10 * FIELD * ROWS, 128)
     fixed = (8 * STATIC * ROWS, 128)
 
-    up, down = call(pack_first, [(17, 8, 128)] * 2)(velocity, forcing, viscosity)
-    left, right = neighbours(GX, up, down)
+    hbm = [pl.BlockSpec(memory_space=pltpu.HBM)] * 3
+    far_away = [pltpu.with_memory_space_constraint(x, pltpu.HBM) for x in (velocity, forcing, viscosity)]
+    *packed, velocity, forcing, viscosity = call(
+        pack_first, [(17, 8, 128)] * 2 + [shape, shape, shape[1:]], [pltpu.SemaphoreType.DMA((17,))], in_specs=hbm
+    )(*far_away)
+    faces = neighbours(GX, *packed)
     (gram,) = call(gram_part, [(1, 128)], flops=4000000)(hist_res, residual_prev)
     edge = (edge_rows(True)[1], 128)
-    up, down = call(
+    packed = call(
         lambda *refs: pack_second(True, *refs), [edge, edge], [(10 * FIELD * 8, 128), (8 * STATIC * 8, 128)]
-    )(velocity, forcing, viscosity, left, right)
-    south, north = neighbours(GY, up, down)
+    )(velocity, forcing, viscosity, *faces)
+    edges = neighbours(GY, *packed)
     value, newest, static, payload = call(first_map, [shape, shape, fixed, fan], [frames, *work])(
-        velocity, forcing, viscosity, left, right, south, north, hist_res, residual_prev, gram
+        velocity, forcing, viscosity, *faces, *edges, hist_res, residual_prev, gram
     )
     sums = exchange(payload)
-    field, up, down = call(lambda *refs: mix_first(entries, *refs), [shape, (9, 8, 128), (9, 8, 128)])(
+    field, *packed = call(lambda *refs: mix_first(entries, *refs), [shape, (9, 8, 128), (9, 8, 128)])(
         sums, value, hist_val
     )
-    left, right = neighbours(GX, up, down)
+    faces = neighbours(GX, *packed)
     edge = (edge_rows(False)[1], 128)
-    up, down = call(lambda *refs: pack_second(False, *refs), [edge, edge], [(10 * FIELD * 8, 128)])(
-        field, left, right
-    )
-    south, north = neighbours(GY, up, down)
+    packed = call(lambda *refs: pack_second(False, *refs), [edge, edge], [(10 * FIELD * 8, 128)])(field, *faces)
+    edges = neighbours(GY, *packed)
     value_next, resid, payload = call(second_map, [shape, shape, fan], [frames, *work])(
-        field, left, right, south, north, static, hist_res, newest
+        field, *faces, *edges, static, hist_res, newest
     )
     (out,) = call(lambda *refs: mix_second(entries, *refs), [shape])(
         exchange(payload), sums, value_next, hist_val, value, value_prev

time: 127 us -> 123 us (0.969)
  blocking collectives: 79.8 us -> 118 us
  starting transfers between devices: 29.9 us -> 0 us
  waiting for transfers between devices: 11 us -> 0 us
  local copies, waits for them, and re-layouts: 2.39 us -> 0.04 us
    all_gather x0 -> x8, blocking collectives: none -> 46.9 us  [the longest x4 27.1 us: neighbours(): lax.all_gather(even_pair, axes, axis_index_groups=pairs[0])]
    ppermute x8 -> x0, starting transfers between devices: 29.9 us -> none  [the longest x4 16.6 us: neighbours(): after = lax.ppermute(down, axis, [(i + 1, i) for i in range(ends)])]
    ppermute x8 -> x0, waiting for transfers between devices: 11 us -> none  [the longest x4 10.9 us: neighbours(): after = lax.ppermute(down, axis, [(i + 1, i) for i in range(ends)])]
    all_to_all x2, blocking collectives: 33.7 us -> 28.6 us  [exchange(): return lax.all_to_all(rows, PLANE, 0, 0)]
    all_to_all x2, blocking collectives: 46.1 us -> 42.5 us  [exchange(): row = jnp.sum(lax.all_to_all(payload, CHAIN, 0, 0), axis=(0, 1))]
    unnamed x14 -> x8, local copies, waits for them, and re-layouts: 2.37 us -> 0.02 us
  transfers between devices with their start and end apart: 8 -> 0, of which waited for: 4 -> 0; matrix products, arithmetic and copies ran while one was open for 0% -> 0% of each run, Pallas kernels for 0% -> 0%
where the time goes in v3:
time: 123 us
  blocking collectives  118 us (96%)
  Pallas kernels  3.99 us (3%)
    all_to_all x2, blocking collectives, exchange(): row = jnp.sum(lax.all_to_all(payload, CHAIN, 0, 0), axis=(0, 1))  42.5 us
    all_to_all x2, blocking collectives, exchange(): return lax.all_to_all(rows, PLANE, 0, 0)  28.6 us
    all_gather x4, blocking collectives, neighbours(): lax.all_gather(even_pair, axes, axis_index_groups=pairs[0])  27.1 us
    all_gather x4, blocking collectives, neighbours(): lax.all_gather(odd_pair, axes, axis_index_groups=pairs[1])  19.9 us

profile of v3, /device:TPU:1, one launch (start us, length us, event | category | flops | bytes accessed | tf_op | source)
XLA Modules:
  0.0 122.9 jit_solution(156306557935337193)
XLA Ops:
  0.6 1.2 shard_map.86
  1.8 15.7 %all-gather = f32[34,8,128]{2,1,0:T(8,128)S(1)} all-gather(f32[17,8,128]{2,1,0:T(8,128)S(1)} %get-tuple-element.24), channel_id=2, replica_groups={{0,16},{32,48},{64,80},{96,112},{128,144},{160,176},{192,208},{224,240}..., dimensions={0}, use_global_device_ids=true | all-gather | bytes 208896 | tf_op jit(solution)/shard_map/all_gather | solution.py:314
  17.5 4.4 %all-gather.1 = f32[34,8,128]{2,1,0:T(8,128)S(1)} all-gather(f32[17,8,128]{2,1,0:T(8,128)S(1)} %get-tuple-element.25), channel_id=3, replica_groups={{16,32},{48,64},{80,96},{112,128},{144,160},{176,192},{208,224},{240,25..., dimensions={0}, use_global_device_ids=true | all-gather | bytes 208896 | tf_op jit(solution)/shard_map/all_gather | solution.py:315
  21.9 0.0 copy-start
  21.9 4.0 %all-gather.2 = f32[208,128]{1,0:T(8,128)S(1)} all-gather(f32[104,128]{1,0:T(8,128)S(1)} %get-tuple-element.26), channel_id=4, replica_groups={{0,1},{2,3},{4,5},{6,7},{8,9},{10,11},{12,13},{14,15},{16,17},{18,19},{..., dimensions={0}, use_global_device_ids=true | all-gather | bytes 159744 | tf_op jit(solution)/shard_map/all_gather | solution.py:314
  26.0 5.9 %all-gather.3 = f32[208,128]{1,0:T(8,128)S(1)} all-gather(f32[104,128]{1,0:T(8,128)S(1)} %get-tuple-element.27), channel_id=5, replica_groups={{1,2},{3,4},{5,6},{7,8},{9,10},{11,12},{13,14},{15,0},{17,18},{19,20},{..., dimensions={0}, use_global_device_ids=true | all-gather | bytes 159744 | tf_op jit(solution)/shard_map/all_gather | solution.py:315
  31.8 0.0 copy-done
  31.8 0.0 copy-done.2
  31.9 0.2 shard_map.88.gram
  32.0 0.5 shard_map.89
  32.6 21.7 %all_to_all.20 = f32[32,1,128]{2,1,0:T(1,128)S(1)} all-to-all(f32[32,1,128]{2,1,0:T(1,128)S(1)} %get-tuple-element.28), channel_id=1, replica_groups=mesh['gx_0'=2,'gx_1'=16,'gx_2'=2,'gy_0'=2,'gy_1'=8] {'gx_1','gx_2'}, dimensions={0} | all-to-all | bytes 32768 | tf_op jit(solution)/shard_map/all_to_all | solution.py:320
  54.3 0.1 reduce_sum.18
  54.4 17.0 %all_to_all.21.refs_0_.refs_1_ = f32[32,1,128]{2,1,0:T(1,128)S(1)} all-to-all(f32[32,1,128]{2,1,0:T(1,128)S(1)} %broadcast_in_dim.4), channel_id=1, replica_groups=mesh['gx_0'=2,'gx_1'=16,'gx_2'=2,'gy_0'=2,'gy_1'=8] {'gx_0','gy_0','gy_1'}, dimensions={0} | all-to-all | bytes 32768 | tf_op jit(solution)/shard_map/all_to_all | solution.py:322
  71.4 0.0 copy-done.1
  71.4 0.2 shard_map.90
  71.6 3.8 %all-gather.4 = f32[18,8,128]{2,1,0:T(8,128)S(1)} all-gather(f32[9,8,128]{2,1,0:T(8,128)S(1)} %get-tuple-element.31), channel_id=6, replica_groups={{0,16},{32,48},{64,80},{96,112},{128,144},{160,176},{192,208},{224,240}..., dimensions={0}, use_global_device_ids=true | all-gather | bytes 110592 | tf_op jit(solution)/shard_map/all_gather | solution.py:314
  75.4 4.1 %all-gather.5 = f32[18,8,128]{2,1,0:T(8,128)S(1)} all-gather(f32[9,8,128]{2,1,0:T(8,128)S(1)} %get-tuple-element.32), channel_id=7, replica_groups={{16,32},{48,64},{80,96},{112,128},{144,160},{176,192},{208,224},{240,25..., dimensions={0}, use_global_device_ids=true | all-gather | bytes 110592 | tf_op jit(solution)/shard_map/all_gather | solution.py:315
  79.5 3.5 %all-gather.6 = f32[128,128]{1,0:T(8,128)S(1)} all-gather(f32[64,128]{1,0:T(8,128)S(1)} %get-tuple-element.33), channel_id=8, replica_groups={{0,1},{2,3},{4,5},{6,7},{8,9},{10,11},{12,13},{14,15},{16,17},{18,19},{..., dimensions={0}, use_global_device_ids=true | all-gather | bytes 98304 | tf_op jit(solution)/shard_map/all_gather | solution.py:314
  83.0 5.5 %all-gather.7 = f32[128,128]{1,0:T(8,128)S(1)} all-gather(f32[64,128]{1,0:T(8,128)S(1)} %get-tuple-element.34), channel_id=9, replica_groups={{1,2},{3,4},{5,6},{7,8},{9,10},{11,12},{13,14},{15,0},{17,18},{19,20},{..., dimensions={0}, use_global_device_ids=true | all-gather | bytes 98304 | tf_op jit(solution)/shard_map/all_gather | solution.py:315
  88.5 1.0 shard_map.92
  89.6 20.8 %all_to_all.22 = f32[32,1,128]{2,1,0:T(1,128)S(1)} all-to-all(f32[32,1,128]{2,1,0:T(1,128)S(1)} %get-tuple-element.37), channel_id=1, replica_groups=mesh['gx_0'=2,'gx_1'=16,'gx_2'=2,'gy_0'=2,'gy_1'=8] {'gx_1','gx_2'}, dimensions={0} | all-to-all | bytes 32768 | tf_op jit(solution)/shard_map/all_to_all | solution.py:320
  110.4 0.1 reduce_sum.19
  110.5 11.6 %all_to_all.23.refs_0_ = f32[32,1,128]{2,1,0:T(1,128)S(1)} all-to-all(f32[32,1,128]{2,1,0:T(1,128)S(1)} %broadcast_in_dim.5), channel_id=1, replica_groups=mesh['gx_0'=2,'gx_1'=16,'gx_2'=2,'gy_0'=2,'gy_1'=8] {'gx_0','gy_0','gy_1'}, dimensions={0} | all-to-all | bytes 32768 | tf_op jit(solution)/shard_map/all_to_all | solution.py:322
  122.1 0.8 shard_map.93
  (8 shorter events, 0.1 us)
Async XLA Ops:
  21.9 9.9 %copy-start = (f32[5,3,4,8,128]{4,3,2,1,0:T(8,128)S(1)}, f32[5,3,4,8,128]{4,3,2,1,0:T(8,128)}, u32[]{:S(2)}) copy-start(f32[5,3,4,8,128]{4,3,2,1,0:T(8,128)} %hist.5) | copy-start | bytes 737284
  26.0 5.9 %copy-start.2 = (f32[3,4,8,128]{3,2,1,0:T(8,128)S(1)}, f32[3,4,8,128]{3,2,1,0:T(8,128)}, u32[]{:S(2)}) copy-start(f32[3,4,8,128]{3,2,1,0:T(8,128)} %prev.3) | copy-start | bytes 147460
  32.0 39.3 %copy-start.1 = (f32[5,3,4,8,128]{4,3,2,1,0:T(8,128)S(1)}, f32[5,3,4,8,128]{4,3,2,1,0:T(8,128)}, u32[]{:S(2)}) copy-start(f32[5,3,4,8,128]{4,3,2,1,0:T(8,128)} %refs_3_.1) | copy-start | bytes 737284
  89.6 32.5 %copy-start.3 = (f32[3,4,8,128]{3,2,1,0:T(8,128)S(1)}, f32[3,4,8,128]{3,2,1,0:T(8,128)}, u32[]{:S(2)}) copy-start(f32[3,4,8,128]{3,2,1,0:T(8,128)} %refs_5_.1) | copy-start | bytes 147460

commit v4 on v3

--- a/solution.py
+++ b/solution.py
@@ -44,18 +44,13 @@
     )
 
 
-def place(axes):
-    index = 0
-    count = 1
-    for axis in axes:
-        index = index * lax.axis_size(axis) + lax.axis_index(axis)
-        count = count * lax.axis_size(axis)
-    return lax.rem(index, 2) == 1, index == 0, index == count - 1
+def odd_place(axes):
+    return lax.rem(lax.axis_index(axes[-1]), 2) == 1
 
 
 def pack_first(vel, forcing, visc, even_pair, odd_pair, vel_near, forcing_near, visc_near, sem):
     cx = vel.shape[1]
-    odd, _, _ = place(GX)
+    odd = odd_place(GX)
     copies = []
     for out, low in ((even_pair, odd), (odd_pair, jnp.logical_not(odd))):
         three = pl.ds(jnp.where(low, 0, cx - 3), 3)
@@ -74,9 +69,11 @@
 
 
 def arrived(axes, even_pair, odd_pair):
-    odd, first, last = place(axes)
-    before = lambda i: jnp.where(odd, even_pair[0, i], jnp.where(first, 0.0, odd_pair[0, i]))
-    after = lambda i: jnp.where(odd, jnp.where(last, 0.0, odd_pair[1, i]), even_pair[1, i])
+    odd = odd_place(axes)
+    if even_pair.shape != odd_pair.shape:
+        even_pair = even_pair.at[jnp.where(odd, 0, 1)]
+    before = lambda i: jnp.where(odd, even_pair[i], odd_pair[i])
+    after = lambda i: jnp.where(odd, odd_pair[i], even_pair[i])
     return before, after
 
 
@@ -112,7 +109,7 @@
             fixed[t * 8 : t * 8 + 8] = static_tile(forcing, visc, left, right, t)
     for t in range(10 * FIELD):
         tiles[t * 8 : t * 8 + 8] = field_tile(vel, left, right, t)
-    odd, _, _ = place(GY)
+    odd = odd_place(GY)
     pieces, _ = edge_rows(with_static)
     for dist, first, count, row, static in pieces:
         src = fixed if static else tiles
@@ -272,7 +269,7 @@
     gram = {pair: s[k] for k, pair in enumerate(PAIRS)}
     gamma = [jnp.broadcast_to(g, (8, 128)) for g in solve(gram, s[RHS:PREV], entries)]
     cx = value.shape[1]
-    odd, _, _ = place(GX)
+    odd = odd_place(GX)
     for c in range(3):
         mixed = []
         for p in range(cx):
@@ -307,13 +304,18 @@
             field[c, p] = tile - gamma[M - 1] * (first_value[c, p] - prev[c, p])
 
 
-def neighbours(axes, even_pair, odd_pair):
-    count = lax.axis_size(axes)
-    pairs = [[[i, (i + 1) % count] for i in range(start, count, 2)] for start in (0, 1)]
-    return (
-        lax.all_gather(even_pair, axes, axis_index_groups=pairs[0]),
-        lax.all_gather(odd_pair, axes, axis_index_groups=pairs[1]),
-    )
+def swap(cells, axes, start):
+    pairs = [(i, i + 1) for i in range(start, lax.axis_size(axes) - 1, 2)]
+    return lax.ppermute(cells, axes, pairs + [(j, i) for i, j in pairs])
+
+
+def faces_of(even_pair, odd_pair):
+    odd_pair = swap(odd_pair, GX, 1)
+    return lax.all_gather(even_pair, GX[2]), odd_pair
+
+
+def edges_of(even_pair, odd_pair):
+    return swap(even_pair, GY, 0), swap(odd_pair, GY, 1)
 
 
 def exchange(payload):
@@ -335,13 +337,13 @@
     *packed, velocity, forcing, viscosity = call(
         pack_first, [(17, 8, 128)] * 2 + [shape, shape, shape[1:]], [pltpu.SemaphoreType.DMA((17,))], in_specs=hbm
     )(*far_away)
-    faces = neighbours(GX, *packed)
+    faces = faces_of(*packed)
     (gram,) = call(gram_part, [(1, 128)], flops=4000000)(hist_res, residual_prev)
     edge = (edge_rows(True)[1], 128)
     packed = call(
         lambda *refs: pack_second(True, *refs), [edge, edge], [(10 * FIELD * 8, 128), (8 * STATIC * 8, 128)]
     )(velocity, forcing, viscosity, *faces)
-    edges = neighbours(GY, *packed)
+    edges = edges_of(*packed)
     value, newest, static, payload = call(first_map, [shape, shape, fixed, fan], [frames, *work])(
         velocity, forcing, viscosity, *faces, *edges, hist_res, residual_prev, gram
     )
@@ -349,10 +351,10 @@
     field, *packed = call(lambda *refs: mix_first(entries, *refs), [shape, (9, 8, 128), (9, 8, 128)])(
         sums, value, hist_val
     )
-    faces = neighbours(GX, *packed)
+    faces = faces_of(*packed)
     edge = (edge_rows(False)[1], 128)
     packed = call(lambda *refs: pack_second(False, *refs), [edge, edge], [(10 * FIELD * 8, 128)])(field, *faces)
-    edges = neighbours(GY, *packed)
+    edges = edges_of(*packed)
     value_next, resid, payload = call(second_map, [shape, shape, fan], [frames, *work])(
         field, *faces, *edges, static, hist_res, newest
     )

time: 123 us -> 119 us (0.967)
  blocking collectives: 118 us -> 94.9 us
  starting transfers between devices: 0 us -> 15.3 us
  waiting for transfers between devices: 0 us -> 3.83 us
    all_gather x8 -> x2, blocking collectives: 46.9 us -> 12.9 us  [faces_of(): return (lax.all_gather(even_pair, GX[2]), odd_pair)]
    ppermute x0 -> x6, starting transfers between devices: none -> 15.3 us  [swap(): return lax.ppermute(cells, axes, pairs + [(j, i) for i, j in pairs])]
    all_to_all x2, blocking collectives: 28.6 us -> 40.6 us  [exchange(): return lax.all_to_all(rows, PLANE, 0, 0)]
    ppermute x0 -> x6, waiting for transfers between devices: none -> 3.83 us  [swap(): return lax.ppermute(cells, axes, pairs + [(j, i) for i, j in pairs])]
  transfers between devices with their start and end apart: 0 -> 6, of which waited for: 0 -> 2; matrix products, arithmetic and copies ran while one was open for 0% -> 0% of each run, Pallas kernels for 0% -> 0%
where the time goes in v4:
time: 119 us
  blocking collectives  94.9 us (80%)
  starting transfers between devices  15.3 us (13%)
  Pallas kernels  3.96 us (3%)
  waiting for transfers between devices  3.83 us (3%)
    all_to_all x2, blocking collectives, exchange(): row = jnp.sum(lax.all_to_all(payload, CHAIN, 0, 0), axis=(0, 1))  41.3 us
    all_to_all x2, blocking collectives, exchange(): return lax.all_to_all(rows, PLANE, 0, 0)  40.6 us
    ppermute x6, starting transfers between devices, swap(): return lax.ppermute(cells, axes, pairs + [(j, i) for i, j in pairs])  15.3 us
    all_gather x2, blocking collectives, faces_of(): return (lax.all_gather(even_pair, GX[2]), odd_pair)  12.9 us
    ppermute x6, waiting for transfers between devices, swap(): return lax.ppermute(cells, axes, pairs + [(j, i) for i, j in pairs])  3.83 us
  transfers between devices with their start and end apart: 6, of which 2 were waited for; matrix products, arithmetic and copies ran while one was open for 0% of the time, Pallas kernels for 0%

profile of v4, /device:TPU:1, one launch (start us, length us, event | category | flops | bytes accessed | tf_op | source)
XLA Modules:
  0.0 118.8 jit_solution(10215164102899038651)
XLA Ops:
  0.6 1.1 shard_map.86
  1.8 5.4 %collective-permute-start = (f32[17,8,128]{2,1,0:T(8,128)S(1)}, f32[17,8,128]{2,1,0:T(8,128)S(1)}, u32[]{:S(2)}, u32[]{:S(2)}) collective-permute-start(f32[17,8,128]{2,1,0:T(8,128)S(1)} %get-tuple-element.25), channel_id=1, source_target_pairs={{16,32},{48,64},{80,96},{112,128},{144,160},{176,192},{208,224},{2... | collective-permute-start | bytes 208904 | tf_op jit(solution)/shard_map/ppermute | solution.py:309
  7.2 0.0 copy-start
  7.2 11.1 %all-gather = f32[34,8,128]{2,1,0:T(8,128)S(1)} all-gather(f32[17,8,128]{2,1,0:T(8,128)S(1)} %get-tuple-element.24), channel_id=2, replica_groups=mesh['gx_0'=2,'gx_1'=16,'gx_2'=2,'gy_0'=2,'gy_1'=8] {'gx_2'}, dimensions={0}, use_global_device_ids=true | all-gather | bytes 208896 | tf_op jit(solution)/shard_map/all_gather | solution.py:314
  18.3 0.0 collective-permute-done.refs_4_.far
  18.3 1.9 %collective-permute-start.1 = (f32[104,128]{1,0:T(8,128)S(1)}, f32[104,128]{1,0:T(8,128)S(1)}, u32[]{:S(2)}, u32[]{:S(2)}) collective-permute-start(f32[104,128]{1,0:T(8,128)S(1)} %get-tuple-element.26), channel_id=1, source_target_pairs={{0,1},{2,3},{4,5},{6,7},{8,9},{10,11},{12,13},{14,15},{1,0},{3,2},... | collective-permute-start | bytes 159752 | tf_op jit(solution)/shard_map/ppermute | solution.py:309
  20.2 0.7 collective-permute-start.2
  20.9 0.2 shard_map.88.gram
  21.1 2.1 %collective-permute-done.1.even_pair = f32[104,128]{1,0:T(8,128)S(1)} collective-permute-done((f32[104,128]{1,0:T(8,128)S(1)}, f32[104,128]{1,0:T(8,128)S(1)}, u32[]{:S(2)}, u32[]{:S(2)}) %collective-permute-start.1) | collective-permute-done | bytes 53280 | tf_op jit(solution)/shard_map/ppermute | solution.py:309
  23.2 0.5 shard_map.89
  23.7 23.5 %all_to_all.20 = f32[32,1,128]{2,1,0:T(1,128)S(1)} all-to-all(f32[32,1,128]{2,1,0:T(1,128)S(1)} %get-tuple-element.28), channel_id=1, replica_groups=mesh['gx_0'=2,'gx_1'=16,'gx_2'=2,'gy_0'=2,'gy_1'=8] {'gx_1','gx_2'}, dimensions={0} | all-to-all | bytes 32768 | tf_op jit(solution)/shard_map/all_to_all | solution.py:322
  47.2 0.1 reduce_sum.18
  47.3 21.9 %all_to_all.21.refs_0_.refs_1_ = f32[32,1,128]{2,1,0:T(1,128)S(1)} all-to-all(f32[32,1,128]{2,1,0:T(1,128)S(1)} %broadcast_in_dim.4), channel_id=1, replica_groups=mesh['gx_0'=2,'gx_1'=16,'gx_2'=2,'gy_0'=2,'gy_1'=8] {'gx_0','gy_0','gy_1'}, dimensions={0} | all-to-all | bytes 32768 | tf_op jit(solution)/shard_map/all_to_all | solution.py:324
  69.3 0.2 shard_map.90
  69.5 4.4 %collective-permute-start.3 = (f32[9,8,128]{2,1,0:T(8,128)S(1)}, f32[9,8,128]{2,1,0:T(8,128)S(1)}, u32[]{:S(2)}, u32[]{:S(2)}) collective-permute-start(f32[9,8,128]{2,1,0:T(8,128)S(1)} %get-tuple-element.32), channel_id=1, source_target_pairs={{16,32},{48,64},{80,96},{112,128},{144,160},{176,192},{208,224},{2... | collective-permute-start | bytes 110600 | tf_op jit(solution)/shard_map/ppermute | solution.py:309
  73.9 1.9 %all-gather.1 = f32[18,8,128]{2,1,0:T(8,128)S(1)} all-gather(f32[9,8,128]{2,1,0:T(8,128)S(1)} %get-tuple-element.31), channel_id=3, replica_groups=mesh['gx_0'=2,'gx_1'=16,'gx_2'=2,'gy_0'=2,'gy_1'=8] {'gx_2'}, dimensions={0}, use_global_device_ids=true | all-gather | bytes 110592 | tf_op jit(solution)/shard_map/all_gather | solution.py:314
  75.8 2.2 %collective-permute-start.4 = (f32[64,128]{1,0:T(8,128)S(1)}, f32[64,128]{1,0:T(8,128)S(1)}, u32[]{:S(2)}, u32[]{:S(2)}) collective-permute-start(f32[64,128]{1,0:T(8,128)S(1)} %get-tuple-element.33), channel_id=1, source_target_pairs={{0,1},{2,3},{4,5},{6,7},{8,9},{10,11},{12,13},{14,15},{1,0},{3,2},... | collective-permute-start | bytes 98312 | tf_op jit(solution)/shard_map/ppermute | solution.py:309
  78.0 0.7 collective-permute-start.5
  78.7 1.7 %collective-permute-done.4.even_pair = f32[64,128]{1,0:T(8,128)S(1)} collective-permute-done((f32[64,128]{1,0:T(8,128)S(1)}, f32[64,128]{1,0:T(8,128)S(1)}, u32[]{:S(2)}, u32[]{:S(2)}) %collective-permute-start.4) | collective-permute-done | bytes 32800 | tf_op jit(solution)/shard_map/ppermute | solution.py:309
  80.4 1.0 shard_map.92
  81.5 17.8 %all_to_all.22 = f32[32,1,128]{2,1,0:T(1,128)S(1)} all-to-all(f32[32,1,128]{2,1,0:T(1,128)S(1)} %get-tuple-element.37), channel_id=1, replica_groups=mesh['gx_0'=2,'gx_1'=16,'gx_2'=2,'gy_0'=2,'gy_1'=8] {'gx_1','gx_2'}, dimensions={0} | all-to-all | bytes 32768 | tf_op jit(solution)/shard_map/all_to_all | solution.py:322
  99.3 0.1 reduce_sum.19
  99.4 18.7 %all_to_all.23.refs_0_ = f32[32,1,128]{2,1,0:T(1,128)S(1)} all-to-all(f32[32,1,128]{2,1,0:T(1,128)S(1)} %broadcast_in_dim.5), channel_id=1, replica_groups=mesh['gx_0'=2,'gx_1'=16,'gx_2'=2,'gy_0'=2,'gy_1'=8] {'gx_0','gy_0','gy_1'}, dimensions={0} | all-to-all | bytes 32768 | tf_op jit(solution)/shard_map/all_to_all | solution.py:324
  118.0 0.8 shard_map.93
  (14 shorter events, 0.1 us)
Async XLA Ops:
  1.8 16.5 %collective-permute-start = (f32[17,8,128]{2,1,0:T(8,128)S(1)}, f32[17,8,128]{2,1,0:T(8,128)S(1)}, u32[]{:S(2)}, u32[]{:S(2)}) collective-permute-start(f32[17,8,128]{2,1,0:T(8,128)S(1)} %get-tuple-element.25), channel_id=1, source_target_pairs={{16,32},{48,64},{80,96},{112,128},{144,160},{176,192},{208,224},{2... | collective-permute-start | bytes 208904 | tf_op jit(solution)/shard_map/ppermute | solution.py:309
  7.2 13.8 %copy-start = (f32[5,3,4,8,128]{4,3,2,1,0:T(8,128)S(1)}, f32[5,3,4,8,128]{4,3,2,1,0:T(8,128)}, u32[]{:S(2)}) copy-start(f32[5,3,4,8,128]{4,3,2,1,0:T(8,128)} %hist.5) | copy-start | bytes 737284
  18.3 2.7 %copy-start.2 = (f32[3,4,8,128]{3,2,1,0:T(8,128)S(1)}, f32[3,4,8,128]{3,2,1,0:T(8,128)}, u32[]{:S(2)}) copy-start(f32[3,4,8,128]{3,2,1,0:T(8,128)} %prev.3) | copy-start | bytes 147460
  18.3 4.9 %collective-permute-start.1 = (f32[104,128]{1,0:T(8,128)S(1)}, f32[104,128]{1,0:T(8,128)S(1)}, u32[]{:S(2)}, u32[]{:S(2)}) collective-permute-start(f32[104,128]{1,0:T(8,128)S(1)} %get-tuple-element.26), channel_id=1, source_target_pairs={{0,1},{2,3},{4,5},{6,7},{8,9},{10,11},{12,13},{14,15},{1,0},{3,2},... | collective-permute-start | bytes 159752 | tf_op jit(solution)/shard_map/ppermute | solution.py:309
  20.2 3.0 %collective-permute-start.2 = (f32[104,128]{1,0:T(8,128)S(1)}, f32[104,128]{1,0:T(8,128)S(1)}, u32[]{:S(2)}, u32[]{:S(2)}) collective-permute-start(f32[104,128]{1,0:T(8,128)S(1)} %get-tuple-element.27), channel_id=1, source_target_pairs={{1,2},{3,4},{5,6},{7,8},{9,10},{11,12},{13,14},{2,1},{4,3},{6,5},{... | collective-permute-start | bytes 159752 | tf_op jit(solution)/shard_map/ppermute | solution.py:309
  21.1 48.1 %copy-start.1 = (f32[5,3,4,8,128]{4,3,2,1,0:T(8,128)S(1)}, f32[5,3,4,8,128]{4,3,2,1,0:T(8,128)}, u32[]{:S(2)}) copy-start(f32[5,3,4,8,128]{4,3,2,1,0:T(8,128)} %refs_3_.1) | copy-start | bytes 737284
  69.5 6.3 %collective-permute-start.3 = (f32[9,8,128]{2,1,0:T(8,128)S(1)}, f32[9,8,128]{2,1,0:T(8,128)S(1)}, u32[]{:S(2)}, u32[]{:S(2)}) collective-permute-start(f32[9,8,128]{2,1,0:T(8,128)S(1)} %get-tuple-element.32), channel_id=1, source_target_pairs={{16,32},{48,64},{80,96},{112,128},{144,160},{176,192},{208,224},{2... | collective-permute-start | bytes 110600 | tf_op jit(solution)/shard_map/ppermute | solution.py:309
  75.8 4.7 %collective-permute-start.4 = (f32[64,128]{1,0:T(8,128)S(1)}, f32[64,128]{1,0:T(8,128)S(1)}, u32[]{:S(2)}, u32[]{:S(2)}) collective-permute-start(f32[64,128]{1,0:T(8,128)S(1)} %get-tuple-element.33), channel_id=1, source_target_pairs={{0,1},{2,3},{4,5},{6,7},{8,9},{10,11},{12,13},{14,15},{1,0},{3,2},... | collective-permute-start | bytes 98312 | tf_op jit(solution)/shard_map/ppermute | solution.py:309
  78.0 2.4 %collective-permute-start.5 = (f32[64,128]{1,0:T(8,128)S(1)}, f32[64,128]{1,0:T(8,128)S(1)}, u32[]{:S(2)}, u32[]{:S(2)}) collective-permute-start(f32[64,128]{1,0:T(8,128)S(1)} %get-tuple-element.34), channel_id=1, source_target_pairs={{1,2},{3,4},{5,6},{7,8},{9,10},{11,12},{13,14},{2,1},{4,3},{6,5},{... | collective-permute-start | bytes 98312 | tf_op jit(solution)/shard_map/ppermute | solution.py:309
  81.5 36.6 %copy-start.3 = (f32[3,4,8,128]{3,2,1,0:T(8,128)S(1)}, f32[3,4,8,128]{3,2,1,0:T(8,128)}, u32[]{:S(2)}) copy-start(f32[3,4,8,128]{3,2,1,0:T(8,128)} %refs_5_.1) | copy-start | bytes 147460

commit v5 on v4

--- a/solution.py
+++ b/solution.py
@@ -7,7 +7,6 @@
 from jax.sharding import PartitionSpec as P
 
 M = 5
-SWEEPS = 3
 AXES = ("gx_0", "gx_1", "gx_2", "gy_0", "gy_1")
 GX = ("gx_0", "gx_1", "gx_2")
 GY = ("gy_0", "gy_1")
@@ -27,10 +26,14 @@
 STATIC = 4
 
 
+GROUPS = 1 + M
+GROUP_ROWS = 56
+
+
 def edge_rows(with_static):
     if with_static:
         return [(1, 3, 24, 0, False), (1, 4, 24, 24, True), (2, 8, 16, 48, True), (2, 6, 18, 64, False), (3, 9, 12, 88, False)], 104
-    return [(1, 3, 24, 0, False), (2, 6, 18, 24, False), (3, 9, 12, 48, False)], 64
+    return [(1, 3, 24, 0, False), (2, 6, 18, 24, False), (3, 9, 12, 42, False)], GROUP_ROWS
 
 
 def call(kernel, outs, scratch=(), flops=20000, **more):
@@ -97,35 +100,54 @@
     return right(9 + 2 * c + plane - 2 - cx)
 
 
-def pack_second(with_static, *refs):
-    if with_static:
-        vel, forcing, visc, near, far, even_pair, odd_pair, tiles, fixed = refs
-    else:
-        vel, near, far, even_pair, odd_pair, tiles = refs
-        fixed = None
-    left, right = arrived(GX, near, far)
-    if with_static:
-        for t in range(8 * STATIC):
-            fixed[t * 8 : t * 8 + 8] = static_tile(forcing, visc, left, right, t)
-    for t in range(10 * FIELD):
-        tiles[t * 8 : t * 8 + 8] = field_tile(vel, left, right, t)
+def pack_edges(tiles, fixed, even_pair, odd_pair, base, with_static):
     odd = odd_place(GY)
     pieces, _ = edge_rows(with_static)
     for dist, first, count, row, static in pieces:
         src = fixed if static else tiles
         up = src[pl.ds(first * 8 + 8 - dist, count, stride=8), :]
         down = src[pl.ds(first * 8 + dist - 1, count, stride=8), :]
-        even_pair[row : row + count] = jnp.where(odd, down, up)
-        odd_pair[row : row + count] = jnp.where(odd, up, down)
-
-
-def fill_frames(with_static, even_pair, odd_pair, frames, fixed):
+        even_pair[base + row : base + row + count] = jnp.where(odd, down, up)
+        odd_pair[base + row : base + row + count] = jnp.where(odd, up, down)
+
+
+def pack_second(vel, forcing, visc, near, far, even_pair, odd_pair, tiles, fixed):
+    left, right = arrived(GX, near, far)
+    for t in range(8 * STATIC):
+        fixed[t * 8 : t * 8 + 8] = static_tile(forcing, visc, left, right, t)
+    for t in range(10 * FIELD):
+        tiles[t * 8 : t * 8 + 8] = field_tile(vel, left, right, t)
+    pack_edges(tiles, fixed, even_pair, odd_pair, 0, True)
+
+
+def pack_mixed_first(value, hist, even_pair, odd_pair):
+    cx = value.shape[1]
+    odd = odd_place(GX)
+    for out, low in ((even_pair, odd), (odd_pair, jnp.logical_not(odd))):
+        first = jnp.where(low, 0, cx - 3)
+        for g in range(GROUPS):
+            src = value if g == 0 else hist.at[g - 1]
+            for c in range(3):
+                for d in range(3):
+                    out[9 * g + 3 * c + d] = src[c, first + d]
+
+
+def pack_mixed_second(value, hist, near, far, even_pair, odd_pair, tiles):
+    left, right = arrived(GX, near, far)
+    for g in range(GROUPS):
+        src = value if g == 0 else hist.at[g - 1]
+        block = tiles.at[g]
+        for t in range(10 * FIELD):
+            block[t * 8 : t * 8 + 8] = field_tile(src, lambda i: left(9 * g + i), lambda i: right(9 * g + i), t)
+        pack_edges(block, None, even_pair, odd_pair, g * GROUP_ROWS, False)
+
+
+def fill_frames(with_static, south, north, frames, fixed):
     pieces, _ = edge_rows(with_static)
-    south, north = arrived(GY, even_pair, odd_pair)
     for dist, first, count, row, static in pieces:
         dst = fixed if static else frames
-        dst[pl.ds(first * ROWS + OWN - dist, count, stride=ROWS), :] = south(pl.ds(row, count))
-        dst[pl.ds(first * ROWS + OWN + 7 + dist, count, stride=ROWS), :] = north(pl.ds(row, count))
+        dst[pl.ds(first * ROWS + OWN - dist, count, stride=ROWS), :] = south(row, count)
+        dst[pl.ds(first * ROWS + OWN + 7 + dist, count, stride=ROWS), :] = north(row, count)
 
 
 def sweeps(frames, fixed, coef, one, two):
@@ -165,12 +187,12 @@
     return out
 
 
-def lanes(row, shape=(1, 128)):
+def lanes(shape=(1, 128)):
     return lax.broadcasted_iota(jnp.int32, shape, 1)
 
 
 def spread(row, parts):
-    lane = lanes(row)
+    lane = lanes()
     for k, part in parts.items():
         whole = jnp.sum(jnp.sum(part, axis=0, keepdims=True), axis=1, keepdims=True)
         row = jnp.where(lane == k, whole, row)
@@ -195,7 +217,8 @@
         fixed[t * ROWS + OWN : t * ROWS + OWN + 8] = static_tile(forcing, visc, left, right, t)
     for t in range(10 * FIELD):
         frames[t * ROWS + OWN : t * ROWS + OWN + 8] = field_tile(vel, left, right, t)
-    fill_frames(True, even_pair, odd_pair, frames, fixed)
+    south, north = arrived(GY, even_pair, odd_pair)
+    fill_frames(True, lambda r, n: south(pl.ds(r, n)), lambda r, n: north(pl.ds(r, n)), frames, fixed)
     result = sweeps(frames, fixed, coef, one, two)
     resid = {}
     fresh = {}
@@ -211,26 +234,8 @@
         payload[k] = row
 
 
-def second_map(vel, near, far, even_pair, odd_pair, fixed, hist, newest, value, resid, payload, frames, coef, one, two):
-    frames[...] = jnp.zeros_like(frames)
-    left, right = arrived(GX, near, far)
-    for t in range(10 * FIELD):
-        frames[t * ROWS + OWN : t * ROWS + OWN + 8] = field_tile(vel, left, right, t)
-    fill_frames(False, even_pair, odd_pair, frames, None)
-    result = sweeps(frames, fixed, coef, one, two)
-    for (c, p), tile in result.items():
-        value[c, p] = tile
-        result[c, p] = tile - vel[c, p]
-        resid[c, p] = result[c, p]
-    parts = {i: sum(hist[i + 1, c, p] * r for (c, p), r in result.items()) for i in range(M - 1)}
-    parts[M - 1] = sum(newest[c, p] * r for (c, p), r in result.items())
-    row = spread(jnp.zeros((1, 128), jnp.float32), parts)
-    for k in range(payload.shape[0]):
-        payload[k] = row
-
-
 def entry(row, k):
-    return jnp.sum(jnp.where(lanes(row) == k, row, 0.0), axis=1, keepdims=True)
+    return jnp.sum(jnp.where(lanes() == k, row, 0.0), axis=1, keepdims=True)
 
 
 def solve(gram, rhs, entries):
@@ -263,24 +268,44 @@
     return total
 
 
-def mix_first(entries, rows, value, hist, field, even_pair, odd_pair):
+def second_map(entries, rows, value, hist_val, near, far, even_pair, odd_pair, fixed, hist, newest, value_next, resid, payload, frames, edges, coef, one, two):
     row = gathered(rows)
     s = [entry(row, k) for k in range(PREV)]
     gram = {pair: s[k] for k, pair in enumerate(PAIRS)}
     gamma = [jnp.broadcast_to(g, (8, 128)) for g in solve(gram, s[RHS:PREV], entries)]
-    cx = value.shape[1]
-    odd = odd_place(GX)
-    for c in range(3):
-        mixed = []
-        for p in range(cx):
-            tile = value[c, p]
-            for j in range(M):
-                tile = tile - gamma[j] * hist[j, c, p]
-            field[c, p] = tile
-            mixed.append(tile)
-        for d in range(3):
-            even_pair[3 * c + d] = jnp.where(odd, mixed[d], mixed[cx - 3 + d])
-            odd_pair[3 * c + d] = jnp.where(odd, mixed[cx - 3 + d], mixed[d])
+
+    def mixed(part):
+        total = part(0)
+        for j in range(M):
+            total = total - gamma[j] * part(j + 1)
+        return total
+
+    frames[...] = jnp.zeros_like(frames)
+    left, right = arrived(GX, near, far)
+    field = {}
+    for t in range(10 * FIELD):
+        plane, c = divmod(t, FIELD)
+        tile = mixed(
+            lambda g: field_tile(value if g == 0 else hist_val.at[g - 1], lambda i: left(9 * g + i), lambda i: right(9 * g + i), t)
+        )
+        frames[t * ROWS + OWN : t * ROWS + OWN + 8] = tile
+        if 3 <= plane < 7:
+            field[c, plane - 3] = tile
+    south, north = arrived(GY, even_pair, odd_pair)
+    for side, reader in enumerate((south, north)):
+        for r in range(0, GROUP_ROWS, 8):
+            edges[side, r : r + 8] = mixed(lambda g: reader(pl.ds(g * GROUP_ROWS + r, 8)))
+    fill_frames(False, lambda r, n: edges[0, r : r + n], lambda r, n: edges[1, r : r + n], frames, None)
+    result = sweeps(frames, fixed, coef, one, two)
+    for (c, p), tile in result.items():
+        value_next[c, p] = tile
+        result[c, p] = tile - field[c, p]
+        resid[c, p] = result[c, p]
+    parts = {i: sum(hist[i + 1, c, p] * r for (c, p), r in result.items()) for i in range(M - 1)}
+    parts[M - 1] = sum(newest[c, p] * r for (c, p), r in result.items())
+    row = spread(jnp.zeros((1, 128), jnp.float32), parts)
+    for k in range(payload.shape[0]):
+        payload[k] = row
 
 
 def mix_second(entries, rows, first_rows, value, hist, first_value, prev, field):
@@ -319,7 +344,8 @@
 
 
 def exchange(payload):
-    row = jnp.sum(lax.all_to_all(payload, CHAIN, 0, 0), axis=(0, 1))
+    rows = lax.all_to_all(payload, CHAIN, 0, 0)
+    row = jnp.sum(rows, axis=(0, 1))
     rows = jnp.broadcast_to(row[None, None, :], (lax.axis_size(PLANE), 1, 128))
     return lax.all_to_all(rows, PLANE, 0, 0)
 
@@ -340,26 +366,25 @@
     faces = faces_of(*packed)
     (gram,) = call(gram_part, [(1, 128)], flops=4000000)(hist_res, residual_prev)
     edge = (edge_rows(True)[1], 128)
-    packed = call(
-        lambda *refs: pack_second(True, *refs), [edge, edge], [(10 * FIELD * 8, 128), (8 * STATIC * 8, 128)]
-    )(velocity, forcing, viscosity, *faces)
+    packed = call(pack_second, [edge, edge], [(10 * FIELD * 8, 128), (8 * STATIC * 8, 128)])(
+        velocity, forcing, viscosity, *faces
+    )
     edges = edges_of(*packed)
     value, newest, static, payload = call(first_map, [shape, shape, fixed, fan], [frames, *work])(
         velocity, forcing, viscosity, *faces, *edges, hist_res, residual_prev, gram
     )
     sums = exchange(payload)
-    field, *packed = call(lambda *refs: mix_first(entries, *refs), [shape, (9, 8, 128), (9, 8, 128)])(
-        sums, value, hist_val
-    )
+    packed = call(pack_mixed_first, [(9 * GROUPS, 8, 128)] * 2)(value, hist_val)
     faces = faces_of(*packed)
-    edge = (edge_rows(False)[1], 128)
-    packed = call(lambda *refs: pack_second(False, *refs), [edge, edge], [(10 * FIELD * 8, 128)])(field, *faces)
+    edge = (GROUPS * GROUP_ROWS, 128)
+    packed = call(pack_mixed_second, [edge, edge], [(GROUPS, 10 * FIELD * 8, 128)])(value, hist_val, *faces)
     edges = edges_of(*packed)
-    value_next, resid, payload = call(second_map, [shape, shape, fan], [frames, *work])(
-        field, *faces, *edges, static, hist_res, newest
-    )
+    value_next, resid, payload = call(
+        lambda *refs: second_map(entries, *refs), [shape, shape, fan], [frames, (2, GROUP_ROWS, 128), *work]
+    )(sums, value, hist_val, *faces, *edges, static, hist_res, newest)
+    next_sums = exchange(payload)
     (out,) = call(lambda *refs: mix_second(entries, *refs), [shape])(
-        exchange(payload), sums, value_next, hist_val, value, value_prev
+        next_sums, sums, value_next, hist_val, value, value_prev
     )
     return (out, resid)
 
@@ -379,4 +404,5 @@
 
 
 def solution(mesh):
-    return build(Mesh(mesh.devices.reshape(2, 16, 2, 2, 8), AXES))
+    torus = Mesh(mesh.devices.reshape(2, 16, 2, 2, 8), AXES)
+    return build(torus)

time: 119 us -> 115 us (0.966)
  blocking collectives: 94.9 us -> 88.5 us
  waiting for transfers between devices: 3.83 us -> 5.3 us
    all_to_all x2, blocking collectives: 40.6 us -> 30.6 us  [exchange(): return lax.all_to_all(rows, PLANE, 0, 0)]
    all_to_all x2, blocking collectives: 41.3 us -> 44.6 us  [exchange(): rows = lax.all_to_all(payload, CHAIN, 0, 0)]
    ppermute x6, waiting for transfers between devices: 3.83 us -> 5.3 us  [swap(): return lax.ppermute(cells, axes, pairs + [(j, i) for i, j in pairs])]
where the time goes in v5:
time: 115 us
  blocking collectives  88.5 us (77%)
  starting transfers between devices  15.8 us (14%)
  waiting for transfers between devices  5.3 us (5%)
  Pallas kernels  4.15 us (4%)
    all_to_all x2, blocking collectives, exchange(): rows = lax.all_to_all(payload, CHAIN, 0, 0)  44.6 us
    all_to_all x2, blocking collectives, exchange(): return lax.all_to_all(rows, PLANE, 0, 0)  30.6 us
    ppermute x6, starting transfers between devices, swap(): return lax.ppermute(cells, axes, pairs + [(j, i) for i, j in pairs])  15.8 us
    all_gather x2, blocking collectives, faces_of(): return (lax.all_gather(even_pair, GX[2]), odd_pair)  13.2 us
    ppermute x6, waiting for transfers between devices, swap(): return lax.ppermute(cells, axes, pairs + [(j, i) for i, j in pairs])  5.3 us
  transfers between devices with their start and end apart: 6, of which 2 were waited for; matrix products, arithmetic and copies ran while one was open for 0% of the time, Pallas kernels for 0%

profile of v5, /device:TPU:1, one launch (start us, length us, event | category | flops | bytes accessed | tf_op | source)
XLA Modules:
  0.0 114.7 jit_solution(6101463967322789106)
XLA Ops:
  0.6 1.1 shard_map.86
  1.8 5.4 %collective-permute-start = (f32[17,8,128]{2,1,0:T(8,128)S(1)}, f32[17,8,128]{2,1,0:T(8,128)S(1)}, u32[]{:S(2)}, u32[]{:S(2)}) collective-permute-start(f32[17,8,128]{2,1,0:T(8,128)S(1)} %get-tuple-element.24), channel_id=1, source_target_pairs={{16,32},{48,64},{80,96},{112,128},{144,160},{176,192},{208,224},{2... | collective-permute-start | bytes 208904 | tf_op jit(solution)/shard_map/ppermute | solution.py:334
  7.2 0.0 copy-start.1
  7.2 11.1 %all-gather = f32[34,8,128]{2,1,0:T(8,128)S(1)} all-gather(f32[17,8,128]{2,1,0:T(8,128)S(1)} %get-tuple-element.23), channel_id=2, replica_groups=mesh['gx_0'=2,'gx_1'=16,'gx_2'=2,'gy_0'=2,'gy_1'=8] {'gx_2'}, dimensions={0}, use_global_device_ids=true | all-gather | bytes 208896 | tf_op jit(solution)/shard_map/all_gather | solution.py:339
  18.3 0.0 collective-permute-done.far
  18.3 1.9 %collective-permute-start.1 = (f32[104,128]{1,0:T(8,128)S(1)}, f32[104,128]{1,0:T(8,128)S(1)}, u32[]{:S(2)}, u32[]{:S(2)}) collective-permute-start(f32[104,128]{1,0:T(8,128)S(1)} %get-tuple-element.25), channel_id=1, source_target_pairs={{0,1},{2,3},{4,5},{6,7},{8,9},{10,11},{12,13},{14,15},{1,0},{3,2},... | collective-permute-start | bytes 159752 | tf_op jit(solution)/shard_map/ppermute | solution.py:334
  20.2 0.7 collective-permute-start.2
  20.9 0.2 shard_map.88.gram
  21.1 2.1 %collective-permute-done.1.even_pair = f32[104,128]{1,0:T(8,128)S(1)} collective-permute-done((f32[104,128]{1,0:T(8,128)S(1)}, f32[104,128]{1,0:T(8,128)S(1)}, u32[]{:S(2)}, u32[]{:S(2)}) %collective-permute-start.1) | collective-permute-done | bytes 53280 | tf_op jit(solution)/shard_map/ppermute | solution.py:334
  23.2 0.5 shard_map.89
  23.8 1.9 %collective-permute-start.3 = (f32[54,8,128]{2,1,0:T(8,128)S(1)}, f32[54,8,128]{2,1,0:T(8,128)S(1)}, u32[]{:S(2)}, u32[]{:S(2)}) collective-permute-start(f32[54,8,128]{2,1,0:T(8,128)S(1)} %get-tuple-element.30), channel_id=1, source_target_pairs={{16,32},{48,64},{80,96},{112,128},{144,160},{176,192},{208,224},{2... | collective-permute-start | bytes 663560 | tf_op jit(solution)/shard_map/ppermute | solution.py:334
  25.7 2.1 %all-gather.1 = f32[108,8,128]{2,1,0:T(8,128)S(1)} all-gather(f32[54,8,128]{2,1,0:T(8,128)S(1)} %get-tuple-element.29), channel_id=3, replica_groups=mesh['gx_0'=2,'gx_1'=16,'gx_2'=2,'gy_0'=2,'gy_1'=8] {'gx_2'}, dimensions={0}, use_global_device_ids=true | all-gather | bytes 663552 | tf_op jit(solution)/shard_map/all_gather | solution.py:339
  27.9 3.2 %collective-permute-done.3.far.refs_4_ = f32[54,8,128]{2,1,0:T(8,128)S(1)} collective-permute-done((f32[54,8,128]{2,1,0:T(8,128)S(1)}, f32[54,8,128]{2,1,0:T(8,128)S(1)}, u32[]{:S(2)}, u32[]{:S(2)}) %collective-permute-start.3) | collective-permute-done | bytes 221216 | tf_op jit(solution)/shard_map/ppermute | solution.py:334
  31.1 0.1 shard_map.91
  31.2 5.3 %collective-permute-start.4 = (f32[336,128]{1,0:T(8,128)S(1)}, f32[336,128]{1,0:T(8,128)S(1)}, u32[]{:S(2)}, u32[]{:S(2)}) collective-permute-start(f32[336,128]{1,0:T(8,128)S(1)} %get-tuple-element.31), channel_id=1, source_target_pairs={{0,1},{2,3},{4,5},{6,7},{8,9},{10,11},{12,13},{14,15},{1,0},{3,2},... | collective-permute-start | bytes 516104 | tf_op jit(solution)/shard_map/ppermute | solution.py:334
  36.5 0.7 collective-permute-start.5
  37.2 27.6 %all_to_all.20 = f32[32,1,128]{2,1,0:T(1,128)S(1)} all-to-all(f32[32,1,128]{2,1,0:T(1,128)S(1)} %get-tuple-element.27), channel_id=1, replica_groups=mesh['gx_0'=2,'gx_1'=16,'gx_2'=2,'gy_0'=2,'gy_1'=8] {'gx_1','gx_2'}, dimensions={0} | all-to-all | bytes 32768 | tf_op jit(solution)/shard_map/all_to_all | solution.py:347
  64.8 0.1 reduce_sum.18
  64.9 19.0 %all_to_all.21.refs_0_.refs_1_ = f32[32,1,128]{2,1,0:T(1,128)S(1)} all-to-all(f32[32,1,128]{2,1,0:T(1,128)S(1)} %broadcast_in_dim.4), channel_id=1, replica_groups=mesh['gx_0'=2,'gx_1'=16,'gx_2'=2,'gy_0'=2,'gy_1'=8] {'gx_0','gy_0','gy_1'}, dimensions={0} | all-to-all | bytes 32768 | tf_op jit(solution)/shard_map/all_to_all | solution.py:350
  83.9 1.3 %shard_map.92 = (f32[3,4,8,128]{3,2,1,0:T(8,128)S(1)}, f32[3,4,8,128]{3,2,1,0:T(8,128)}, f32[32,1,128]{2,1,0:T(1,128)S(1)}) custom-call(f32[32,1,128]{2,1,0:T(1,128)S(1)} %all_to_all.21.refs_0_.refs_1_, f32[3,4,8,128]{3,2,1,0:T(8,128)S(1)} %get-tuple-element.28.value.refs_1_.refs_4_, f32[5,3,4,8,128]{4,3,2,1,0:T(8,128)S(1)} %copy-done, ...), custom_call_target="tpu_custom_call" | custom-call | flops 20000 | bytes 100000 | tf_op jit(solution)/shard_map/pallas_call | solution.py:382
  85.2 17.0 %all_to_all.22 = f32[32,1,128]{2,1,0:T(1,128)S(1)} all-to-all(f32[32,1,128]{2,1,0:T(1,128)S(1)} %get-tuple-element.35), channel_id=1, replica_groups=mesh['gx_0'=2,'gx_1'=16,'gx_2'=2,'gy_0'=2,'gy_1'=8] {'gx_1','gx_2'}, dimensions={0} | all-to-all | bytes 32768 | tf_op jit(solution)/shard_map/all_to_all | solution.py:347
  102.2 0.1 reduce_sum.19
  102.2 11.6 %all_to_all.23.refs_0_ = f32[32,1,128]{2,1,0:T(1,128)S(1)} all-to-all(f32[32,1,128]{2,1,0:T(1,128)S(1)} %broadcast_in_dim.5), channel_id=1, replica_groups=mesh['gx_0'=2,'gx_1'=16,'gx_2'=2,'gy_0'=2,'gy_1'=8] {'gx_0','gy_0','gy_1'}, dimensions={0} | all-to-all | bytes 32768 | tf_op jit(solution)/shard_map/all_to_all | solution.py:350
  113.9 0.8 shard_map.93
  (14 shorter events, 0.1 us)
Async XLA Ops:
  1.8 16.5 %collective-permute-start = (f32[17,8,128]{2,1,0:T(8,128)S(1)}, f32[17,8,128]{2,1,0:T(8,128)S(1)}, u32[]{:S(2)}, u32[]{:S(2)}) collective-permute-start(f32[17,8,128]{2,1,0:T(8,128)S(1)} %get-tuple-element.24), channel_id=1, source_target_pairs={{16,32},{48,64},{80,96},{112,128},{144,160},{176,192},{208,224},{2... | collective-permute-start | bytes 208904 | tf_op jit(solution)/shard_map/ppermute | solution.py:334
  7.2 13.8 %copy-start.1 = (f32[5,3,4,8,128]{4,3,2,1,0:T(8,128)S(1)}, f32[5,3,4,8,128]{4,3,2,1,0:T(8,128)}, u32[]{:S(2)}) copy-start(f32[5,3,4,8,128]{4,3,2,1,0:T(8,128)} %refs_8_.1) | copy-start | bytes 737284
  18.3 2.7 %copy-start.2 = (f32[3,4,8,128]{3,2,1,0:T(8,128)S(1)}, f32[3,4,8,128]{3,2,1,0:T(8,128)}, u32[]{:S(2)}) copy-start(f32[3,4,8,128]{3,2,1,0:T(8,128)} %prev.3) | copy-start | bytes 147460
  18.3 4.9 %collective-permute-start.1 = (f32[104,128]{1,0:T(8,128)S(1)}, f32[104,128]{1,0:T(8,128)S(1)}, u32[]{:S(2)}, u32[]{:S(2)}) collective-permute-start(f32[104,128]{1,0:T(8,128)S(1)} %get-tuple-element.25), channel_id=1, source_target_pairs={{0,1},{2,3},{4,5},{6,7},{8,9},{10,11},{12,13},{14,15},{1,0},{3,2},... | collective-permute-start | bytes 159752 | tf_op jit(solution)/shard_map/ppermute | solution.py:334
  20.2 3.0 %collective-permute-start.2 = (f32[104,128]{1,0:T(8,128)S(1)}, f32[104,128]{1,0:T(8,128)S(1)}, u32[]{:S(2)}, u32[]{:S(2)}) collective-permute-start(f32[104,128]{1,0:T(8,128)S(1)} %get-tuple-element.26), channel_id=1, source_target_pairs={{1,2},{3,4},{5,6},{7,8},{9,10},{11,12},{13,14},{2,1},{4,3},{6,5},{... | collective-permute-start | bytes 159752 | tf_op jit(solution)/shard_map/ppermute | solution.py:334
  21.1 2.6 %copy-start = (f32[5,3,4,8,128]{4,3,2,1,0:T(8,128)S(1)}, f32[5,3,4,8,128]{4,3,2,1,0:T(8,128)}, u32[]{:S(2)}) copy-start(f32[5,3,4,8,128]{4,3,2,1,0:T(8,128)} %refs_3_.1) | copy-start | bytes 737284
  23.8 7.3 %collective-permute-start.3 = (f32[54,8,128]{2,1,0:T(8,128)S(1)}, f32[54,8,128]{2,1,0:T(8,128)S(1)}, u32[]{:S(2)}, u32[]{:S(2)}) collective-permute-start(f32[54,8,128]{2,1,0:T(8,128)S(1)} %get-tuple-element.30), channel_id=1, source_target_pairs={{16,32},{48,64},{80,96},{112,128},{144,160},{176,192},{208,224},{2... | collective-permute-start | bytes 663560 | tf_op jit(solution)/shard_map/ppermute | solution.py:334
  31.2 52.7 %collective-permute-start.4 = (f32[336,128]{1,0:T(8,128)S(1)}, f32[336,128]{1,0:T(8,128)S(1)}, u32[]{:S(2)}, u32[]{:S(2)}) collective-permute-start(f32[336,128]{1,0:T(8,128)S(1)} %get-tuple-element.31), channel_id=1, source_target_pairs={{0,1},{2,3},{4,5},{6,7},{8,9},{10,11},{12,13},{14,15},{1,0},{3,2},... | collective-permute-start | bytes 516104 | tf_op jit(solution)/shard_map/ppermute | solution.py:334
  36.5 47.4 %collective-permute-start.5 = (f32[336,128]{1,0:T(8,128)S(1)}, f32[336,128]{1,0:T(8,128)S(1)}, u32[]{:S(2)}, u32[]{:S(2)}) collective-permute-start(f32[336,128]{1,0:T(8,128)S(1)} %get-tuple-element.32), channel_id=1, source_target_pairs={{1,2},{3,4},{5,6},{7,8},{9,10},{11,12},{13,14},{2,1},{4,3},{6,5},{... | collective-permute-start | bytes 516104 | tf_op jit(solution)/shard_map/ppermute | solution.py:334
  85.2 28.7 %copy-start.3 = (f32[3,4,8,128]{3,2,1,0:T(8,128)S(1)}, f32[3,4,8,128]{3,2,1,0:T(8,128)}, u32[]{:S(2)}) copy-start(f32[3,4,8,128]{3,2,1,0:T(8,128)} %refs_5_.1) | copy-start | bytes 147460

commit v6 on v5

--- a/solution.py
+++ b/solution.py
@@ -308,7 +308,8 @@
         payload[k] = row
 
 
-def mix_second(entries, rows, first_rows, value, hist, first_value, prev, field):
+def mix_second(entries, rows, first_rows, value, hist, first_value, prev, resid, field, resid_out):
+    resid_out[...] = resid[...]
     row = gathered(first_rows)
     s = [entry(row, k) for k in range(NORM + 1)]
     gram = {}
@@ -340,7 +341,9 @@
 
 
 def edges_of(even_pair, odd_pair):
-    return swap(even_pair, GY, 0), swap(odd_pair, GY, 1)
+    even_pair = swap(even_pair, GY, 0)
+    odd_pair = swap(odd_pair, GY, 1)
+    return even_pair, odd_pair
 
 
 def exchange(payload):
@@ -383,10 +386,9 @@
         lambda *refs: second_map(entries, *refs), [shape, shape, fan], [frames, (2, GROUP_ROWS, 128), *work]
     )(sums, value, hist_val, *faces, *edges, static, hist_res, newest)
     next_sums = exchange(payload)
-    (out,) = call(lambda *refs: mix_second(entries, *refs), [shape])(
-        next_sums, sums, value_next, hist_val, value, value_prev
+    return call(lambda *refs: mix_second(entries, *refs), [shape, shape])(
+        next_sums, sums, value_next, hist_val, value, value_prev, resid
     )
-    return (out, resid)
 
 
 def build(torus):

time: 115 us -> 115 us (level)
  no operation moved by 1% of the time
where the time goes in v6:
time: 115 us; the launch traced here: 114 us
  blocking collectives  88.5 us (77%)
  starting transfers between devices  15.8 us (14%)
  waiting for transfers between devices  5.3 us (5%)
  Pallas kernels  3.63 us (3%)
    all_to_all x2, blocking collectives, exchange(): rows = lax.all_to_all(payload, CHAIN, 0, 0)  44.6 us
    all_to_all x2, blocking collectives, exchange(): return lax.all_to_all(rows, PLANE, 0, 0)  30.6 us
    ppermute x6, starting transfers between devices, swap(): return lax.ppermute(cells, axes, pairs + [(j, i) for i, j in pairs])  15.8 us
    all_gather x2, blocking collectives, faces_of(): return (lax.all_gather(even_pair, GX[2]), odd_pair)  13.2 us
    ppermute x6, waiting for transfers between devices, swap(): return lax.ppermute(cells, axes, pairs + [(j, i) for i, j in pairs])  5.3 us
  transfers between devices with their start and end apart: 6, of which 2 were waited for; matrix products, arithmetic and copies ran while one was open for 0% of the time, Pallas kernels for 0%

profile of v6, /device:TPU:1, one launch (start us, length us, event | category | flops | bytes accessed | tf_op | source)
XLA Modules:
  0.0 114.2 jit_solution(5512539135597328931)
XLA Ops:
  0.6 1.1 %shard_map.86 = (f32[17,8,128]{2,1,0:T(8,128)S(1)}, f32[17,8,128]{2,1,0:T(8,128)S(1)}, f32[3,4,8,128]{3,2,1,0:T(8,128)S(1)}, f32[3,4,8,128]{3,2,1,0:T(8,128)S(1)}, f32[4,8,128]{2,1,0:T(8,128)S(1)}) custom-call(f32[3,4,8,128]{3,2,1,0:T(8,128)} %vel.1, f32[3,4,8,128]{3,2,1,0:T(8,128)} %forcing.1, f32[4,8,128]{2,1,0:T(8,128)} %visc.1), custom_call_target="tpu_custom_call" | custom-call | flops 20000 | bytes 100000 | tf_op jit(solution)/shard_map/pallas_call | solution.py:366
  1.8 5.4 %collective-permute-start = (f32[17,8,128]{2,1,0:T(8,128)S(1)}, f32[17,8,128]{2,1,0:T(8,128)S(1)}, u32[]{:S(2)}, u32[]{:S(2)}) collective-permute-start(f32[17,8,128]{2,1,0:T(8,128)S(1)} %get-tuple-element.24), channel_id=1, source_target_pairs={{16,32},{48,64},{80,96},{112,128},{144,160},{176,192},{208,224},{2... | collective-permute-start | bytes 208904 | tf_op jit(solution)/shard_map/ppermute | solution.py:335
  7.2 0.0 copy-start.1
  7.2 11.1 %all-gather = f32[34,8,128]{2,1,0:T(8,128)S(1)} all-gather(f32[17,8,128]{2,1,0:T(8,128)S(1)} %get-tuple-element.23), channel_id=2, replica_groups=mesh['gx_0'=2,'gx_1'=16,'gx_2'=2,'gy_0'=2,'gy_1'=8] {'gx_2'}, dimensions={0}, use_global_device_ids=true | all-gather | bytes 208896 | tf_op jit(solution)/shard_map/all_gather | solution.py:340
  18.3 1.9 %collective-permute-start.1 = (f32[104,128]{1,0:T(8,128)S(1)}, f32[104,128]{1,0:T(8,128)S(1)}, u32[]{:S(2)}, u32[]{:S(2)}) collective-permute-start(f32[104,128]{1,0:T(8,128)S(1)} %get-tuple-element.25), channel_id=1, source_target_pairs={{0,1},{2,3},{4,5},{6,7},{8,9},{10,11},{12,13},{14,15},{1,0},{3,2},... | collective-permute-start | bytes 159752 | tf_op jit(solution)/shard_map/ppermute | solution.py:335
  20.2 0.7 collective-permute-start.2
  20.9 0.2 shard_map.88.gram
  21.1 2.1 %collective-permute-done.1.even_pair = f32[104,128]{1,0:T(8,128)S(1)} collective-permute-done((f32[104,128]{1,0:T(8,128)S(1)}, f32[104,128]{1,0:T(8,128)S(1)}, u32[]{:S(2)}, u32[]{:S(2)}) %collective-permute-start.1) | collective-permute-done | bytes 53280 | tf_op jit(solution)/shard_map/ppermute | solution.py:335
  23.2 0.5 shard_map.89
  23.8 1.9 %collective-permute-start.3 = (f32[54,8,128]{2,1,0:T(8,128)S(1)}, f32[54,8,128]{2,1,0:T(8,128)S(1)}, u32[]{:S(2)}, u32[]{:S(2)}) collective-permute-start(f32[54,8,128]{2,1,0:T(8,128)S(1)} %get-tuple-element.30), channel_id=1, source_target_pairs={{16,32},{48,64},{80,96},{112,128},{144,160},{176,192},{208,224},{2... | collective-permute-start | bytes 663560 | tf_op jit(solution)/shard_map/ppermute | solution.py:335
  25.7 2.1 %all-gather.1 = f32[108,8,128]{2,1,0:T(8,128)S(1)} all-gather(f32[54,8,128]{2,1,0:T(8,128)S(1)} %get-tuple-element.29), channel_id=3, replica_groups=mesh['gx_0'=2,'gx_1'=16,'gx_2'=2,'gy_0'=2,'gy_1'=8] {'gx_2'}, dimensions={0}, use_global_device_ids=true | all-gather | bytes 663552 | tf_op jit(solution)/shard_map/all_gather | solution.py:340
  27.9 3.2 %collective-permute-done.3.far.refs_4_ = f32[54,8,128]{2,1,0:T(8,128)S(1)} collective-permute-done((f32[54,8,128]{2,1,0:T(8,128)S(1)}, f32[54,8,128]{2,1,0:T(8,128)S(1)}, u32[]{:S(2)}, u32[]{:S(2)}) %collective-permute-start.3) | collective-permute-done | bytes 221216 | tf_op jit(solution)/shard_map/ppermute | solution.py:335
  31.1 0.1 shard_map.91
  31.2 5.3 %collective-permute-start.4 = (f32[336,128]{1,0:T(8,128)S(1)}, f32[336,128]{1,0:T(8,128)S(1)}, u32[]{:S(2)}, u32[]{:S(2)}) collective-permute-start(f32[336,128]{1,0:T(8,128)S(1)} %get-tuple-element.31), channel_id=1, source_target_pairs={{0,1},{2,3},{4,5},{6,7},{8,9},{10,11},{12,13},{14,15},{1,0},{3,2},... | collective-permute-start | bytes 516104 | tf_op jit(solution)/shard_map/ppermute | solution.py:335
  36.5 0.7 collective-permute-start.5
  37.2 27.6 %all_to_all.20 = f32[32,1,128]{2,1,0:T(1,128)S(1)} all-to-all(f32[32,1,128]{2,1,0:T(1,128)S(1)} %get-tuple-element.27), channel_id=1, replica_groups=mesh['gx_0'=2,'gx_1'=16,'gx_2'=2,'gy_0'=2,'gy_1'=8] {'gx_1','gx_2'}, dimensions={0} | all-to-all | bytes 32768 | tf_op jit(solution)/shard_map/all_to_all | solution.py:350
  64.8 0.1 reduce_sum.18
  64.9 19.0 %all_to_all.21.refs_0_.refs_1_ = f32[32,1,128]{2,1,0:T(1,128)S(1)} all-to-all(f32[32,1,128]{2,1,0:T(1,128)S(1)} %broadcast_in_dim.4), channel_id=1, replica_groups=mesh['gx_0'=2,'gx_1'=16,'gx_2'=2,'gy_0'=2,'gy_1'=8] {'gx_0','gy_0','gy_1'}, dimensions={0} | all-to-all | bytes 32768 | tf_op jit(solution)/shard_map/all_to_all | solution.py:353
  83.9 0.8 shard_map.92
  84.6 0.0 copy-start.3
  84.7 17.0 %all_to_all.22 = f32[32,1,128]{2,1,0:T(1,128)S(1)} all-to-all(f32[32,1,128]{2,1,0:T(1,128)S(1)} %get-tuple-element.35), channel_id=1, replica_groups=mesh['gx_0'=2,'gx_1'=16,'gx_2'=2,'gy_0'=2,'gy_1'=8] {'gx_1','gx_2'}, dimensions={0} | all-to-all | bytes 32768 | tf_op jit(solution)/shard_map/all_to_all | solution.py:350
  101.7 0.1 reduce_sum.19
  101.7 11.6 %all_to_all.23.refs_0_ = f32[32,1,128]{2,1,0:T(1,128)S(1)} all-to-all(f32[32,1,128]{2,1,0:T(1,128)S(1)} %broadcast_in_dim.5), channel_id=1, replica_groups=mesh['gx_0'=2,'gx_1'=16,'gx_2'=2,'gy_0'=2,'gy_1'=8] {'gx_0','gy_0','gy_1'}, dimensions={0} | all-to-all | bytes 32768 | tf_op jit(solution)/shard_map/all_to_all | solution.py:353
  113.4 0.8 shard_map.93
  (14 shorter events, 0.1 us)
Async XLA Ops:
  1.8 16.5 %collective-permute-start = (f32[17,8,128]{2,1,0:T(8,128)S(1)}, f32[17,8,128]{2,1,0:T(8,128)S(1)}, u32[]{:S(2)}, u32[]{:S(2)}) collective-permute-start(f32[17,8,128]{2,1,0:T(8,128)S(1)} %get-tuple-element.24), channel_id=1, source_target_pairs={{16,32},{48,64},{80,96},{112,128},{144,160},{176,192},{208,224},{2... | collective-permute-start | bytes 208904 | tf_op jit(solution)/shard_map/ppermute | solution.py:335
  7.2 13.8 %copy-start.1 = (f32[5,3,4,8,128]{4,3,2,1,0:T(8,128)S(1)}, f32[5,3,4,8,128]{4,3,2,1,0:T(8,128)}, u32[]{:S(2)}) copy-start(f32[5,3,4,8,128]{4,3,2,1,0:T(8,128)} %refs_8_.1) | copy-start | bytes 737284
  18.3 2.7 %copy-start.2 = (f32[3,4,8,128]{3,2,1,0:T(8,128)S(1)}, f32[3,4,8,128]{3,2,1,0:T(8,128)}, u32[]{:S(2)}) copy-start(f32[3,4,8,128]{3,2,1,0:T(8,128)} %prev.3) | copy-start | bytes 147460
  18.3 4.9 %collective-permute-start.1 = (f32[104,128]{1,0:T(8,128)S(1)}, f32[104,128]{1,0:T(8,128)S(1)}, u32[]{:S(2)}, u32[]{:S(2)}) collective-permute-start(f32[104,128]{1,0:T(8,128)S(1)} %get-tuple-element.25), channel_id=1, source_target_pairs={{0,1},{2,3},{4,5},{6,7},{8,9},{10,11},{12,13},{14,15},{1,0},{3,2},... | collective-permute-start | bytes 159752 | tf_op jit(solution)/shard_map/ppermute | solution.py:335
  20.2 3.0 %collective-permute-start.2 = (f32[104,128]{1,0:T(8,128)S(1)}, f32[104,128]{1,0:T(8,128)S(1)}, u32[]{:S(2)}, u32[]{:S(2)}) collective-permute-start(f32[104,128]{1,0:T(8,128)S(1)} %get-tuple-element.26), channel_id=1, source_target_pairs={{1,2},{3,4},{5,6},{7,8},{9,10},{11,12},{13,14},{2,1},{4,3},{6,5},{... | collective-permute-start | bytes 159752 | tf_op jit(solution)/shard_map/ppermute | solution.py:335
  21.1 2.6 %copy-start = (f32[5,3,4,8,128]{4,3,2,1,0:T(8,128)S(1)}, f32[5,3,4,8,128]{4,3,2,1,0:T(8,128)}, u32[]{:S(2)}) copy-start(f32[5,3,4,8,128]{4,3,2,1,0:T(8,128)} %refs_3_.1) | copy-start | bytes 737284
  23.8 7.3 %collective-permute-start.3 = (f32[54,8,128]{2,1,0:T(8,128)S(1)}, f32[54,8,128]{2,1,0:T(8,128)S(1)}, u32[]{:S(2)}, u32[]{:S(2)}) collective-permute-start(f32[54,8,128]{2,1,0:T(8,128)S(1)} %get-tuple-element.30), channel_id=1, source_target_pairs={{16,32},{48,64},{80,96},{112,128},{144,160},{176,192},{208,224},{2... | collective-permute-start | bytes 663560 | tf_op jit(solution)/shard_map/ppermute | solution.py:335
  31.2 52.7 %collective-permute-start.4 = (f32[336,128]{1,0:T(8,128)S(1)}, f32[336,128]{1,0:T(8,128)S(1)}, u32[]{:S(2)}, u32[]{:S(2)}) collective-permute-start(f32[336,128]{1,0:T(8,128)S(1)} %get-tuple-element.31), channel_id=1, source_target_pairs={{0,1},{2,3},{4,5},{6,7},{8,9},{10,11},{12,13},{14,15},{1,0},{3,2},... | collective-permute-start | bytes 516104 | tf_op jit(solution)/shard_map/ppermute | solution.py:335
  36.5 47.4 %collective-permute-start.5 = (f32[336,128]{1,0:T(8,128)S(1)}, f32[336,128]{1,0:T(8,128)S(1)}, u32[]{:S(2)}, u32[]{:S(2)}) collective-permute-start(f32[336,128]{1,0:T(8,128)S(1)} %get-tuple-element.32), channel_id=1, source_target_pairs={{1,2},{3,4},{5,6},{7,8},{9,10},{11,12},{13,14},{2,1},{4,3},{6,5},{... | collective-permute-start | bytes 516104 | tf_op jit(solution)/shard_map/ppermute | solution.py:335
  84.6 28.7 %copy-start.3 = (f32[3,4,8,128]{3,2,1,0:T(8,128)S(1)}, f32[3,4,8,128]{3,2,1,0:T(8,128)}, u32[]{:S(2)}) copy-start(f32[3,4,8,128]{3,2,1,0:T(8,128)} %refs_5_.1) | copy-start | bytes 147460

commit v7 on v6

--- a/solution.py
+++ b/solution.py
@@ -51,7 +51,7 @@
     return lax.rem(lax.axis_index(axes[-1]), 2) == 1
 
 
-def pack_first(vel, forcing, visc, even_pair, odd_pair, vel_near, forcing_near, visc_near, sem):
+def pack_first(vel, forcing, visc, hist, even_pair, odd_pair, vel_near, forcing_near, visc_near, sem):
     cx = vel.shape[1]
     odd = odd_place(GX)
     copies = []
@@ -61,6 +61,8 @@
         pieces = [(vel.at[c, three], out.at[pl.ds(3 * c, 3)]) for c in range(3)]
         pieces += [(forcing.at[c, two], out.at[pl.ds(9 + 2 * c, 2)]) for c in range(3)]
         pieces += [(visc.at[two], out.at[pl.ds(15, 2)])]
+        if out is even_pair:
+            pieces += [(hist.at[j, c, three], out.at[pl.ds(17 + 9 * j + 3 * c, 3)]) for j in range(M) for c in range(3)]
         for src, dst in pieces:
             copies.append(pltpu.make_async_copy(src, dst, sem.at[len(copies)]))
             copies[-1].start()
@@ -120,20 +122,32 @@
     pack_edges(tiles, fixed, even_pair, odd_pair, 0, True)
 
 
-def pack_mixed_first(value, hist, even_pair, odd_pair):
-    cx = value.shape[1]
+def pack_faces(field, even_pair, odd_pair):
+    cx = field.shape[-3]
     odd = odd_place(GX)
     for out, low in ((even_pair, odd), (odd_pair, jnp.logical_not(odd))):
-        first = jnp.where(low, 0, cx - 3)
-        for g in range(GROUPS):
-            src = value if g == 0 else hist.at[g - 1]
-            for c in range(3):
-                for d in range(3):
-                    out[9 * g + 3 * c + d] = src[c, first + d]
-
-
-def pack_mixed_second(value, hist, near, far, even_pair, odd_pair, tiles):
-    left, right = arrived(GX, near, far)
+        if out is not None:
+            first = jnp.where(low, 0, cx - 3)
+            for g in range(out.shape[0] // 9):
+                src = field.at[g] if len(field.shape) == 5 else field
+                for c in range(3):
+                    for d in range(3):
+                        out[9 * g + 3 * c + d] = src[c, first + d]
+
+
+def mixed_sides(near, near_value, far_value, far_hist):
+    odd = odd_place(GX)
+    near = near.at[jnp.where(odd, 0, 1)]
+    near_value = near_value.at[jnp.where(odd, 0, 1)]
+    even_pair = lambda i: near_value[i] if i < 9 else near[17 + i - 9]
+    odd_pair = lambda i: far_value[i] if i < 9 else far_hist[i - 9]
+    before = lambda i: jnp.where(odd, even_pair(i), odd_pair(i))
+    after = lambda i: jnp.where(odd, odd_pair(i), even_pair(i))
+    return before, after
+
+
+def pack_mixed_second(value, hist, near, near_value, far_value, far_hist, even_pair, odd_pair, tiles):
+    left, right = mixed_sides(near, near_value, far_value, far_hist)
     for g in range(GROUPS):
         src = value if g == 0 else hist.at[g - 1]
         block = tiles.at[g]
@@ -268,7 +282,7 @@
     return total
 
 
-def second_map(entries, rows, value, hist_val, near, far, even_pair, odd_pair, fixed, hist, newest, value_next, resid, payload, frames, edges, coef, one, two):
+def second_map(entries, rows, value, hist_val, near, near_value, far_value, far_hist, even_pair, odd_pair, fixed, hist, newest, value_next, resid, payload, frames, edges, coef, one, two):
     row = gathered(rows)
     s = [entry(row, k) for k in range(PREV)]
     gram = {pair: s[k] for k, pair in enumerate(PAIRS)}
@@ -281,7 +295,7 @@
         return total
 
     frames[...] = jnp.zeros_like(frames)
-    left, right = arrived(GX, near, far)
+    left, right = mixed_sides(near, near_value, far_value, far_hist)
     field = {}
     for t in range(10 * FIELD):
         plane, c = divmod(t, FIELD)
@@ -361,10 +375,13 @@
     frames = (10 * FIELD * ROWS, 128)
     fixed = (8 * STATIC * ROWS, 128)
 
-    hbm = [pl.BlockSpec(memory_space=pltpu.HBM)] * 3
-    far_away = [pltpu.with_memory_space_constraint(x, pltpu.HBM) for x in (velocity, forcing, viscosity)]
+    hbm = [pl.BlockSpec(memory_space=pltpu.HBM)] * 4
+    far_away = [pltpu.with_memory_space_constraint(x, pltpu.HBM) for x in (velocity, forcing, viscosity, hist_val)]
     *packed, velocity, forcing, viscosity = call(
-        pack_first, [(17, 8, 128)] * 2 + [shape, shape, shape[1:]], [pltpu.SemaphoreType.DMA((17,))], in_specs=hbm
+        pack_first,
+        [(17 + 9 * M, 8, 128), (17, 8, 128), shape, shape, shape[1:]],
+        [pltpu.SemaphoreType.DMA((17 + 3 * M,))],
+        in_specs=hbm,
     )(*far_away)
     faces = faces_of(*packed)
     (gram,) = call(gram_part, [(1, 128)], flops=4000000)(hist_res, residual_prev)
@@ -373,18 +390,21 @@
         velocity, forcing, viscosity, *faces
     )
     edges = edges_of(*packed)
+    (far_hist,) = call(lambda field, out: pack_faces(field, None, out), [(9 * M, 8, 128)])(hist_val)
+    far_hist = swap(far_hist, GX, 1)
     value, newest, static, payload = call(first_map, [shape, shape, fixed, fan], [frames, *work])(
         velocity, forcing, viscosity, *faces, *edges, hist_res, residual_prev, gram
     )
     sums = exchange(payload)
-    packed = call(pack_mixed_first, [(9 * GROUPS, 8, 128)] * 2)(value, hist_val)
-    faces = faces_of(*packed)
+    packed = call(pack_faces, [(9, 8, 128)] * 2)(value)
+    near_value, far_value = faces_of(*packed)
+    near = (faces[0], near_value, far_value, far_hist)
     edge = (GROUPS * GROUP_ROWS, 128)
-    packed = call(pack_mixed_second, [edge, edge], [(GROUPS, 10 * FIELD * 8, 128)])(value, hist_val, *faces)
+    packed = call(pack_mixed_second, [edge, edge], [(GROUPS, 10 * FIELD * 8, 128)])(value, hist_val, *near)
     edges = edges_of(*packed)
     value_next, resid, payload = call(
         lambda *refs: second_map(entries, *refs), [shape, shape, fan], [frames, (2, GROUP_ROWS, 128), *work]
-    )(sums, value, hist_val, *faces, *edges, static, hist_res, newest)
+    )(sums, value, hist_val, *near, *edges, static, hist_res, newest)
     next_sums = exchange(payload)
     return call(lambda *refs: mix_second(entries, *refs), [shape, shape])(
         next_sums, sums, value_next, hist_val, value, value_prev, resid

time: 115 us -> 120 us (1.043)
  blocking collectives: 88.5 us -> 92.7 us
  starting transfers between devices: 15.8 us -> 17.9 us
  waiting for transfers between devices: 5.3 us -> 3.59 us
    all_to_all x2, blocking collectives: 44.6 us -> 47.5 us  [exchange(): rows = lax.all_to_all(payload, CHAIN, 0, 0)]
    all_to_all x2, blocking collectives: 30.6 us -> 33.4 us  [exchange(): return lax.all_to_all(rows, PLANE, 0, 0)]
    ppermute x6 -> x7, starting transfers between devices: 15.8 us -> 17.9 us  [swap(): return lax.ppermute(cells, axes, pairs + [(j, i) for i, j in pairs])]
    ppermute x6 -> x7, waiting for transfers between devices: 5.3 us -> 3.59 us  [swap(): return lax.ppermute(cells, axes, pairs + [(j, i) for i, j in pairs])]
    all_gather x2, blocking collectives: 13.2 us -> 11.8 us  [faces_of(): return (lax.all_gather(even_pair, GX[2]), odd_pair)]
  transfers between devices with their start and end apart: 6 -> 7, of which waited for: 2 -> 2; matrix products, arithmetic and copies ran while one was open for 0% -> 0% of each run, Pallas kernels for 0% -> 2%
where the time goes in v7:
time: 120 us
  blocking collectives  92.7 us (77%)
  starting transfers between devices  17.9 us (15%)
  Pallas kernels  3.82 us (3%)
  waiting for transfers between devices  3.59 us (3%)
    all_to_all x2, blocking collectives, exchange(): rows = lax.all_to_all(payload, CHAIN, 0, 0)  47.5 us
    all_to_all x2, blocking collectives, exchange(): return lax.all_to_all(rows, PLANE, 0, 0)  33.4 us
    ppermute x7, starting transfers between devices, swap(): return lax.ppermute(cells, axes, pairs + [(j, i) for i, j in pairs])  17.9 us
    all_gather x2, blocking collectives, faces_of(): return (lax.all_gather(even_pair, GX[2]), odd_pair)  11.8 us
    ppermute x7, waiting for transfers between devices, swap(): return lax.ppermute(cells, axes, pairs + [(j, i) for i, j in pairs])  3.59 us
  transfers between devices with their start and end apart: 7, of which 2 were waited for; matrix products, arithmetic and copies ran while one was open for 0% of the time, Pallas kernels for 2%

profile of v7, /device:TPU:1, one launch (start us, length us, event | category | flops | bytes accessed | tf_op | source)
XLA Modules:
  0.0 119.9 jit_solution(12108380819310225954)
XLA Ops:
  0.6 0.9 copy-done
  1.6 5.4 %collective-permute-start.4 = (f32[45,8,128]{2,1,0:T(8,128)S(1)}, f32[45,8,128]{2,1,0:T(8,128)S(1)}, u32[]{:S(2)}, u32[]{:S(2)}) collective-permute-start(f32[45,8,128]{2,1,0:T(8,128)S(1)} %shard_map.91), channel_id=1, source_target_pairs={{16,32},{48,64},{80,96},{112,128},{144,160},{176,192},{208,224},{2... | collective-permute-start | bytes 552968 | tf_op jit(solution)/shard_map/ppermute | solution.py:349
  7.0 1.3 %shard_map.86 = (f32[62,8,128]{2,1,0:T(8,128)S(1)}, f32[17,8,128]{2,1,0:T(8,128)S(1)}, f32[3,4,8,128]{3,2,1,0:T(8,128)S(1)}, f32[3,4,8,128]{3,2,1,0:T(8,128)S(1)}, f32[4,8,128]{2,1,0:T(8,128)S(1)}) custom-call(f32[3,4,8,128]{3,2,1,0:T(8,128)} %vel.1, f32[3,4,8,128]{3,2,1,0:T(8,128)} %forcing.1, f32[4,8,128]{2,1,0:T(8,128)} %visc.1, f32[5,3,4,8,128]{4,3,2,1,0:T(8,128)} %refs_3_.1), custom_call_target="tpu_custom_call" | custom-call | flops 20000 | bytes 100000 | tf_op jit(solution)/shard_map/pallas_call | solution.py:380
  8.3 1.9 %collective-permute-start = (f32[17,8,128]{2,1,0:T(8,128)S(1)}, f32[17,8,128]{2,1,0:T(8,128)S(1)}, u32[]{:S(2)}, u32[]{:S(2)}) collective-permute-start(f32[17,8,128]{2,1,0:T(8,128)S(1)} %get-tuple-element.24), channel_id=1, source_target_pairs={{16,32},{48,64},{80,96},{112,128},{144,160},{176,192},{208,224},{2... | collective-permute-start | bytes 208904 | tf_op jit(solution)/shard_map/ppermute | solution.py:349
  10.3 9.9 %all-gather = f32[124,8,128]{2,1,0:T(8,128)S(1)} all-gather(f32[62,8,128]{2,1,0:T(8,128)S(1)} %get-tuple-element.23), channel_id=2, replica_groups=mesh['gx_0'=2,'gx_1'=16,'gx_2'=2,'gy_0'=2,'gy_1'=8] {'gx_2'}, dimensions={0}, use_global_device_ids=true | all-gather | bytes 761856 | tf_op jit(solution)/shard_map/all_gather | solution.py:354
  20.3 2.1 %collective-permute-start.1 = (f32[104,128]{1,0:T(8,128)S(1)}, f32[104,128]{1,0:T(8,128)S(1)}, u32[]{:S(2)}, u32[]{:S(2)}) collective-permute-start(f32[104,128]{1,0:T(8,128)S(1)} %get-tuple-element.25), channel_id=1, source_target_pairs={{0,1},{2,3},{4,5},{6,7},{8,9},{10,11},{12,13},{14,15},{1,0},{3,2},... | collective-permute-start | bytes 159752 | tf_op jit(solution)/shard_map/ppermute | solution.py:349
  22.3 0.7 collective-permute-start.2
  23.0 0.2 shard_map.88.gram
  23.2 2.1 %collective-permute-done.1.even_pair = f32[104,128]{1,0:T(8,128)S(1)} collective-permute-done((f32[104,128]{1,0:T(8,128)S(1)}, f32[104,128]{1,0:T(8,128)S(1)}, u32[]{:S(2)}, u32[]{:S(2)}) %collective-permute-start.1) | collective-permute-done | bytes 53280 | tf_op jit(solution)/shard_map/ppermute | solution.py:349
  25.3 0.5 shard_map.89
  25.9 1.9 %collective-permute-start.3 = (f32[9,8,128]{2,1,0:T(8,128)S(1)}, f32[9,8,128]{2,1,0:T(8,128)S(1)}, u32[]{:S(2)}, u32[]{:S(2)}) collective-permute-start(f32[9,8,128]{2,1,0:T(8,128)S(1)} %get-tuple-element.30), channel_id=1, source_target_pairs={{16,32},{48,64},{80,96},{112,128},{144,160},{176,192},{208,224},{2... | collective-permute-start | bytes 110600 | tf_op jit(solution)/shard_map/ppermute | solution.py:349
  27.8 1.9 %all-gather.1 = f32[18,8,128]{2,1,0:T(8,128)S(1)} all-gather(f32[9,8,128]{2,1,0:T(8,128)S(1)} %get-tuple-element.29), channel_id=3, replica_groups=mesh['gx_0'=2,'gx_1'=16,'gx_2'=2,'gy_0'=2,'gy_1'=8] {'gx_2'}, dimensions={0}, use_global_device_ids=true | all-gather | bytes 110592 | tf_op jit(solution)/shard_map/all_gather | solution.py:354
  29.6 1.5 %collective-permute-done.3.far_value.refs_5_ = f32[9,8,128]{2,1,0:T(8,128)S(1)} collective-permute-done((f32[9,8,128]{2,1,0:T(8,128)S(1)}, f32[9,8,128]{2,1,0:T(8,128)S(1)}, u32[]{:S(2)}, u32[]{:S(2)}) %collective-permute-start.3) | collective-permute-done | bytes 36896 | tf_op jit(solution)/shard_map/ppermute | solution.py:349
  31.1 0.1 shard_map.92
  31.3 5.3 %collective-permute-start.5 = (f32[336,128]{1,0:T(8,128)S(1)}, f32[336,128]{1,0:T(8,128)S(1)}, u32[]{:S(2)}, u32[]{:S(2)}) collective-permute-start(f32[336,128]{1,0:T(8,128)S(1)} %get-tuple-element.31), channel_id=1, source_target_pairs={{0,1},{2,3},{4,5},{6,7},{8,9},{10,11},{12,13},{14,15},{1,0},{3,2},... | collective-permute-start | bytes 516104 | tf_op jit(solution)/shard_map/ppermute | solution.py:349
  36.5 0.7 collective-permute-start.6
  37.2 30.5 %all_to_all.20 = f32[32,1,128]{2,1,0:T(1,128)S(1)} all-to-all(f32[32,1,128]{2,1,0:T(1,128)S(1)} %get-tuple-element.27), channel_id=1, replica_groups=mesh['gx_0'=2,'gx_1'=16,'gx_2'=2,'gy_0'=2,'gy_1'=8] {'gx_1','gx_2'}, dimensions={0} | all-to-all | bytes 32768 | tf_op jit(solution)/shard_map/all_to_all | solution.py:364
  67.7 0.1 reduce_sum.18
  67.8 21.8 %all_to_all.21.refs_0_.refs_1_ = f32[32,1,128]{2,1,0:T(1,128)S(1)} all-to-all(f32[32,1,128]{2,1,0:T(1,128)S(1)} %broadcast_in_dim.4), channel_id=1, replica_groups=mesh['gx_0'=2,'gx_1'=16,'gx_2'=2,'gy_0'=2,'gy_1'=8] {'gx_0','gy_0','gy_1'}, dimensions={0} | all-to-all | bytes 32768 | tf_op jit(solution)/shard_map/all_to_all | solution.py:367
  89.6 0.8 shard_map.93
  90.4 17.0 %all_to_all.22 = f32[32,1,128]{2,1,0:T(1,128)S(1)} all-to-all(f32[32,1,128]{2,1,0:T(1,128)S(1)} %get-tuple-element.35), channel_id=1, replica_groups=mesh['gx_0'=2,'gx_1'=16,'gx_2'=2,'gy_0'=2,'gy_1'=8] {'gx_1','gx_2'}, dimensions={0} | all-to-all | bytes 32768 | tf_op jit(solution)/shard_map/all_to_all | solution.py:364
  107.4 0.1 reduce_sum.19
  107.4 11.6 %all_to_all.23.refs_0_ = f32[32,1,128]{2,1,0:T(1,128)S(1)} all-to-all(f32[32,1,128]{2,1,0:T(1,128)S(1)} %broadcast_in_dim.5), channel_id=1, replica_groups=mesh['gx_0'=2,'gx_1'=16,'gx_2'=2,'gy_0'=2,'gy_1'=8] {'gx_0','gy_0','gy_1'}, dimensions={0} | all-to-all | bytes 32768 | tf_op jit(solution)/shard_map/all_to_all | solution.py:367
  119.1 0.8 shard_map.94
  (19 shorter events, 0.1 us)
Async XLA Ops:
  0.6 0.9 copy-start
  1.6 29.5 %collective-permute-start.4 = (f32[45,8,128]{2,1,0:T(8,128)S(1)}, f32[45,8,128]{2,1,0:T(8,128)S(1)}, u32[]{:S(2)}, u32[]{:S(2)}) collective-permute-start(f32[45,8,128]{2,1,0:T(8,128)S(1)} %shard_map.91), channel_id=1, source_target_pairs={{16,32},{48,64},{80,96},{112,128},{144,160},{176,192},{208,224},{2... | collective-permute-start | bytes 552968 | tf_op jit(solution)/shard_map/ppermute | solution.py:349
  8.3 11.9 %collective-permute-start = (f32[17,8,128]{2,1,0:T(8,128)S(1)}, f32[17,8,128]{2,1,0:T(8,128)S(1)}, u32[]{:S(2)}, u32[]{:S(2)}) collective-permute-start(f32[17,8,128]{2,1,0:T(8,128)S(1)} %get-tuple-element.24), channel_id=1, source_target_pairs={{16,32},{48,64},{80,96},{112,128},{144,160},{176,192},{208,224},{2... | collective-permute-start | bytes 208904 | tf_op jit(solution)/shard_map/ppermute | solution.py:349
  20.2 2.8 %copy-start.2 = (f32[5,3,4,8,128]{4,3,2,1,0:T(8,128)S(1)}, f32[5,3,4,8,128]{4,3,2,1,0:T(8,128)}, u32[]{:S(2)}) copy-start(f32[5,3,4,8,128]{4,3,2,1,0:T(8,128)} %refs_10_.1) | copy-start | bytes 737284
  20.2 2.8 %copy-start.3 = (f32[3,4,8,128]{3,2,1,0:T(8,128)S(1)}, f32[3,4,8,128]{3,2,1,0:T(8,128)}, u32[]{:S(2)}) copy-start(f32[3,4,8,128]{3,2,1,0:T(8,128)} %prev.3) | copy-start | bytes 147460
  20.3 5.0 %collective-permute-start.1 = (f32[104,128]{1,0:T(8,128)S(1)}, f32[104,128]{1,0:T(8,128)S(1)}, u32[]{:S(2)}, u32[]{:S(2)}) collective-permute-start(f32[104,128]{1,0:T(8,128)S(1)} %get-tuple-element.25), channel_id=1, source_target_pairs={{0,1},{2,3},{4,5},{6,7},{8,9},{10,11},{12,13},{14,15},{1,0},{3,2},... | collective-permute-start | bytes 159752 | tf_op jit(solution)/shard_map/ppermute | solution.py:349
  22.3 3.0 %collective-permute-start.2 = (f32[104,128]{1,0:T(8,128)S(1)}, f32[104,128]{1,0:T(8,128)S(1)}, u32[]{:S(2)}, u32[]{:S(2)}) collective-permute-start(f32[104,128]{1,0:T(8,128)S(1)} %get-tuple-element.26), channel_id=1, source_target_pairs={{1,2},{3,4},{5,6},{7,8},{9,10},{11,12},{13,14},{2,1},{4,3},{6,5},{... | collective-permute-start | bytes 159752 | tf_op jit(solution)/shard_map/ppermute | solution.py:349
  25.3 5.9 %copy-start.1 = (f32[5,3,4,8,128]{4,3,2,1,0:T(8,128)S(1)}, f32[5,3,4,8,128]{4,3,2,1,0:T(8,128)}, u32[]{:S(2)}) copy-start(f32[5,3,4,8,128]{4,3,2,1,0:T(8,128)} %refs_3_.1) | copy-start | bytes 737284
  25.9 5.3 %collective-permute-start.3 = (f32[9,8,128]{2,1,0:T(8,128)S(1)}, f32[9,8,128]{2,1,0:T(8,128)S(1)}, u32[]{:S(2)}, u32[]{:S(2)}) collective-permute-start(f32[9,8,128]{2,1,0:T(8,128)S(1)} %get-tuple-element.30), channel_id=1, source_target_pairs={{16,32},{48,64},{80,96},{112,128},{144,160},{176,192},{208,224},{2... | collective-permute-start | bytes 110600 | tf_op jit(solution)/shard_map/ppermute | solution.py:349
  31.3 58.4 %collective-permute-start.5 = (f32[336,128]{1,0:T(8,128)S(1)}, f32[336,128]{1,0:T(8,128)S(1)}, u32[]{:S(2)}, u32[]{:S(2)}) collective-permute-start(f32[336,128]{1,0:T(8,128)S(1)} %get-tuple-element.31), channel_id=1, source_target_pairs={{0,1},{2,3},{4,5},{6,7},{8,9},{10,11},{12,13},{14,15},{1,0},{3,2},... | collective-permute-start | bytes 516104 | tf_op jit(solution)/shard_map/ppermute | solution.py:349
  36.5 53.1 %collective-permute-start.6 = (f32[336,128]{1,0:T(8,128)S(1)}, f32[336,128]{1,0:T(8,128)S(1)}, u32[]{:S(2)}, u32[]{:S(2)}) collective-permute-start(f32[336,128]{1,0:T(8,128)S(1)} %get-tuple-element.32), channel_id=1, source_target_pairs={{1,2},{3,4},{5,6},{7,8},{9,10},{11,12},{13,14},{2,1},{4,3},{6,5},{... | collective-permute-start | bytes 516104 | tf_op jit(solution)/shard_map/ppermute | solution.py:349
  90.4 28.7 %copy-start.4 = (f32[3,4,8,128]{3,2,1,0:T(8,128)S(1)}, f32[3,4,8,128]{3,2,1,0:T(8,128)}, u32[]{:S(2)}) copy-start(f32[3,4,8,128]{3,2,1,0:T(8,128)} %refs_5_.1) | copy-start | bytes 147460

commit v8 on v7

--- a/solution.py
+++ b/solution.py
@@ -223,7 +223,7 @@
     out[...] = spread(jnp.zeros((1, 128), jnp.float32), parts)
 
 
-def first_map(vel, forcing, visc, near, far, even_pair, odd_pair, hist, prev, gram, value, newest, fixed, payload, frames, coef, one, two):
+def first_map(vel, forcing, visc, near, far, even_pair, odd_pair, hist, prev, gram, value, newest, fixed, even_faces, odd_faces, frames, coef, one, two):
     frames[...] = jnp.zeros_like(frames)
     fixed[...] = jnp.zeros_like(fixed)
     left, right = arrived(GX, near, far)
@@ -243,7 +243,12 @@
         newest[c, p] = fresh[c, p]
     parts = {RHS + i: sum(hist[i, c, p] * r for (c, p), r in resid.items()) for i in range(M)}
     parts[NORM] = sum(f * f for f in fresh.values())
-    row = spread(gram[...], parts)
+    even_faces[9] = jnp.broadcast_to(spread(gram[...], parts), (8, 128))
+    pack_faces(value, even_faces, odd_faces)
+
+
+def chip_row(gathered_faces, payload):
+    row = gathered_faces[0, 9, 0:1] + gathered_faces[1, 9, 0:1]
     for k in range(payload.shape[0]):
         payload[k] = row
 
@@ -360,8 +365,8 @@
     return even_pair, odd_pair
 
 
-def exchange(payload):
-    rows = lax.all_to_all(payload, CHAIN, 0, 0)
+def exchange(payload, group):
+    rows = lax.all_to_all(payload, group, 0, 0)
     row = jnp.sum(rows, axis=(0, 1))
     rows = jnp.broadcast_to(row[None, None, :], (lax.axis_size(PLANE), 1, 128))
     return lax.all_to_all(rows, PLANE, 0, 0)
@@ -392,12 +397,13 @@
     edges = edges_of(*packed)
     (far_hist,) = call(lambda field, out: pack_faces(field, None, out), [(9 * M, 8, 128)])(hist_val)
     far_hist = swap(far_hist, GX, 1)
-    value, newest, static, payload = call(first_map, [shape, shape, fixed, fan], [frames, *work])(
-        velocity, forcing, viscosity, *faces, *edges, hist_res, residual_prev, gram
-    )
-    sums = exchange(payload)
-    packed = call(pack_faces, [(9, 8, 128)] * 2)(value)
-    near_value, far_value = faces_of(*packed)
+    value, newest, static, even_faces, odd_faces = call(
+        first_map, [shape, shape, fixed, (10, 8, 128), (9, 8, 128)], [frames, *work]
+    )(velocity, forcing, viscosity, *faces, *edges, hist_res, residual_prev, gram)
+    near_value = lax.all_gather(even_faces, GX[2])
+    (payload,) = call(chip_row, [(lax.axis_size(GX[1]), 1, 128)])(near_value)
+    sums = exchange(payload, GX[1])
+    far_value = swap(odd_faces, GX, 1)
     near = (faces[0], near_value, far_value, far_hist)
     edge = (GROUPS * GROUP_ROWS, 128)
     packed = call(pack_mixed_second, [edge, edge], [(GROUPS, 10 * FIELD * 8, 128)])(value, hist_val, *near)
@@ -405,7 +411,7 @@
     value_next, resid, payload = call(
         lambda *refs: second_map(entries, *refs), [shape, shape, fan], [frames, (2, GROUP_ROWS, 128), *work]
     )(sums, value, hist_val, *near, *edges, static, hist_res, newest)
-    next_sums = exchange(payload)
+    next_sums = exchange(payload, CHAIN)
     return call(lambda *refs: mix_second(entries, *refs), [shape, shape])(
         next_sums, sums, value_next, hist_val, value, value_prev, resid
     )

time: 120 us -> 115 us (0.958)
  blocking collectives: 92.7 us -> 88.1 us
    all_to_all x2, blocking collectives: 33.4 us -> 29.3 us  [exchange(): return lax.all_to_all(rows, PLANE, 0, 0)]
    all_gather x0 -> x1, blocking collectives: none -> 1.87 us  [local(): near_value = lax.all_gather(even_faces, GX[2])]
    all_gather x2 -> x1, blocking collectives: 11.8 us -> 9.95 us  [faces_of(): return (lax.all_gather(even_pair, GX[2]), odd_pair)]
  transfers between devices with their start and end apart: 7 -> 7, of which waited for: 2 -> 2; matrix products, arithmetic and copies ran while one was open for 0% -> 0% of each run, Pallas kernels for 2% -> 1%
where the time goes in v8:
time: 115 us; the launch traced here: 114 us
  blocking collectives  88.1 us (77%)
  starting transfers between devices  17.9 us (16%)
  Pallas kernels  3.84 us (3%)
  waiting for transfers between devices  3.59 us (3%)
    all_to_all x2, blocking collectives, exchange(): rows = lax.all_to_all(payload, group, 0, 0)  47 us
    all_to_all x2, blocking collectives, exchange(): return lax.all_to_all(rows, PLANE, 0, 0)  29.3 us
    ppermute x7, starting transfers between devices, swap(): return lax.ppermute(cells, axes, pairs + [(j, i) for i, j in pairs])  17.9 us
    all_gather x1, blocking collectives, faces_of(): return (lax.all_gather(even_pair, GX[2]), odd_pair)  9.95 us
    ppermute x7, waiting for transfers between devices, swap(): return lax.ppermute(cells, axes, pairs + [(j, i) for i, j in pairs])  3.59 us
  transfers between devices with their start and end apart: 7, of which 2 were waited for; matrix products, arithmetic and copies ran while one was open for 0% of the time, Pallas kernels for 1%

profile of v8, /device:TPU:1, one launch (start us, length us, event | category | flops | bytes accessed | tf_op | source)
XLA Modules:
  0.0 114.4 jit_solution(4694621917719010270)
XLA Ops:
  0.6 1.4 %shard_map.86 = (f32[62,8,128]{2,1,0:T(8,128)S(1)}, f32[17,8,128]{2,1,0:T(8,128)S(1)}, f32[3,4,8,128]{3,2,1,0:T(8,128)S(1)}, f32[3,4,8,128]{3,2,1,0:T(8,128)S(1)}, f32[4,8,128]{2,1,0:T(8,128)S(1)}) custom-call(f32[3,4,8,128]{3,2,1,0:T(8,128)} %vel.1, f32[3,4,8,128]{3,2,1,0:T(8,128)} %forcing.1, f32[4,8,128]{2,1,0:T(8,128)} %visc.1, f32[5,3,4,8,128]{4,3,2,1,0:T(8,128)} %refs_3_.1), custom_call_target="tpu_custom_call" | custom-call | flops 20000 | bytes 100000 | tf_op jit(solution)/shard_map/pallas_call | solution.py:385
  2.0 5.4 %collective-permute-start = (f32[17,8,128]{2,1,0:T(8,128)S(1)}, f32[17,8,128]{2,1,0:T(8,128)S(1)}, u32[]{:S(2)}, u32[]{:S(2)}) collective-permute-start(f32[17,8,128]{2,1,0:T(8,128)S(1)} %get-tuple-element.23), channel_id=1, source_target_pairs={{16,32},{48,64},{80,96},{112,128},{144,160},{176,192},{208,224},{2... | collective-permute-start | bytes 208904 | tf_op jit(solution)/shard_map/ppermute | solution.py:354
  7.4 1.9 %collective-permute-start.4 = (f32[45,8,128]{2,1,0:T(8,128)S(1)}, f32[45,8,128]{2,1,0:T(8,128)S(1)}, u32[]{:S(2)}, u32[]{:S(2)}) collective-permute-start(f32[45,8,128]{2,1,0:T(8,128)S(1)} %shard_map.91), channel_id=1, source_target_pairs={{16,32},{48,64},{80,96},{112,128},{144,160},{176,192},{208,224},{2... | collective-permute-start | bytes 552968 | tf_op jit(solution)/shard_map/ppermute | solution.py:354
  9.4 9.9 %all-gather = f32[124,8,128]{2,1,0:T(8,128)S(1)} all-gather(f32[62,8,128]{2,1,0:T(8,128)S(1)} %get-tuple-element.22), channel_id=2, replica_groups=mesh['gx_0'=2,'gx_1'=16,'gx_2'=2,'gy_0'=2,'gy_1'=8] {'gx_2'}, dimensions={0}, use_global_device_ids=true | all-gather | bytes 761856 | tf_op jit(solution)/shard_map/all_gather | solution.py:359
  19.3 0.0 collective-permute-done.far
  19.4 2.1 %collective-permute-start.1 = (f32[104,128]{1,0:T(8,128)S(1)}, f32[104,128]{1,0:T(8,128)S(1)}, u32[]{:S(2)}, u32[]{:S(2)}) collective-permute-start(f32[104,128]{1,0:T(8,128)S(1)} %get-tuple-element.24), channel_id=1, source_target_pairs={{0,1},{2,3},{4,5},{6,7},{8,9},{10,11},{12,13},{14,15},{1,0},{3,2},... | collective-permute-start | bytes 159752 | tf_op jit(solution)/shard_map/ppermute | solution.py:354
  21.4 0.7 collective-permute-start.2
  22.1 0.2 shard_map.88.gram
  22.3 2.1 %collective-permute-done.1.even_pair = f32[104,128]{1,0:T(8,128)S(1)} collective-permute-done((f32[104,128]{1,0:T(8,128)S(1)}, f32[104,128]{1,0:T(8,128)S(1)}, u32[]{:S(2)}, u32[]{:S(2)}) %collective-permute-start.1) | collective-permute-done | bytes 53280 | tf_op jit(solution)/shard_map/ppermute | solution.py:354
  24.4 0.5 shard_map.89
  24.9 1.9 %collective-permute-start.3 = (f32[9,8,128]{2,1,0:T(8,128)S(1)}, f32[9,8,128]{2,1,0:T(8,128)S(1)}, u32[]{:S(2)}, u32[]{:S(2)}) collective-permute-start(f32[9,8,128]{2,1,0:T(8,128)S(1)} %get-tuple-element.28), channel_id=1, source_target_pairs={{16,32},{48,64},{80,96},{112,128},{144,160},{176,192},{208,224},{2... | collective-permute-start | bytes 110600 | tf_op jit(solution)/shard_map/ppermute | solution.py:354
  26.9 1.9 %all-gather.1 = f32[20,8,128]{2,1,0:T(8,128)S(1)} all-gather(f32[10,8,128]{2,1,0:T(8,128)S(1)} %get-tuple-element.26), channel_id=3, replica_groups=mesh['gx_0'=2,'gx_1'=16,'gx_2'=2,'gy_0'=2,'gy_1'=8] {'gx_2'}, dimensions={0}, use_global_device_ids=true | all-gather | bytes 122880 | tf_op jit(solution)/shard_map/all_gather | solution.py:403
  28.7 1.5 %collective-permute-done.3.far_value.refs_5_ = f32[9,8,128]{2,1,0:T(8,128)S(1)} collective-permute-done((f32[9,8,128]{2,1,0:T(8,128)S(1)}, f32[9,8,128]{2,1,0:T(8,128)S(1)}, u32[]{:S(2)}, u32[]{:S(2)}) %collective-permute-start.3) | collective-permute-done | bytes 36896 | tf_op jit(solution)/shard_map/ppermute | solution.py:354
  30.2 0.1 shard_map.92
  30.3 5.3 %collective-permute-start.5 = (f32[336,128]{1,0:T(8,128)S(1)}, f32[336,128]{1,0:T(8,128)S(1)}, u32[]{:S(2)}, u32[]{:S(2)}) collective-permute-start(f32[336,128]{1,0:T(8,128)S(1)} %get-tuple-element.29), channel_id=1, source_target_pairs={{0,1},{2,3},{4,5},{6,7},{8,9},{10,11},{12,13},{14,15},{1,0},{3,2},... | collective-permute-start | bytes 516104 | tf_op jit(solution)/shard_map/ppermute | solution.py:354
  35.6 0.7 collective-permute-start.6
  36.3 28.0 %all_to_all.20 = f32[16,1,128]{2,1,0:T(1,128)S(1)} all-to-all(f32[16,1,128]{2,1,0:T(1,128)S(1)} %shard_map.90), channel_id=1, replica_groups=mesh['gx_0'=2,'gx_1'=16,'gx_2'=2,'gy_0'=2,'gy_1'=8] {'gx_1'}, dimensions={0} | all-to-all | bytes 16384 | tf_op jit(solution)/shard_map/all_to_all | solution.py:369
  64.4 17.7 %all_to_all.21.refs_0_.refs_1_ = f32[32,1,128]{2,1,0:T(1,128)S(1)} all-to-all(f32[32,1,128]{2,1,0:T(1,128)S(1)} %broadcast_in_dim.4), channel_id=1, replica_groups=mesh['gx_0'=2,'gx_1'=16,'gx_2'=2,'gy_0'=2,'gy_1'=8] {'gx_0','gy_0','gy_1'}, dimensions={0} | all-to-all | bytes 32768 | tf_op jit(solution)/shard_map/all_to_all | solution.py:372
  82.0 0.8 shard_map.93
  82.8 0.0 copy-start.3
  82.8 19.0 %all_to_all.22 = f32[32,1,128]{2,1,0:T(1,128)S(1)} all-to-all(f32[32,1,128]{2,1,0:T(1,128)S(1)} %get-tuple-element.33), channel_id=1, replica_groups=mesh['gx_0'=2,'gx_1'=16,'gx_2'=2,'gy_0'=2,'gy_1'=8] {'gx_1','gx_2'}, dimensions={0} | all-to-all | bytes 32768 | tf_op jit(solution)/shard_map/all_to_all | solution.py:369
  101.8 0.1 reduce_sum.19
  101.9 11.6 %all_to_all.23.refs_0_ = f32[32,1,128]{2,1,0:T(1,128)S(1)} all-to-all(f32[32,1,128]{2,1,0:T(1,128)S(1)} %broadcast_in_dim.5), channel_id=1, replica_groups=mesh['gx_0'=2,'gx_1'=16,'gx_2'=2,'gy_0'=2,'gy_1'=8] {'gx_0','gy_0','gy_1'}, dimensions={0} | all-to-all | bytes 32768 | tf_op jit(solution)/shard_map/all_to_all | solution.py:372
  113.5 0.8 shard_map.94
  (17 shorter events, 0.2 us)
Async XLA Ops:
  0.6 6.8 %copy-start = (f32[5,3,4,8,128]{4,3,2,1,0:T(8,128)S(1)}, f32[5,3,4,8,128]{4,3,2,1,0:T(8,128)}, u32[]{:S(2)}) copy-start(f32[5,3,4,8,128]{4,3,2,1,0:T(8,128)} %refs_3_.1) | copy-start | bytes 737284
  2.0 17.3 %collective-permute-start = (f32[17,8,128]{2,1,0:T(8,128)S(1)}, f32[17,8,128]{2,1,0:T(8,128)S(1)}, u32[]{:S(2)}, u32[]{:S(2)}) collective-permute-start(f32[17,8,128]{2,1,0:T(8,128)S(1)} %get-tuple-element.23), channel_id=1, source_target_pairs={{16,32},{48,64},{80,96},{112,128},{144,160},{176,192},{208,224},{2... | collective-permute-start | bytes 208904 | tf_op jit(solution)/shard_map/ppermute | solution.py:354
  7.4 22.8 %collective-permute-start.4 = (f32[45,8,128]{2,1,0:T(8,128)S(1)}, f32[45,8,128]{2,1,0:T(8,128)S(1)}, u32[]{:S(2)}, u32[]{:S(2)}) collective-permute-start(f32[45,8,128]{2,1,0:T(8,128)S(1)} %shard_map.91), channel_id=1, source_target_pairs={{16,32},{48,64},{80,96},{112,128},{144,160},{176,192},{208,224},{2... | collective-permute-start | bytes 552968 | tf_op jit(solution)/shard_map/ppermute | solution.py:354
  19.3 2.8 %copy-start.1 = (f32[5,3,4,8,128]{4,3,2,1,0:T(8,128)S(1)}, f32[5,3,4,8,128]{4,3,2,1,0:T(8,128)}, u32[]{:S(2)}) copy-start(f32[5,3,4,8,128]{4,3,2,1,0:T(8,128)} %refs_10_.1) | copy-start | bytes 737284
  19.3 2.8 %copy-start.2 = (f32[3,4,8,128]{3,2,1,0:T(8,128)S(1)}, f32[3,4,8,128]{3,2,1,0:T(8,128)}, u32[]{:S(2)}) copy-start(f32[3,4,8,128]{3,2,1,0:T(8,128)} %prev.3) | copy-start | bytes 147460
  19.4 5.0 %collective-permute-start.1 = (f32[104,128]{1,0:T(8,128)S(1)}, f32[104,128]{1,0:T(8,128)S(1)}, u32[]{:S(2)}, u32[]{:S(2)}) collective-permute-start(f32[104,128]{1,0:T(8,128)S(1)} %get-tuple-element.24), channel_id=1, source_target_pairs={{0,1},{2,3},{4,5},{6,7},{8,9},{10,11},{12,13},{14,15},{1,0},{3,2},... | collective-permute-start | bytes 159752 | tf_op jit(solution)/shard_map/ppermute | solution.py:354
  21.4 3.0 %collective-permute-start.2 = (f32[104,128]{1,0:T(8,128)S(1)}, f32[104,128]{1,0:T(8,128)S(1)}, u32[]{:S(2)}, u32[]{:S(2)}) collective-permute-start(f32[104,128]{1,0:T(8,128)S(1)} %get-tuple-element.25), channel_id=1, source_target_pairs={{1,2},{3,4},{5,6},{7,8},{9,10},{11,12},{13,14},{2,1},{4,3},{6,5},{... | collective-permute-start | bytes 159752 | tf_op jit(solution)/shard_map/ppermute | solution.py:354
  24.9 5.3 %collective-permute-start.3 = (f32[9,8,128]{2,1,0:T(8,128)S(1)}, f32[9,8,128]{2,1,0:T(8,128)S(1)}, u32[]{:S(2)}, u32[]{:S(2)}) collective-permute-start(f32[9,8,128]{2,1,0:T(8,128)S(1)} %get-tuple-element.28), channel_id=1, source_target_pairs={{16,32},{48,64},{80,96},{112,128},{144,160},{176,192},{208,224},{2... | collective-permute-start | bytes 110600 | tf_op jit(solution)/shard_map/ppermute | solution.py:354
  30.3 51.7 %collective-permute-start.5 = (f32[336,128]{1,0:T(8,128)S(1)}, f32[336,128]{1,0:T(8,128)S(1)}, u32[]{:S(2)}, u32[]{:S(2)}) collective-permute-start(f32[336,128]{1,0:T(8,128)S(1)} %get-tuple-element.29), channel_id=1, source_target_pairs={{0,1},{2,3},{4,5},{6,7},{8,9},{10,11},{12,13},{14,15},{1,0},{3,2},... | collective-permute-start | bytes 516104 | tf_op jit(solution)/shard_map/ppermute | solution.py:354
  35.6 46.4 %collective-permute-start.6 = (f32[336,128]{1,0:T(8,128)S(1)}, f32[336,128]{1,0:T(8,128)S(1)}, u32[]{:S(2)}, u32[]{:S(2)}) collective-permute-start(f32[336,128]{1,0:T(8,128)S(1)} %get-tuple-element.30), channel_id=1, source_target_pairs={{1,2},{3,4},{5,6},{7,8},{9,10},{11,12},{13,14},{2,1},{4,3},{6,5},{... | collective-permute-start | bytes 516104 | tf_op jit(solution)/shard_map/ppermute | solution.py:354
  82.8 30.7 %copy-start.3 = (f32[3,4,8,128]{3,2,1,0:T(8,128)S(1)}, f32[3,4,8,128]{3,2,1,0:T(8,128)}, u32[]{:S(2)}) copy-start(f32[3,4,8,128]{3,2,1,0:T(8,128)} %refs_5_.1) | copy-start | bytes 147460

commit v9 on v7

--- a/solution.py
+++ b/solution.py
@@ -360,11 +360,11 @@
     return even_pair, odd_pair
 
 
-def exchange(payload):
-    rows = lax.all_to_all(payload, CHAIN, 0, 0)
+def exchange(payload, first, second):
+    rows = lax.all_to_all(payload, first, 0, 0)
     row = jnp.sum(rows, axis=(0, 1))
-    rows = jnp.broadcast_to(row[None, None, :], (lax.axis_size(PLANE), 1, 128))
-    return lax.all_to_all(rows, PLANE, 0, 0)
+    rows = jnp.broadcast_to(row[None, None, :], (lax.axis_size(second), 1, 128))
+    return lax.all_to_all(rows, second, 0, 0)
 
 
 def local(velocity, forcing, viscosity, residual_prev, value_prev, hist_res, hist_val):
@@ -395,7 +395,7 @@
     value, newest, static, payload = call(first_map, [shape, shape, fixed, fan], [frames, *work])(
         velocity, forcing, viscosity, *faces, *edges, hist_res, residual_prev, gram
     )
-    sums = exchange(payload)
+    sums = exchange(payload, CHAIN, PLANE)
     packed = call(pack_faces, [(9, 8, 128)] * 2)(value)
     near_value, far_value = faces_of(*packed)
     near = (faces[0], near_value, far_value, far_hist)
@@ -403,9 +403,9 @@
     packed = call(pack_mixed_second, [edge, edge], [(GROUPS, 10 * FIELD * 8, 128)])(value, hist_val, *near)
     edges = edges_of(*packed)
     value_next, resid, payload = call(
-        lambda *refs: second_map(entries, *refs), [shape, shape, fan], [frames, (2, GROUP_ROWS, 128), *work]
+        lambda *refs: second_map(entries, *refs), [shape, shape, (lax.axis_size(PLANE), 1, 128)], [frames, (2, GROUP_ROWS, 128), *work]
     )(sums, value, hist_val, *near, *edges, static, hist_res, newest)
-    next_sums = exchange(payload)
+    next_sums = exchange(payload, PLANE, CHAIN)
     return call(lambda *refs: mix_second(entries, *refs), [shape, shape])(
         next_sums, sums, value_next, hist_val, value, value_prev, resid
     )

time: 120 us -> 122 us (1.017)
  no operation moved by 1% of the time
where the time goes in v9:
time: 122 us; the launch traced here: 121 us
  blocking collectives  93.9 us (77%)
  starting transfers between devices  17.9 us (15%)
  Pallas kernels  3.82 us (3%)
  waiting for transfers between devices  3.59 us (3%)
    all_to_all x2, blocking collectives, exchange(): rows = lax.all_to_all(payload, first, 0, 0)  42.3 us
    all_to_all x2, blocking collectives, exchange(): return lax.all_to_all(rows, second, 0, 0)  39.8 us
    ppermute x7, starting transfers between devices, swap(): return lax.ppermute(cells, axes, pairs + [(j, i) for i, j in pairs])  17.9 us
    all_gather x2, blocking collectives, faces_of(): return (lax.all_gather(even_pair, GX[2]), odd_pair)  11.8 us
    ppermute x7, waiting for transfers between devices, swap(): return lax.ppermute(cells, axes, pairs + [(j, i) for i, j in pairs])  3.59 us
  transfers between devices with their start and end apart: 7, of which 2 were waited for; matrix products, arithmetic and copies ran while one was open for 0% of the time, Pallas kernels for 2%

profile of v9, /device:TPU:1, one launch (start us, length us, event | category | flops | bytes accessed | tf_op | source)
XLA Modules:
  0.0 121.1 jit_solution(1839891429577182274)
XLA Ops:
  0.6 0.9 copy-done
  1.6 5.4 %collective-permute-start.4 = (f32[45,8,128]{2,1,0:T(8,128)S(1)}, f32[45,8,128]{2,1,0:T(8,128)S(1)}, u32[]{:S(2)}, u32[]{:S(2)}) collective-permute-start(f32[45,8,128]{2,1,0:T(8,128)S(1)} %shard_map.91), channel_id=1, source_target_pairs={{16,32},{48,64},{80,96},{112,128},{144,160},{176,192},{208,224},{2... | collective-permute-start | bytes 552968 | tf_op jit(solution)/shard_map/ppermute | solution.py:349
  7.0 1.3 %shard_map.86 = (f32[62,8,128]{2,1,0:T(8,128)S(1)}, f32[17,8,128]{2,1,0:T(8,128)S(1)}, f32[3,4,8,128]{3,2,1,0:T(8,128)S(1)}, f32[3,4,8,128]{3,2,1,0:T(8,128)S(1)}, f32[4,8,128]{2,1,0:T(8,128)S(1)}) custom-call(f32[3,4,8,128]{3,2,1,0:T(8,128)} %vel.1, f32[3,4,8,128]{3,2,1,0:T(8,128)} %forcing.1, f32[4,8,128]{2,1,0:T(8,128)} %visc.1, f32[5,3,4,8,128]{4,3,2,1,0:T(8,128)} %refs_3_.1), custom_call_target="tpu_custom_call" | custom-call | flops 20000 | bytes 100000 | tf_op jit(solution)/shard_map/pallas_call | solution.py:380
  8.3 1.9 %collective-permute-start = (f32[17,8,128]{2,1,0:T(8,128)S(1)}, f32[17,8,128]{2,1,0:T(8,128)S(1)}, u32[]{:S(2)}, u32[]{:S(2)}) collective-permute-start(f32[17,8,128]{2,1,0:T(8,128)S(1)} %get-tuple-element.24), channel_id=1, source_target_pairs={{16,32},{48,64},{80,96},{112,128},{144,160},{176,192},{208,224},{2... | collective-permute-start | bytes 208904 | tf_op jit(solution)/shard_map/ppermute | solution.py:349
  10.3 9.9 %all-gather = f32[124,8,128]{2,1,0:T(8,128)S(1)} all-gather(f32[62,8,128]{2,1,0:T(8,128)S(1)} %get-tuple-element.23), channel_id=2, replica_groups=mesh['gx_0'=2,'gx_1'=16,'gx_2'=2,'gy_0'=2,'gy_1'=8] {'gx_2'}, dimensions={0}, use_global_device_ids=true | all-gather | bytes 761856 | tf_op jit(solution)/shard_map/all_gather | solution.py:354
  20.3 2.1 %collective-permute-start.1 = (f32[104,128]{1,0:T(8,128)S(1)}, f32[104,128]{1,0:T(8,128)S(1)}, u32[]{:S(2)}, u32[]{:S(2)}) collective-permute-start(f32[104,128]{1,0:T(8,128)S(1)} %get-tuple-element.25), channel_id=1, source_target_pairs={{0,1},{2,3},{4,5},{6,7},{8,9},{10,11},{12,13},{14,15},{1,0},{3,2},... | collective-permute-start | bytes 159752 | tf_op jit(solution)/shard_map/ppermute | solution.py:349
  22.3 0.7 collective-permute-start.2
  23.0 0.2 shard_map.88.gram
  23.2 2.1 %collective-permute-done.1.even_pair = f32[104,128]{1,0:T(8,128)S(1)} collective-permute-done((f32[104,128]{1,0:T(8,128)S(1)}, f32[104,128]{1,0:T(8,128)S(1)}, u32[]{:S(2)}, u32[]{:S(2)}) %collective-permute-start.1) | collective-permute-done | bytes 53280 | tf_op jit(solution)/shard_map/ppermute | solution.py:349
  25.3 0.5 shard_map.89
  25.9 1.9 %collective-permute-start.3 = (f32[9,8,128]{2,1,0:T(8,128)S(1)}, f32[9,8,128]{2,1,0:T(8,128)S(1)}, u32[]{:S(2)}, u32[]{:S(2)}) collective-permute-start(f32[9,8,128]{2,1,0:T(8,128)S(1)} %get-tuple-element.30), channel_id=1, source_target_pairs={{16,32},{48,64},{80,96},{112,128},{144,160},{176,192},{208,224},{2... | collective-permute-start | bytes 110600 | tf_op jit(solution)/shard_map/ppermute | solution.py:349
  27.8 1.9 %all-gather.1 = f32[18,8,128]{2,1,0:T(8,128)S(1)} all-gather(f32[9,8,128]{2,1,0:T(8,128)S(1)} %get-tuple-element.29), channel_id=3, replica_groups=mesh['gx_0'=2,'gx_1'=16,'gx_2'=2,'gy_0'=2,'gy_1'=8] {'gx_2'}, dimensions={0}, use_global_device_ids=true | all-gather | bytes 110592 | tf_op jit(solution)/shard_map/all_gather | solution.py:354
  29.6 1.5 %collective-permute-done.3.far_value.refs_5_ = f32[9,8,128]{2,1,0:T(8,128)S(1)} collective-permute-done((f32[9,8,128]{2,1,0:T(8,128)S(1)}, f32[9,8,128]{2,1,0:T(8,128)S(1)}, u32[]{:S(2)}, u32[]{:S(2)}) %collective-permute-start.3) | collective-permute-done | bytes 36896 | tf_op jit(solution)/shard_map/ppermute | solution.py:349
  31.1 0.1 shard_map.92
  31.3 5.3 %collective-permute-start.5 = (f32[336,128]{1,0:T(8,128)S(1)}, f32[336,128]{1,0:T(8,128)S(1)}, u32[]{:S(2)}, u32[]{:S(2)}) collective-permute-start(f32[336,128]{1,0:T(8,128)S(1)} %get-tuple-element.31), channel_id=1, source_target_pairs={{0,1},{2,3},{4,5},{6,7},{8,9},{10,11},{12,13},{14,15},{1,0},{3,2},... | collective-permute-start | bytes 516104 | tf_op jit(solution)/shard_map/ppermute | solution.py:349
  36.5 0.7 collective-permute-start.6
  37.2 30.5 %all_to_all.20 = f32[32,1,128]{2,1,0:T(1,128)S(1)} all-to-all(f32[32,1,128]{2,1,0:T(1,128)S(1)} %get-tuple-element.27), channel_id=1, replica_groups=mesh['gx_0'=2,'gx_1'=16,'gx_2'=2,'gy_0'=2,'gy_1'=8] {'gx_1','gx_2'}, dimensions={0} | all-to-all | bytes 32768 | tf_op jit(solution)/shard_map/all_to_all | solution.py:364
  67.7 0.1 reduce_sum.18
  67.8 21.8 %all_to_all.21.refs_0_.refs_1_ = f32[32,1,128]{2,1,0:T(1,128)S(1)} all-to-all(f32[32,1,128]{2,1,0:T(1,128)S(1)} %broadcast_in_dim.4), channel_id=1, replica_groups=mesh['gx_0'=2,'gx_1'=16,'gx_2'=2,'gy_0'=2,'gy_1'=8] {'gx_0','gy_0','gy_1'}, dimensions={0} | all-to-all | bytes 32768 | tf_op jit(solution)/shard_map/all_to_all | solution.py:367
  89.6 0.8 shard_map.93
  90.4 11.8 %all_to_all.22 = f32[32,1,128]{2,1,0:T(1,128)S(1)} all-to-all(f32[32,1,128]{2,1,0:T(1,128)S(1)} %get-tuple-element.35), channel_id=1, replica_groups=mesh['gx_0'=2,'gx_1'=16,'gx_2'=2,'gy_0'=2,'gy_1'=8] {'gx_0','gy_0','gy_1'}, dimensions={0} | all-to-all | bytes 32768 | tf_op jit(solution)/shard_map/all_to_all | solution.py:364
  102.2 0.1 reduce_sum.19
  102.2 18.0 %all_to_all.23.refs_0_ = f32[32,1,128]{2,1,0:T(1,128)S(1)} all-to-all(f32[32,1,128]{2,1,0:T(1,128)S(1)} %broadcast_in_dim.5), channel_id=1, replica_groups=mesh['gx_0'=2,'gx_1'=16,'gx_2'=2,'gy_0'=2,'gy_1'=8] {'gx_1','gx_2'}, dimensions={0} | all-to-all | bytes 32768 | tf_op jit(solution)/shard_map/all_to_all | solution.py:367
  120.2 0.8 shard_map.94
  (19 shorter events, 0.1 us)
Async XLA Ops:
  0.6 0.9 copy-start
  1.6 29.5 %collective-permute-start.4 = (f32[45,8,128]{2,1,0:T(8,128)S(1)}, f32[45,8,128]{2,1,0:T(8,128)S(1)}, u32[]{:S(2)}, u32[]{:S(2)}) collective-permute-start(f32[45,8,128]{2,1,0:T(8,128)S(1)} %shard_map.91), channel_id=1, source_target_pairs={{16,32},{48,64},{80,96},{112,128},{144,160},{176,192},{208,224},{2... | collective-permute-start | bytes 552968 | tf_op jit(solution)/shard_map/ppermute | solution.py:349
  8.3 11.9 %collective-permute-start = (f32[17,8,128]{2,1,0:T(8,128)S(1)}, f32[17,8,128]{2,1,0:T(8,128)S(1)}, u32[]{:S(2)}, u32[]{:S(2)}) collective-permute-start(f32[17,8,128]{2,1,0:T(8,128)S(1)} %get-tuple-element.24), channel_id=1, source_target_pairs={{16,32},{48,64},{80,96},{112,128},{144,160},{176,192},{208,224},{2... | collective-permute-start | bytes 208904 | tf_op jit(solution)/shard_map/ppermute | solution.py:349
  20.2 2.8 %copy-start.2 = (f32[5,3,4,8,128]{4,3,2,1,0:T(8,128)S(1)}, f32[5,3,4,8,128]{4,3,2,1,0:T(8,128)}, u32[]{:S(2)}) copy-start(f32[5,3,4,8,128]{4,3,2,1,0:T(8,128)} %refs_10_.1) | copy-start | bytes 737284
  20.2 2.8 %copy-start.3 = (f32[3,4,8,128]{3,2,1,0:T(8,128)S(1)}, f32[3,4,8,128]{3,2,1,0:T(8,128)}, u32[]{:S(2)}) copy-start(f32[3,4,8,128]{3,2,1,0:T(8,128)} %prev.3) | copy-start | bytes 147460
  20.3 5.0 %collective-permute-start.1 = (f32[104,128]{1,0:T(8,128)S(1)}, f32[104,128]{1,0:T(8,128)S(1)}, u32[]{:S(2)}, u32[]{:S(2)}) collective-permute-start(f32[104,128]{1,0:T(8,128)S(1)} %get-tuple-element.25), channel_id=1, source_target_pairs={{0,1},{2,3},{4,5},{6,7},{8,9},{10,11},{12,13},{14,15},{1,0},{3,2},... | collective-permute-start | bytes 159752 | tf_op jit(solution)/shard_map/ppermute | solution.py:349
  22.3 3.0 %collective-permute-start.2 = (f32[104,128]{1,0:T(8,128)S(1)}, f32[104,128]{1,0:T(8,128)S(1)}, u32[]{:S(2)}, u32[]{:S(2)}) collective-permute-start(f32[104,128]{1,0:T(8,128)S(1)} %get-tuple-element.26), channel_id=1, source_target_pairs={{1,2},{3,4},{5,6},{7,8},{9,10},{11,12},{13,14},{2,1},{4,3},{6,5},{... | collective-permute-start | bytes 159752 | tf_op jit(solution)/shard_map/ppermute | solution.py:349
  25.3 5.9 %copy-start.1 = (f32[5,3,4,8,128]{4,3,2,1,0:T(8,128)S(1)}, f32[5,3,4,8,128]{4,3,2,1,0:T(8,128)}, u32[]{:S(2)}) copy-start(f32[5,3,4,8,128]{4,3,2,1,0:T(8,128)} %refs_3_.1) | copy-start | bytes 737284
  25.9 5.3 %collective-permute-start.3 = (f32[9,8,128]{2,1,0:T(8,128)S(1)}, f32[9,8,128]{2,1,0:T(8,128)S(1)}, u32[]{:S(2)}, u32[]{:S(2)}) collective-permute-start(f32[9,8,128]{2,1,0:T(8,128)S(1)} %get-tuple-element.30), channel_id=1, source_target_pairs={{16,32},{48,64},{80,96},{112,128},{144,160},{176,192},{208,224},{2... | collective-permute-start | bytes 110600 | tf_op jit(solution)/shard_map/ppermute | solution.py:349
  31.3 58.4 %collective-permute-start.5 = (f32[336,128]{1,0:T(8,128)S(1)}, f32[336,128]{1,0:T(8,128)S(1)}, u32[]{:S(2)}, u32[]{:S(2)}) collective-permute-start(f32[336,128]{1,0:T(8,128)S(1)} %get-tuple-element.31), channel_id=1, source_target_pairs={{0,1},{2,3},{4,5},{6,7},{8,9},{10,11},{12,13},{14,15},{1,0},{3,2},... | collective-permute-start | bytes 516104 | tf_op jit(solution)/shard_map/ppermute | solution.py:349
  36.5 53.1 %collective-permute-start.6 = (f32[336,128]{1,0:T(8,128)S(1)}, f32[336,128]{1,0:T(8,128)S(1)}, u32[]{:S(2)}, u32[]{:S(2)}) collective-permute-start(f32[336,128]{1,0:T(8,128)S(1)} %get-tuple-element.32), channel_id=1, source_target_pairs={{1,2},{3,4},{5,6},{7,8},{9,10},{11,12},{13,14},{2,1},{4,3},{6,5},{... | collective-permute-start | bytes 516104 | tf_op jit(solution)/shard_map/ppermute | solution.py:349
  90.4 29.8 %copy-start.4 = (f32[3,4,8,128]{3,2,1,0:T(8,128)S(1)}, f32[3,4,8,128]{3,2,1,0:T(8,128)}, u32[]{:S(2)}) copy-start(f32[3,4,8,128]{3,2,1,0:T(8,128)} %refs_5_.1) | copy-start | bytes 147460
